TPU v7x, 128 devices: a whole 4x4x4 slice. The times are simulated.
128 devices in a mesh: expert: 32 (over y, x, core), dp: 4 (over z).
Axes of the slice: x: 4, y: 4, z: 4, core: 2. Of those that a mesh axis runs over, the one named last changes fastest.
Arguments:
- out_grads: bfloat16 [4, 4096, 7168], P('dp', 'expert'), may hold values from -6 to 6
- expert_ids: int32 [4, 4096, 8], P('dp', 'expert'), may hold values from 0 to 255, all different within a row; in each aligned block of 128 rows (0 to 127, 128 to 255, ..., all dimensions but the last counted through in order) at most 6 rows name the same one
- gate_probs: float32 [4, 4096, 8], P('dp', 'expert'), may hold values from 0.05 to 0.5
- hidden_acts: bfloat16 [4, 256, 192, 2048], P('dp', 'expert'), may hold values from -6 to 6
- q_previous: bfloat16 [256, 32, 7168], P('expert'), may hold values from -0.0625 to 0.0625
Outputs:
- new_basis: float32 [256, 32, 2048], P('expert')
- q_update: float32 [256, 32, 7168], P('expert', None, 'dp')
Inputs may be any that keep to these rules, and one draw needn't show every extreme that they name: `expert_ids`: each row names 8 different experts; among the rows of one device no expert is named more than 6 times.
All inputs are finite; a program needn't handle non-finite values.
Results may differ from a plain program's by a relative error of at most 0.014.
Values may be sent and summed in bfloat16 or wider, within the bound.
No kernel may reach another device: no remote copies, remote signals or barrier semaphores. Data moves between devices by JAX's collectives and lax.ppermute only.
A program may use at most 192 MiB of HBM per device.

v0:
```python
import math

import jax
import jax.numpy as jnp
from jax import lax
from jax.sharding import PartitionSpec as P


def cut_along(shard, dim, length):
    shape = shard.shape
    blocks = shard.reshape(*shape[:dim], length, shape[dim] // length, *shape[dim + 1 :])
    return jnp.moveaxis(blocks, dim, 0)


def sent_and_summed(shard, axis, dim):
    blocks = cut_along(shard, dim, lax.axis_size(axis))
    arrived = lax.all_to_all(blocks, axis, split_axis=0, concat_axis=0, tiled=True)
    return arrived.sum(axis=0)


def copy_for_each(shard, axis):
    length = lax.axis_size(axis)
    return lax.all_to_all(
        jnp.broadcast_to(shard[None], (length, *shard.shape)), axis, 0, 0, tiled=True
    )


def of_everyone(shard, axis):
    return copy_for_each(shard, axis).astype(jnp.float32).sum(axis=0)


def in_order(blocks, dim):
    shape = list(blocks.shape[1:])
    shape[dim] *= blocks.shape[0]
    return jnp.moveaxis(blocks, 0, dim).reshape(shape)


def collect(shard, axis, dim):
    blocks = copy_for_each(shard, axis)
    return in_order(blocks, dim)


def sum_at_owner(shard, axis, dim):
    length = lax.axis_size(axis)
    blocks = lax.all_to_all(cut_along(shard, dim, length), axis, 0, 0, tiled=True)
    return jnp.sum(blocks.astype(jnp.float32), axis=0)


def slot_tables(route_ids, gate_values, num_experts, capacity):
    flat_ids = route_ids.reshape(-1)
    row_count = flat_ids.shape[0]
    top_k = route_ids.shape[-1]
    one_hot = (flat_ids[:, None] == jnp.arange(num_experts, dtype=jnp.int32)[None, :]).astype(
        jnp.int32
    )
    earlier = jnp.cumsum(one_hot, axis=0) - one_hot
    position = jnp.sum(earlier * one_hot, axis=1)
    slot_index = flat_ids * capacity + position
    token_of = (
        jnp.zeros((num_experts * capacity,), jnp.int32)
        .at[slot_index]
        .set(jnp.arange(row_count, dtype=jnp.int32) // top_k)
    )
    gate_of = (
        jnp.zeros((num_experts * capacity,), jnp.float32)
        .at[slot_index]
        .set(gate_values.reshape(-1))
    )
    return (token_of, gate_of)


def first_factor(arrived, q_part, hidden_part):
    mixed = jnp.einsum(
        "sjcd,jrd->jscr", arrived, q_part, preferred_element_type=jnp.float32
    ).astype(jnp.bfloat16)
    return jnp.einsum("jscr,jscf->jrf", mixed, hidden_part, preferred_element_type=jnp.float32)


def second_factor(arrived, projected):
    return jnp.einsum("jscr,sjcd->jrd", projected, arrived, preferred_element_type=jnp.float32)


def lower_inverse(gram):
    lower = jnp.linalg.cholesky(gram)
    identity = jnp.broadcast_to(jnp.eye(gram.shape[1], dtype=jnp.float32), gram.shape)
    return jax.vmap(lambda left, right: jax.scipy.linalg.solve_triangular(left, right, lower=True))(
        lower, identity
    )


def gram_of(values):
    return jnp.einsum("jrf,jsf->jrs", values, values)


def apply_inverse(inverse, values):
    return jnp.einsum("jrs,jsf->jrf", inverse, values)


def local(out_grads, expert_ids, gate_probs, hidden_acts, q_previous):
    n_expert = lax.axis_size("expert")
    local_count = hidden_acts.shape[1]
    slot_count = hidden_acts.shape[2]
    capacity = slot_count // n_expert
    width = out_grads.shape[2]
    token_of, gate_of = slot_tables(expert_ids[0], gate_probs[0], local_count * n_expert, capacity)
    picked = jnp.take(out_grads[0], token_of, axis=0)
    routed = (picked.astype(jnp.float32) * gate_of[:, None]).astype(jnp.bfloat16)
    routed = routed.reshape(n_expert, local_count, capacity, width)
    hidden_blocks = hidden_acts[0].reshape(local_count, n_expert, capacity, hidden_acts.shape[3])
    arrived = lax.all_to_all(routed, "expert", split_axis=0, concat_axis=0, tiled=True)
    factor = first_factor(arrived, q_previous, hidden_blocks)
    share = sent_and_summed(factor, "dp", 2)
    gram = of_everyone(gram_of(share).astype(jnp.bfloat16), "dp").astype(jnp.float32)
    inverse = lower_inverse(gram)
    ortho = collect(apply_inverse(inverse, share).astype(jnp.bfloat16), "dp", 2).astype(jnp.float32)
    ortho_half = ortho.astype(jnp.bfloat16)
    projected = jnp.einsum(
        "jscf,jrf->jscr", hidden_blocks, ortho_half, preferred_element_type=jnp.float32
    ).astype(jnp.bfloat16)
    terms = second_factor(arrived, projected)
    q_update = sum_at_owner(terms.astype(jnp.bfloat16), "dp", 2)
    new_basis = ortho * math.sqrt(ortho.shape[2])
    return (new_basis, q_update)


def solution(mesh):
    return jax.shard_map(
        local,
        mesh=mesh,
        in_specs=(
            P("dp", "expert", None),
            P("dp", "expert", None),
            P("dp", "expert", None),
            P("dp", "expert", None, None),
            P("expert", None, None),
        ),
        out_specs=(P("expert", None, None), P("expert", None, "dp")),
        check_vma=False,
    )
```

profile of v0, /device:TPU:6, one launch (start us, length us, event | category | flops | bytes accessed | tf_op | source)
XLA Modules:
  0.0 630.6 jit_solution(4050087780140486832)
XLA Ops:
  3.8 4.3 scatter_custom_fusion
  8.2 16.4 %gather_fusion = bf16[1536,7168]{1,0:T(8,128)(2,1)} fusion(bf16[128,7168]{1,0:T(8,128)(2,1)S(1)} %bitcast.65, s32[2048]{0:T(1024)S(1)} %pad_clamp_fusion), kind=kCustom, calls=%fused_computation | custom fusion | bytes 44046336 | tf_op jit(solution)/shard_map/jit(_take)/gather | solution.py:106
  24.6 30.7 %gather.7 = bf16[32,8,6,7168]{3,2,1,0:T(8,128)(2,1)} reshape(bf16[1536,7168]{1,0:T(8,128)(2,1)} %gather_fusion) | data formatting | bytes 44040192 | tf_op jit(solution)/shard_map/jit(_take)/gather | solution.py:106
  55.7 4.3 scatter_custom_fusion.1
  60.2 20.4 %multiply_convert_fusion = bf16[32,8,6,7168]{3,2,1,0:T(8,128)(2,1)} fusion(f32[32,8,6]{2,1,0:T(8,128)S(1)} %mul.40, bf16[32,8,6,7168]{3,2,1,0:T(8,128)(2,1)} %gather.7, pred[32,8,6]{2,1,0:T(8,128)(4,1)S(1)} %broadcast_in_dim.44), kind=kLoop, calls=%fused_computation.3 | loop fusion | flops 44040192 | bytes 44047872 | tf_op jit(solution)/shard_map/convert_element_type | solution.py:107
  80.5 25.2 %copy.62 = bf16[32,8,6,7168]{3,1,2,0:T(8,128)(2,1)} copy(bf16[32,8,6,7168]{3,2,1,0:T(8,128)(2,1)} %multiply_convert_fusion) | data formatting | bytes 44040192 | tf_op jit(solution)/shard_map/convert_element_type | solution.py:107
  105.7 8.0 %all-to-all-start = ((bf16[32,8,6,7168]{3,1,2,0:T(8,128)(2,1)}), bf16[32,8,6,7168]{3,1,2,0:T(8,128)(2,1)}, u32[]{:S(2)}, u32[]{:S(2)}) async-start(bf16[32,8,6,7168]{3,1,2,0:T(8,128)(2,1)} %copy.62), calls=%async_computation | async-start | bytes 44040192 | tf_op jit(solution)/shard_map/all_to_all | solution.py:110
  113.7 9.0 %copy.64 = bf16[1,8,192,2048]{3,1,2,0:T(8,128)(2,1)} copy(bf16[1,8,192,2048]{3,2,1,0:T(8,128)(2,1)} %param.8) | data formatting | bytes 12582912 | tf_op args[3]
  122.7 266.2 %all-to-all-done = bf16[32,8,6,7168]{3,1,2,0:T(8,128)(2,1)} async-done(((bf16[32,8,6,7168]{3,1,2,0:T(8,128)(2,1)}), bf16[32,8,6,7168]{3,1,2,0:T(8,128)(2,1)}, u32[]{:S(2)}, u32[]{:S(2)}) %all-to-all-start) | async-done | bytes 22020128 | tf_op jit(solution)/shard_map/all_to_all | solution.py:110
  388.9 22.8 %fusion.18 = bf16[8,32,6,32]{3,1,2,0:T(8,128)(2,1)S(1)} fusion(bf16[8,32,7168]{2,1,0:T(8,128)(2,1)} %param.9, bf16[32,8,6,7168]{3,1,2,0:T(8,128)(2,1)} %all-to-all-done), kind=kOutput, calls=%fused_computation.20 | convolution fusion | flops 704692224 | bytes 25788416 | tf_op jit(solution)/shard_map/sjcd,jrd->jscr/dot_general | solution.py:73
  411.6 7.0 %fusion.12 = f32[8,32,2048,1]{2,1,3,0:T(8,128)S(1)} fusion(bf16[8,32,6,32]{3,1,2,0:T(8,128)(2,1)S(1)} %fusion.18, bf16[8,32,6,2048]{3,0,2,1:T(8,128)(2,1)S(1)} %bitcast.68), kind=kOutput, calls=%fused_computation.13 | convolution fusion | flops 201326592 | bytes 8486912 | tf_op jit(solution)/shard_map/jscr,jscf->jrf/dot_general | solution.py:76
  420.2 5.3 all-to-all-start.1
  425.5 26.5 %all-to-all-done.1 = f32[4,8,32,512]{3,2,1,0:T(8,128)} async-done(((f32[4,8,32,512]{3,2,1,0:T(8,128)}), f32[4,8,32,512]{3,2,1,0:T(8,128)}, u32[]{:S(2)}, u32[]{:S(2)}) %all-to-all-start.1) | async-done | bytes 2097184 | tf_op jit(solution)/shard_map/all_to_all | solution.py:17
  455.0 3.3 all-to-all-start.2
  458.4 5.8 all-to-all-done.2
  464.5 23.4 %custom-call.8 = f32[8,32,32]{2,1,0:T(8,128)S(1)} custom-call(f32[8,32,32]{2,1,0:T(8,128)S(1)} %fusion.34), custom_call_target="Cholesky" | custom-call | tf_op jit(solution)/shard_map/jit(cholesky)/cholesky | solution.py:84
  488.2 19.7 %custom-call.9 = f32[8,1,32,32]{2,3,1,0:T(8,128)S(1)} custom-call(f32[8,1,32,32]{3,2,1,0:T(8,128)S(1)} %select_bitcast_fusion), custom_call_target="InvertDiagBlocksLowerTriangular" | custom-call | tf_op jit(solution)/shard_map/vmap(jit(_solve_triangular))/triangular_solve | solution.py:86
  508.6 18.5 %all_to_all.25 = bf16[4,8,32,512]{3,2,1,0:T(8,128)(2,1)S(1)} all-to-all(bf16[4,8,32,512]{3,2,1,0:T(8,128)(2,1)S(1)} %broadcast_in_dim.51), channel_id=1, replica_groups=mesh['expert'=32,'dp'=4] {'dp'}, dimensions={0} | all-to-all | bytes 2097152 | tf_op jit(solution)/shard_map/all_to_all | solution.py:23
  529.6 10.3 %fusion.23 = bf16[8,32,6,32]{1,3,2,0:T(8,128)(2,1)S(1)} fusion(bf16[8,32,6,2048]{3,0,2,1:T(8,128)(2,1)} %bitcast.67, bf16[8,32,2048,1]{2,1,0,3:T(8,128)(2,1)} %reshape.120), kind=kOutput, calls=%fused_computation.21 | convolution fusion | flops 201375744 | bytes 7438336 | tf_op jit(solution)/shard_map/jscf,jrf->jscr/dot_general | solution.py:117
  539.9 36.5 %fusion.7 = bf16[8,32,7168]{2,1,0:T(8,128)(2,1)S(1)} fusion(bf16[8,32,6,32]{1,3,2,0:T(8,128)(2,1)S(1)} %fusion.23, bf16[32,8,6,7168]{3,1,2,0:T(8,128)(2,1)} %all-to-all-done), kind=kOutput, calls=%fused_computation.9 | convolution fusion | flops 706478080 | bytes 25788416 | tf_op jit(solution)/shard_map/jscr,sjcd->jrd/dot_general | solution.py:80
  576.4 2.3 copy.103
  578.7 4.7 all-to-all-start.4
  585.2 41.2 %all-to-all-done.4 = bf16[4,8,32,1792]{3,2,1,0:T(8,128)(2,1)} async-done(((bf16[4,8,32,1792]{3,2,1,0:T(8,128)(2,1)}), bf16[4,8,32,1792]{3,2,1,0:T(8,128)(2,1)}, u32[]{:S(2)}, u32[]{:S(2)}) %all-to-all-start.4) | async-done | bytes 3670048 | tf_op jit(solution)/shard_map/all_to_all | solution.py:45
  626.4 4.0 convert_reduce_fusion
  (53 shorter events, 13.7 us)
Async XLA Ops:
  0.6 7.6 %copy-start = (bf16[1,128,7168]{2,1,0:T(8,128)(2,1)S(1)}, bf16[1,128,7168]{2,1,0:T(8,128)(2,1)}, u32[]{:S(2)}) copy-start(bf16[1,128,7168]{2,1,0:T(8,128)(2,1)} %param.5) | copy-start | bytes 5505028
  24.6 30.9 %copy-start.3 = (f32[1,128,8]{1,2,0:T(8,128)S(1)}, f32[1,128,8]{1,2,0:T(8,128)}, u32[]{:S(2)}) copy-start(f32[1,128,8]{1,2,0:T(8,128)} %param.7) | copy-start | bytes 12292
  105.7 283.1 %all-to-all-start = ((bf16[32,8,6,7168]{3,1,2,0:T(8,128)(2,1)}), bf16[32,8,6,7168]{3,1,2,0:T(8,128)(2,1)}, u32[]{:S(2)}, u32[]{:S(2)}) async-start(bf16[32,8,6,7168]{3,1,2,0:T(8,128)(2,1)} %copy.62), calls=%async_computation | async-start | bytes 44040192 | tf_op jit(solution)/shard_map/all_to_all | solution.py:110
  388.9 22.8 %copy-start.2 = (bf16[1,8,192,2048]{3,1,2,0:T(8,128)(2,1)S(1)}, bf16[1,8,192,2048]{3,1,2,0:T(8,128)(2,1)}, u32[]{:S(2)}) copy-start(bf16[1,8,192,2048]{3,1,2,0:T(8,128)(2,1)} %copy.64) | copy-start | bytes 18874372
  420.2 31.8 %all-to-all-start.1 = ((f32[4,8,32,512]{3,2,1,0:T(8,128)}), f32[4,8,32,512]{3,2,1,0:T(8,128)}, u32[]{:S(2)}, u32[]{:S(2)}) async-start(f32[4,8,32,512]{3,2,1,0:T(8,128)} %bitcast.72), calls=%async_computation.1 | async-start | bytes 4194304 | tf_op jit(solution)/shard_map/all_to_all | solution.py:17
  455.0 9.1 %all-to-all-start.2 = ((bf16[4,2,4096]{2,1,0:T(2,128)(2,1)}), bf16[4,2,4096]{2,1,0:T(2,128)(2,1)S(1)}, u32[]{:S(2)}, u32[]{:S(2)}) async-start(bf16[4,2,4096]{2,1,0:T(2,128)(2,1)} %reshape.127), calls=%async_computation.2 | async-start | bytes 131072 | tf_op jit(solution)/shard_map/all_to_all | solution.py:23
  578.7 47.7 %all-to-all-start.4 = ((bf16[4,8,32,1792]{3,2,1,0:T(8,128)(2,1)}), bf16[4,8,32,1792]{3,2,1,0:T(8,128)(2,1)}, u32[]{:S(2)}, u32[]{:S(2)}) async-start(bf16[4,8,32,1792]{3,2,1,0:T(8,128)(2,1)} %bitcast.69), calls=%async_computation.4 | async-start | bytes 7340032 | tf_op jit(solution)/shard_map/all_to_all | solution.py:45
  583.5 47.0 %copy-start.1 = (bf16[1,128,7168]{2,1,0:T(8,128)(2,1)S(1)}, bf16[1,128,7168]{2,1,0:T(8,128)(2,1)}, u32[]{:S(2)}) copy-start(bf16[1,128,7168]{2,1,0:T(8,128)(2,1)} %param.5) | copy-start | bytes 5505028
where the time goes:
time: 639 us; the launch traced here: 631 us
  waiting for transfers between devices  340 us (53%)
  local copies, waits for them, and re-layouts  99.9 us (16%)
  matrix products  77.4 us (12%)
  other arithmetic  72.7 us (11%)
  starting transfers between devices  21.3 us (3%)
  blocking collectives  18.5 us (3%)
    all_to_all x1, waiting for transfers between devices, local(): lax.all_to_all(routed, 'expert', split_axis=0, concat_axis=0, tiled=True)  266 us
    gather x2, local copies, waits for them, and re-layouts, local(): picked = jnp.take(out_grads[0], token_of, axis=0)  47.1 us
    all_to_all x1, waiting for transfers between devices, sum_at_owner(): lax.all_to_all(cut_along(shard, dim, length), axis, 0, 0, tiled=True)  41.2 us
    dot_general x1, matrix products, second_factor(): jnp.einsum('jscr,sjcd->jrd', projected, arrived, preferred_element_type=j...  36.5 us
    all_to_all x1, waiting for transfers between devices, sent_and_summed(): lax.all_to_all(blocks, axis, split_axis=0, concat_axis=0, tiled=True)  26.5 us
    convert_element_type x1, local copies, waits for them, and re-layouts, local(): (picked.astype(jnp.float32) * gate_of[:, None]).astype(jnp.bfloat16)  25.2 us
    another operation x4, other arithmetic, lower_inverse(): lower = jnp.linalg.cholesky(gram)  23.6 us
    dot_general x1, matrix products, first_factor(): jnp.einsum('sjcd,jrd->jscr', arrived, q_part, preferred_element_type=jnp....  22.8 us
  transfers between devices with their start and end apart: 4, of which 4 were waited for; matrix products, arithmetic and copies ran while one was open for 2% of the time, Pallas kernels for 0%

commit v1 on v0

v1 whole, which is shorter than its diff:
```python
import math

import jax
import jax.numpy as jnp
from jax import lax
from jax.experimental import pallas as pl
from jax.experimental.pallas import tpu as pltpu
from jax.sharding import Mesh, PartitionSpec as P

F32 = jnp.float32
BF16 = jnp.bfloat16
HIGHEST = lax.Precision.HIGHEST
NN = (((1,), (0,)), ((), ()))
NT = (((1,), (1,)), ((), ()))
CP = 8


def params(limit_mib=48, **kw):
    return pltpu.CompilerParams(vmem_limit_bytes=limit_mib * 2**20, **kw)


def table_kernel(ids_ref, gates_ref, out_ref):
    ids = ids_ref[...]
    gates = gates_ref[...]
    tokens, top = ids.shape
    shape = (tokens, 256)
    lane = lax.broadcasted_iota(jnp.int32, shape, 1)
    rem = lane % 128
    expert = 16 * (rem // 8) + 8 * (lane // 128) + rem % 8
    hit = jnp.zeros(shape, F32)
    gate = jnp.zeros(shape, F32)
    for k in range(top):
        same = ids[:, k : k + 1] == expert
        hit = jnp.where(same, 1.0, hit)
        gate = jnp.where(same, gates[:, k : k + 1], gate)
    row = lax.broadcasted_iota(jnp.int32, (tokens, tokens), 0)
    col = lax.broadcasted_iota(jnp.int32, (tokens, tokens), 1)
    before = jnp.where(col < row, 1.0, 0.0).astype(BF16)
    pos = lax.dot_general(before, hit.astype(BF16), NN, preferred_element_type=F32)
    code = lax.broadcasted_iota(jnp.int32, shape, 0).astype(F32) + gate
    code = jnp.where(hit > 0, code, -1.0)
    for c in range(CP):
        picked = jnp.max(jnp.where(pos == c, code, -1.0), axis=0, keepdims=True)
        out_ref[0, c : c + 1, :] = picked[:, :128]
        out_ref[1, c : c + 1, :] = picked[:, 128:]


def slot_codes(ids, gates):
    return pl.pallas_call(
        table_kernel,
        out_shape=jax.ShapeDtypeStruct((2, CP, 128), F32),
        name="slot_codes",
    )(ids, gates)


def dispatch_kernel(core_ref, codes_ref, xt_ref, out_ref):
    token = lax.broadcasted_iota(jnp.int32, (CP, 128), 1).astype(F32)
    group = 32
    for g in range(128 // group):
        rows = []
        for i in range(2):
            code = codes_ref[i, 0]
            parts = []
            for x in range(g * group, (g + 1) * group):
                u = code[:, x : x + 1] - token
                parts.append(jnp.where((u > 0) & (u < 1), u, 0.0))
            picks = jnp.concatenate(parts, axis=0).astype(BF16)
            got = lax.dot_general(picks, xt_ref[i], NT, preferred_element_type=F32)
            rows.append(got.reshape(group, CP, got.shape[1]))
        out_ref[g * group : (g + 1) * group] = jnp.concatenate(rows, axis=1).astype(BF16)


def dispatch(core, codes, xt, half):
    chips, width, tokens = xt.shape

    def code_map(i, core_ref):
        c = core_ref[0]
        return (i, c if half == 0 else 1 - c, 0, 0)

    return pl.pallas_call(
        dispatch_kernel,
        grid_spec=pltpu.PrefetchScalarGridSpec(
            num_scalar_prefetch=1,
            grid=(chips // 2,),
            in_specs=[
                pl.BlockSpec((2, 1, CP, 128), code_map),
                pl.BlockSpec((2, width, tokens), lambda i, _: (i, 0, 0)),
            ],
            out_specs=pl.BlockSpec((128, 2 * CP, width), lambda i, _: (0, i, 0)),
        ),
        out_shape=jax.ShapeDtypeStruct((128, chips * CP, width), BF16),
        compiler_params=params(),
        cost_estimate=pl.CostEstimate(
            flops=2 * 128 * CP * chips * tokens * width, bytes_accessed=128 * chips * CP * width * 2, transcendentals=0
        ),
        name="dispatch",
    )(core, codes, xt)


def mix_kernel(core_ref, own_ref, sib_ref, qt_ref, out_ref, tmp_ref):
    core = core_ref[0]
    owner = lax.broadcasted_iota(jnp.int32, (128, 256), 1) // 32
    for half, ref in enumerate((own_ref, sib_ref)):
        experts, rows, width = ref.shape
        got = lax.dot_general(
            ref[...].reshape(experts * rows, width), qt_ref[0], NN, preferred_element_type=F32
        )
        acc = got[:rows]
        for x in range(1, experts):
            acc = jnp.where(owner == x, got[x * rows : (x + 1) * rows], acc)
        place = core if half == 0 else 1 - core
        for i in range(2):
            lanes = slice(i * 128, (i + 1) * 128)
            tmp_ref[i] = acc[:, lanes]
            for c in range(6):
                out_ref[0, c, place, :, lanes] = tmp_ref[i, pl.ds(c, 16, stride=CP), :].astype(BF16)


def mix(core, own, sib, qt):
    chips = qt.shape[0]
    width = own.shape[2]
    block = pl.BlockSpec((8, 128, width), lambda i, _: (i, 0, 0))
    return pl.pallas_call(
        mix_kernel,
        grid_spec=pltpu.PrefetchScalarGridSpec(
            num_scalar_prefetch=1,
            grid=(chips,),
            in_specs=[block, block, pl.BlockSpec((1, width, 256), lambda i, _: (i, 0, 0))],
            out_specs=pl.BlockSpec((1, 6, 2, 16, 256), lambda i, _: (i, 0, 0, 0, 0)),
            scratch_shapes=[pltpu.VMEM((2, 128, 128), F32)],
        ),
        out_shape=jax.ShapeDtypeStruct((chips, 6, 2, 16, 256), BF16),
        compiler_params=params(),
        cost_estimate=pl.CostEstimate(
            flops=2 * 128 * 256 * width * 256, bytes_accessed=128 * 256 * width * 2, transcendentals=0
        ),
        name="mix",
    )(core, own, sib, qt)


def factor_kernel(parts_ref, hidden_ref, out_ref, tmp_ref, lhs_ref):
    x = pl.program_id(0)

    @pl.when(x == 0)
    def _():
        for c in range(6):
            for k in range(2):
                total = parts_ref[0, c, k].astype(F32)
                for j in range(1, parts_ref.shape[0]):
                    total = total + parts_ref[j, c, k].astype(F32)
                for i in range(2):
                    tmp_ref[i, pl.ds(k * 6 + c, 16, stride=12), :] = total[:, i * 128 : (i + 1) * 128]
        for i in range(2):
            lhs_ref[i * 128 : (i + 1) * 128] = tmp_ref[i].T

    start = pl.multiple_of(x * 32, 32)
    lhs = lhs_ref[pl.ds(start, 32), 0:192].astype(BF16)
    out_ref[0] = lax.dot_general(lhs, hidden_ref[0], NN, preferred_element_type=F32).astype(BF16)


def first_factor(parts, hidden):
    experts, slots, units = hidden.shape
    return pl.pallas_call(
        factor_kernel,
        grid=(experts,),
        in_specs=[
            pl.BlockSpec(parts.shape, lambda i: (0, 0, 0, 0, 0)),
            pl.BlockSpec((1, slots, units), lambda i: (i, 0, 0)),
        ],
        out_specs=pl.BlockSpec((1, 32, units), lambda i: (i, 0, 0)),
        out_shape=jax.ShapeDtypeStruct((experts, 32, units), BF16),
        scratch_shapes=[pltpu.VMEM((2, 256, 128), F32), pltpu.VMEM((256, 256), F32)],
        compiler_params=params(),
        name="first_factor",
    )(parts, hidden)


def ortho_kernel(parts_ref, out_ref):
    count = parts_ref.shape[1]
    factors, systems = [], []
    row = lax.broadcasted_iota(jnp.int32, (32, 32), 0)
    col = lax.broadcasted_iota(jnp.int32, (32, 32), 1)
    eye = jnp.where(row == col, 1.0, 0.0)
    for m in range(count):
        value = parts_ref[0, m].astype(F32)
        for p in range(1, parts_ref.shape[0]):
            value = value + parts_ref[p, m].astype(F32)
        factors.append(value)
        gram = lax.dot_general(value, value, NT, precision=HIGHEST, preferred_element_type=F32)
        systems.append(jnp.concatenate([gram, eye], axis=1))
    index = lax.broadcasted_iota(jnp.int32, (32, 64), 0)
    for k in range(32):
        for m in range(count):
            a = systems[m]
            inv = lax.rsqrt(a[k : k + 1, k : k + 1])
            pivot = a[k : k + 1, :] * inv
            lower = a[:, k : k + 1] * inv
            below = a - lower * pivot
            systems[m] = jnp.where(index > k, below, jnp.where(index == k, pivot, a))
    for m in range(count):
        inverse = systems[m][:, 32:]
        out_ref[m] = lax.dot_general(
            inverse, factors[m], NN, precision=HIGHEST, preferred_element_type=F32
        ).astype(BF16)


def ortho_of(parts):
    _, count, rank, units = parts.shape
    return pl.pallas_call(
        ortho_kernel,
        out_shape=jax.ShapeDtypeStruct((count, rank, units), BF16),
        compiler_params=params(),
        name="ortho",
    )(parts)


def project_kernel(ortho_ref, hidden_ref, basis_ref, out_ref, tmp_ref, rows_ref):
    x = pl.program_id(0)
    ortho = ortho_ref[0]
    basis_ref[0] = ortho.astype(F32) * math.sqrt(ortho.shape[1])
    got = lax.dot_general(ortho, hidden_ref[0], NT, preferred_element_type=F32)
    start = pl.multiple_of(x * 32, 32)
    tmp_ref[pl.ds(start, 32), 0:192] = got

    @pl.when(x == pl.num_programs(0) - 1)
    def _():
        for i in range(2):
            rows_ref[i] = tmp_ref[i * 128 : (i + 1) * 128, :].T
            for c in range(6):
                for k in range(2):
                    out_ref[c, k, :, i * 128 : (i + 1) * 128] = rows_ref[
                        i, pl.ds(k * 6 + c, 16, stride=12), :
                    ].astype(BF16)


def project(ortho, hidden):
    experts, slots, units = hidden.shape
    return pl.pallas_call(
        project_kernel,
        grid=(experts,),
        in_specs=[
            pl.BlockSpec((1, 32, units), lambda i: (i, 0, 0)),
            pl.BlockSpec((1, slots, units), lambda i: (i, 0, 0)),
        ],
        out_specs=[
            pl.BlockSpec((1, 32, units), lambda i: (i, 0, 0)),
            pl.BlockSpec((6, 2, 16, 256), lambda i: (0, 0, 0, 0)),
        ],
        out_shape=[
            jax.ShapeDtypeStruct((experts, 32, units), F32),
            jax.ShapeDtypeStruct((6, 2, 16, 256), BF16),
        ],
        scratch_shapes=[pltpu.VMEM((256, 256), F32), pltpu.VMEM((2, 256, 128), F32)],
        compiler_params=params(),
        name="project",
    )(ortho, hidden)


def terms_kernel(core_ref, own_ref, sib_ref, proj_ref, out_ref, rows_ref, sum_ref):
    core = core_ref[0]
    experts, rows, width = own_ref.shape

    @pl.when(pl.program_id(0) == 0)
    def _():
        rows_ref[...] = jnp.zeros_like(rows_ref)
        sum_ref[...] = jnp.zeros_like(sum_ref)

    for half in range(2):
        place = core if half == 0 else 1 - core
        for c in range(6):
            values = proj_ref[0, c, place].astype(F32)
            for i in range(2):
                rows_ref[i, pl.ds(half * 128 + c, 16, stride=CP), :] = values[:, i * 128 : (i + 1) * 128]
    turned = [rows_ref[i].T.astype(BF16) for i in range(2)]
    for x in range(experts):
        at = (x % 4) * 32
        lhs = turned[x // 4][at : at + 32]
        got = lax.dot_general(lhs[:, :128], own_ref[x], NN, preferred_element_type=F32)
        got = got + lax.dot_general(lhs[:, 128:], sib_ref[x], NN, preferred_element_type=F32)
        sum_ref[x * 32 : (x + 1) * 32, 0:width] = got
    for i in range(4):
        turned = sum_ref[:, i * 128 : (i + 1) * 128].T
        tall = min(width - i * 128, 128)
        rows_out = turned[:tall].astype(BF16)
        done = 0
        while done < tall:
            at = i * 128 + done
            part, offset = divmod(at, width // 4)
            step = min(tall - done, width // 4 - offset)
            out_ref[part, 0, offset : offset + step, :] = rows_out[done : done + step]
            done += step


def second_terms(core, own, sib, proj):
    chips = proj.shape[0]
    width = own.shape[2]
    block = pl.BlockSpec((8, 128, width), lambda i, _: (i, 0, 0))
    return pl.pallas_call(
        terms_kernel,
        grid_spec=pltpu.PrefetchScalarGridSpec(
            num_scalar_prefetch=1,
            grid=(chips,),
            in_specs=[block, block, pl.BlockSpec((1, 6, 2, 16, 256), lambda i, _: (i, 0, 0, 0, 0))],
            out_specs=pl.BlockSpec((4, 1, width // 4, 256), lambda i, _: (0, i, 0, 0)),
            scratch_shapes=[pltpu.VMEM((2, 256, 128), F32), pltpu.VMEM((256, 512), F32)],
        ),
        out_shape=jax.ShapeDtypeStruct((4, chips, width // 4, 256), BF16),
        compiler_params=params(),
        name="second_terms",
    )(core, own, sib, proj)


def gather_kernel(parts_ref, out_ref):
    total = parts_ref[0].astype(F32)
    for p in range(1, parts_ref.shape[0]):
        total = total + parts_ref[p].astype(F32)
    out_ref[...] = total.T


def owned_columns(parts):
    copies, columns, rows = parts.shape
    return pl.pallas_call(
        gather_kernel,
        grid=(columns // 128,),
        in_specs=[pl.BlockSpec((copies, 128, rows), lambda i: (0, i, 0))],
        out_specs=pl.BlockSpec((rows, 128), lambda i: (0, i)),
        out_shape=jax.ShapeDtypeStruct((rows, columns), F32),
        name="owned_columns",
    )(parts)


def exchange(values, axes):
    return lax.all_to_all(values, axes, split_axis=0, concat_axis=0, tiled=True)


def for_chips(turned, chips, copies):
    columns, lanes = turned.shape
    cut = turned.reshape(copies, chips, columns // (copies * chips), lanes)
    return jnp.swapaxes(cut, 0, 1).reshape(chips, columns // chips, lanes)


def local(out_grads, expert_ids, gate_probs, hidden_acts, q_previous):
    chips = lax.axis_size("chip")
    copies = lax.axis_size("dp")
    core = lax.axis_index("core").astype(jnp.int32).reshape(1)
    hidden = hidden_acts[0]
    experts, rank, width = q_previous.shape
    units = hidden.shape[2]

    codes = slot_codes(expert_ids[0], gate_probs[0])
    codes = jnp.broadcast_to(codes[None], (chips, *codes.shape)).reshape(2 * chips, CP, 128)
    codes = exchange(codes, ("chip", "core")).reshape(chips, 2, CP, 128)

    own_t = exchange(for_chips(out_grads[0].T, chips, copies), "chip")
    sib_t = lax.ppermute(own_t, "core", [(0, 1), (1, 0)])
    q_t = for_chips(q_previous.reshape(experts * rank, width).T, chips, copies)
    q_t = exchange(q_t, "chip")

    own = dispatch(core, codes, own_t, 0)
    sib = dispatch(core, codes, sib_t, 1)
    mixed = exchange(mix(core, own, sib, q_t), "chip")
    factor = first_factor(mixed, hidden)
    factor = exchange(factor, "dp").reshape(copies, experts // copies, rank, units)
    ortho = ortho_of(factor)
    ortho = exchange(jnp.broadcast_to(ortho[None], (copies, *ortho.shape)), "dp")
    ortho = ortho.reshape(experts, rank, units)
    new_basis, proj = project(ortho, hidden)
    proj = exchange(jnp.broadcast_to(proj[None], (chips, *proj.shape)), "chip")
    terms = second_terms(core, own, sib, proj)
    terms = terms.reshape(copies * chips, -1, experts * rank)
    terms = exchange(terms, ("dp", "chip")).reshape(copies, width // copies, experts * rank)
    q_update = owned_columns(terms).reshape(experts, rank, width // copies)
    return (new_basis, q_update)


def solution(mesh):
    at = mesh.axis_names.index("expert")
    shape = mesh.devices.shape
    devices = mesh.devices.reshape(*shape[:at], shape[at] // 2, 2, *shape[at + 1 :])
    names = (*mesh.axis_names[:at], "chip", "core", *mesh.axis_names[at + 1 :])
    expert = ("chip", "core")
    return jax.shard_map(
        local,
        mesh=Mesh(devices, names),
        in_specs=(
            P("dp", expert, None),
            P("dp", expert, None),
            P("dp", expert, None),
            P("dp", expert, None, None),
            P(expert, None, None),
        ),
        out_specs=(P(expert, None, None), P(expert, None, "dp")),
        check_vma=False,
    )
```

time: 639 us -> 309 us (0.48)
  waiting for transfers between devices: 340 us -> 47.9 us
  blocking collectives: 18.5 us -> 127 us
  Pallas kernels: 0 us -> 88.5 us
  local copies, waits for them, and re-layouts: 99.9 us -> 19.4 us
  matrix products: 77.4 us -> 0 us
  other arithmetic: 72.7 us -> 0 us
    all_to_all x4 -> x3, waiting for transfers between devices: 340 us -> 47.9 us  [exchange(): return lax.all_to_all(values, axes, split_axis=0, concat_axis=0, tiled=True)]
    all_to_all x1 -> x5, blocking collectives: 18.5 us -> 127 us  [exchange(): return lax.all_to_all(values, axes, split_axis=0, concat_axis=0, tiled=True)]
    pallas_call x0 -> x9, Pallas kernels: none -> 88.5 us  [the longest x1 20.4 us: mix(): pl.pallas_call(mix_kernel, grid_spec=pltpu.PrefetchScalarGridSpec(num_sca...]
    dot_general x6 -> x0, matrix products: 76.9 us -> none  [the longest x1 36.5 us: second_factor(): jnp.einsum('jscr,sjcd->jrd', projected, arrived, preferred_element_type=j...]
    gather x2 -> x0, local copies, waits for them, and re-layouts: 47.1 us -> none  [local(): picked = jnp.take(out_grads[0], token_of, axis=0)]
    another operation x10 -> x0, other arithmetic: 43.7 us -> none  [the longest x4 23.6 us: lower_inverse(): lower = jnp.linalg.cholesky(gram)]
    convert_element_type x1 -> x0, local copies, waits for them, and re-layouts: 25.2 us -> none  [local(): (picked.astype(jnp.float32) * gate_of[:, None]).astype(jnp.bfloat16)]
    convert_element_type x2 -> x0, other arithmetic: 20.4 us -> none  [the longest x1 20.4 us: local(): (picked.astype(jnp.float32) * gate_of[:, None]).astype(jnp.bfloat16)]
  transfers between devices with their start and end apart: 4 -> 4, of which waited for: 4 -> 3; matrix products, arithmetic and copies ran while one was open for 2% -> 5% of each run, Pallas kernels for 0% -> 6%
where the time goes in v1:
time: 309 us; the launch traced here: 305 us
  blocking collectives  127 us (41%)
  Pallas kernels  88.5 us (29%)
  waiting for transfers between devices  47.9 us (16%)
  starting transfers between devices  21.7 us (7%)
  local copies, waits for them, and re-layouts  19.4 us (6%)
    all_to_all x5, blocking collectives, exchange(): return lax.all_to_all(values, axes, split_axis=0, concat_axis=0, tiled=True)  127 us
    all_to_all x3, waiting for transfers between devices, exchange(): return lax.all_to_all(values, axes, split_axis=0, concat_axis=0, tiled=True)  47.9 us
    all_to_all x3, starting transfers between devices, exchange(): return lax.all_to_all(values, axes, split_axis=0, concat_axis=0, tiled=True)  21.7 us
    pallas_call x1, Pallas kernels, mix(): pl.pallas_call(mix_kernel, grid_spec=pltpu.PrefetchScalarGridSpec(num_sca...  20.4 us
    pallas_call x2, Pallas kernels, dispatch(): pl.pallas_call(dispatch_kernel, grid_spec=pltpu.PrefetchScalarGridSpec(nu...  19.8 us
    pallas_call x1, Pallas kernels, second_terms(): pl.pallas_call(terms_kernel, grid_spec=pltpu.PrefetchScalarGridSpec(num_s...  18.9 us
    pallas_call x1, Pallas kernels, owned_columns(): pl.pallas_call(gather_kernel, grid=(columns // 128,), in_specs=[pl.BlockS...  9.17 us
    pallas_call x1, Pallas kernels, project(): pl.pallas_call(project_kernel, grid=(experts,), in_specs=[pl.BlockSpec((1...  7.9 us
  transfers between devices with their start and end apart: 4, of which 3 were waited for; matrix products, arithmetic and copies ran while one was open for 5% of the time, Pallas kernels for 6%

profile of v1, /device:TPU:6, one launch (start us, length us, event | category | flops | bytes accessed | tf_op | source)
XLA Modules:
  0.0 304.9 jit_solution(6529091085631302211)
XLA Ops:
  0.6 1.4 copy.16
  3.5 2.0 slot_codes.1
  6.9 7.6 %all-to-all-start = ((f32[32,8,128]{2,1,0:T(8,128)}), f32[32,8,128]{2,1,0:T(8,128)S(1)}, u32[]{:S(2)}, u32[]{:S(2)}) async-start(f32[32,8,128]{2,1,0:T(8,128)} %bitcast.3), calls=%async_computation | async-start | bytes 262144 | tf_op jit(solution)/shard_map/all_to_all | solution.py:333
  14.4 3.3 %copy.18 = bf16[1,128,7168]{1,2,0:T(8,128)(2,1)S(1)} copy(bf16[1,128,7168]{2,1,0:T(8,128)(2,1)} %param.5) | data formatting | bytes 3670016 | tf_op args[0]
  17.7 1.4 copy.19
  20.5 5.9 %all-to-all-start.1 = ((bf16[16,448,128]{2,1,0:T(8,128)(2,1)}), bf16[16,448,128]{2,1,0:T(8,128)(2,1)S(1)}, u32[]{:S(2)}, u32[]{:S(2)}) async-start(bf16[16,448,128]{2,1,0:T(8,128)(2,1)} %bitcast.36), calls=%async_computation.1 | async-start | bytes 3670016 | tf_op jit(solution)/shard_map/all_to_all | solution.py:333
  26.4 5.9 %copy.20 = bf16[7168,256]{1,0:T(8,128)(2,1)} copy(bf16[7168,256]{0,1:T(8,128)(2,1)} %bitcast.38) | data formatting | bytes 7340032 | tf_op jit(solution)/shard_map/transpose | solution.py:356
  32.3 4.3 %copy.21 = bf16[16,4,112,256]{3,2,1,0:T(8,128)(2,1)} copy(bf16[16,4,112,256]{3,2,0,1:T(8,128)(2,1)} %bitcast.34) | data formatting | bytes 7340032 | tf_op jit(solution)/shard_map/transpose | solution.py:339
  36.6 14.8 %all-to-all-done.1.xt_ref = bf16[16,448,128]{2,1,0:T(8,128)(2,1)S(1)} async-done(((bf16[16,448,128]{2,1,0:T(8,128)(2,1)}), bf16[16,448,128]{2,1,0:T(8,128)(2,1)S(1)}, u32[]{:S(2)}, u32[]{:S(2)}) %all-to-all-start.1) | async-done | bytes 1835040 | tf_op jit(solution)/shard_map/all_to_all | solution.py:333
  51.4 8.2 %all-to-all-start.2 = ((bf16[16,448,256]{2,1,0:T(8,128)(2,1)}), bf16[16,448,256]{2,1,0:T(8,128)(2,1)}, u32[]{:S(2)}, u32[]{:S(2)}) async-start(bf16[16,448,256]{2,1,0:T(8,128)(2,1)} %bitcast.33), calls=%async_computation.2 | async-start | bytes 7340032 | tf_op jit(solution)/shard_map/all_to_all | solution.py:333
  59.6 9.2 %dispatch.2.own_ref = bf16[128,128,448]{2,1,0:T(8,128)(2,1)} custom-call(s32[1]{0:T(128)} %bitcast.core_ref, f32[16,2,8,128]{3,2,1,0:T(8,128)S(1)} %bitcast.29, bf16[16,448,128]{2,1,0:T(8,128)(2,1)S(1)} %all-to-all-done.1.xt_ref), custom_call_target="tpu_custom_call" | custom-call | flops 1879048192 | bytes 14680064 | tf_op jit(solution)/shard_map/dispatch/pallas_call | solution.py:80
  68.9 10.6 %dispatch.3.sib_ref = bf16[128,128,448]{2,1,0:T(8,128)(2,1)} custom-call(s32[1]{0:T(128)} %bitcast.core_ref, f32[16,2,8,128]{3,2,1,0:T(8,128)S(1)} %bitcast.30, bf16[16,448,128]{2,1,0:T(8,128)(2,1)} %collective-permute-done.xt_ref), custom_call_target="tpu_custom_call" | custom-call | flops 1879048192 | bytes 14680064 | tf_op jit(solution)/shard_map/dispatch/pallas_call | solution.py:80
  79.4 31.8 %all-to-all-done.2.qt_ref = bf16[16,448,256]{2,1,0:T(8,128)(2,1)} async-done(((bf16[16,448,256]{2,1,0:T(8,128)(2,1)}), bf16[16,448,256]{2,1,0:T(8,128)(2,1)}, u32[]{:S(2)}, u32[]{:S(2)}) %all-to-all-start.2) | async-done | bytes 3670048 | tf_op jit(solution)/shard_map/all_to_all | solution.py:333
  111.2 20.4 %mix.1 = bf16[16,6,2,16,256]{4,3,2,1,0:T(8,128)(2,1)S(1)} custom-call(s32[1]{0:T(128)} %bitcast.core_ref, bf16[128,128,448]{2,1,0:T(8,128)(2,1)} %dispatch.2.own_ref, bf16[128,128,448]{2,1,0:T(8,128)(2,1)} %dispatch.3.sib_ref, bf16[16,448,256]{2,1,0:T(8,128)(2,1)} %all-to-all-done.2.qt_ref), custom_call_target="tpu_custom_call" | custom-call | flops 7516192768 | bytes 29360128 | tf_op jit(solution)/shard_map/mix/pallas_call | solution.py:123
  131.6 25.3 %all_to_all.40.parts_ref = bf16[16,6,2,16,256]{4,3,2,1,0:T(8,128)(2,1)S(1)} all-to-all(bf16[16,6,2,16,256]{4,3,2,1,0:T(8,128)(2,1)S(1)} %mix.1), channel_id=1, replica_groups=mesh['chip'=16,'core'=2,'dp'=4] {'chip'}, dimensions={0} | all-to-all | bytes 3145728 | tf_op jit(solution)/shard_map/all_to_all | solution.py:333
  156.9 6.3 %first_factor.1 = bf16[8,32,2048]{2,1,0:T(8,128)(2,1)S(1)} custom-call(bf16[16,6,2,16,256]{4,3,2,1,0:T(8,128)(2,1)S(1)} %all_to_all.40.parts_ref, bf16[8,192,2048]{2,1,0:T(8,128)(2,1)} %bitcast.31), custom_call_target="tpu_custom_call" | custom-call | tf_op jit(solution)/shard_map/first_factor/pallas_call | solution.py:163
  163.2 18.4 %all_to_all.41 = bf16[8,32,2048]{2,1,0:T(8,128)(2,1)S(1)} all-to-all(bf16[8,32,2048]{2,1,0:T(8,128)(2,1)S(1)} %first_factor.1), channel_id=1, replica_groups=mesh['chip'=16,'core'=2,'dp'=4] {'dp'}, dimensions={0} | all-to-all | bytes 2097152 | tf_op jit(solution)/shard_map/all_to_all | solution.py:333
  181.6 3.9 %ortho.1 = bf16[2,32,2048]{2,1,0:T(8,128)(2,1)S(1)} custom-call(bf16[4,2,32,2048]{3,2,1,0:T(8,128)(2,1)S(1)} %bitcast.28), custom_call_target="tpu_custom_call" | custom-call | tf_op jit(solution)/shard_map/ortho/pallas_call | solution.py:209
  185.7 14.5 %all_to_all.42 = bf16[4,2,32,2048]{3,2,1,0:T(8,128)(2,1)S(1)} all-to-all(bf16[4,2,32,2048]{3,2,1,0:T(8,128)(2,1)S(1)} %broadcast_in_dim.7), channel_id=1, replica_groups=mesh['chip'=16,'core'=2,'dp'=4] {'dp'}, dimensions={0} | all-to-all | bytes 2097152 | tf_op jit(solution)/shard_map/all_to_all | solution.py:333
  200.2 7.9 %project.1 = (f32[8,32,2048]{2,1,0:T(8,128)}, bf16[6,2,16,256]{3,2,1,0:T(8,128)(2,1)S(1)}) custom-call(bf16[8,32,2048]{2,1,0:T(8,128)(2,1)S(1)} %bitcast.27, bf16[8,192,2048]{2,1,0:T(8,128)(2,1)} %bitcast.32), custom_call_target="tpu_custom_call" | custom-call | tf_op jit(solution)/shard_map/project/pallas_call | solution.py:238
  208.3 20.9 %all_to_all.43.proj_ref = bf16[16,6,2,16,256]{4,3,2,1,0:T(8,128)(2,1)S(1)} all-to-all(bf16[16,6,2,16,256]{4,3,2,1,0:T(8,128)(2,1)S(1)} %broadcast_in_dim.8), channel_id=1, replica_groups=mesh['chip'=16,'core'=2,'dp'=4] {'chip'}, dimensions={0} | all-to-all | bytes 3145728 | tf_op jit(solution)/shard_map/all_to_all | solution.py:333
  229.3 18.9 %second_terms.1 = bf16[4,16,112,256]{3,2,1,0:T(8,128)(2,1)S(1)} custom-call(s32[1]{0:T(128)} %bitcast.core_ref, bf16[128,128,448]{2,1,0:T(8,128)(2,1)} %dispatch.2.own_ref, bf16[128,128,448]{2,1,0:T(8,128)(2,1)} %dispatch.3.sib_ref, bf16[16,6,2,16,256]{4,3,2,1,0:T(8,128)(2,1)S(1)} %all_to_all.43.proj_ref), custom_call_target="tpu_custom_call" | custom-call | tf_op jit(solution)/shard_map/second_terms/pallas_call | solution.py:298
  248.1 47.6 %all_to_all.44 = bf16[64,112,256]{2,1,0:T(8,128)(2,1)} all-to-all(bf16[64,112,256]{2,1,0:T(8,128)(2,1)S(1)} %bitcast.26), channel_id=1, replica_groups=mesh['chip'=16,'core'=2,'dp'=4] {'dp','chip'}, dimensions={0} | all-to-all | bytes 7340032 | tf_op jit(solution)/shard_map/all_to_all | solution.py:333
  295.8 9.2 %owned_columns.1 = f32[256,1792]{1,0:T(8,128)} custom-call(bf16[4,1792,256]{2,1,0:T(8,128)(2,1)} %bitcast.35), custom_call_target="tpu_custom_call" | custom-call | tf_op jit(solution)/shard_map/owned_columns/pallas_call | solution.py:322
  (7 shorter events, 4.4 us)
Async XLA Ops:
  6.9 13.6 %all-to-all-start = ((f32[32,8,128]{2,1,0:T(8,128)}), f32[32,8,128]{2,1,0:T(8,128)S(1)}, u32[]{:S(2)}, u32[]{:S(2)}) async-start(f32[32,8,128]{2,1,0:T(8,128)} %bitcast.3), calls=%async_computation | async-start | bytes 262144 | tf_op jit(solution)/shard_map/all_to_all | solution.py:333
  20.5 30.9 %all-to-all-start.1 = ((bf16[16,448,128]{2,1,0:T(8,128)(2,1)}), bf16[16,448,128]{2,1,0:T(8,128)(2,1)S(1)}, u32[]{:S(2)}, u32[]{:S(2)}) async-start(bf16[16,448,128]{2,1,0:T(8,128)(2,1)} %bitcast.36), calls=%async_computation.1 | async-start | bytes 3670016 | tf_op jit(solution)/shard_map/all_to_all | solution.py:333
  51.4 59.9 %all-to-all-start.2 = ((bf16[16,448,256]{2,1,0:T(8,128)(2,1)}), bf16[16,448,256]{2,1,0:T(8,128)(2,1)}, u32[]{:S(2)}, u32[]{:S(2)}) async-start(bf16[16,448,256]{2,1,0:T(8,128)(2,1)} %bitcast.33), calls=%async_computation.2 | async-start | bytes 7340032 | tf_op jit(solution)/shard_map/all_to_all | solution.py:333
  59.6 9.2 %collective-permute-start = (bf16[16,448,128]{2,1,0:T(8,128)(2,1)S(1)}, bf16[16,448,128]{2,1,0:T(8,128)(2,1)}, u32[]{:S(2)}, u32[]{:S(2)}) collective-permute-start(bf16[16,448,128]{2,1,0:T(8,128)(2,1)S(1)} %all-to-all-done.1.xt_ref), channel_id=1, source_target_pairs={{0,4},{4,0},{1,5},{5,1},{2,6},{6,2},{3,7},{7,3},{8,12},{12,8},{9,1... | collective-permute-start | bytes 5505032 | tf_op jit(solution)/shard_map/ppermute | solution.py:355

commit v2 on v1

v2 whole, which is shorter than its diff:
```python
import math

import jax
import jax.numpy as jnp
from jax import lax
from jax.experimental import pallas as pl
from jax.experimental.pallas import tpu as pltpu
from jax.sharding import Mesh, PartitionSpec as P

F32 = jnp.float32
BF16 = jnp.bfloat16
HIGHEST = lax.Precision.HIGHEST
NN = (((1,), (0,)), ((), ()))
NT = (((1,), (1,)), ((), ()))
CP = 8
CAP = 6
STREAMS = 2


def params(limit_mib=48, **kw):
    return pltpu.CompilerParams(vmem_limit_bytes=limit_mib * 2**20, **kw)


def shape_of(shape, dtype):
    return jax.ShapeDtypeStruct(shape, dtype)


def place_rows(out_ref, turned, first, part_rows, base):
    done = 0
    while done < turned.shape[0]:
        chip, offset = divmod(first + done, part_rows)
        step = min(turned.shape[0] - done, part_rows - offset)
        out_ref[chip, base + offset : base + offset + step, :] = turned[done : done + step]
        done += step


def prepare_kernel(ids_ref, gates_ref, grads_ref, out_ref):
    ids = ids_ref[...].T
    gates = gates_ref[...].T
    chips, total, _ = out_ref.shape
    tokens, top = ids.shape
    width = grads_ref.shape[1]
    shape = (tokens, 256)
    lane = lax.broadcasted_iota(jnp.int32, shape, 1)
    rem = lane % 128
    expert = 16 * (rem // 8) + 8 * (lane // 128) + rem % 8
    hit = jnp.zeros(shape, F32)
    gate = jnp.zeros(shape, F32)
    for k in range(top):
        same = ids[:, k : k + 1] == expert
        hit = jnp.where(same, 1.0, hit)
        gate = jnp.where(same, gates[:, k : k + 1], gate)
    row = lax.broadcasted_iota(jnp.int32, (tokens, tokens), 0)
    col = lax.broadcasted_iota(jnp.int32, (tokens, tokens), 1)
    before = jnp.where(col < row, 1.0, 0.0).astype(BF16)
    pos = lax.dot_general(before, hit.astype(BF16), NN, preferred_element_type=F32)
    pos = jnp.where(hit > 0, pos, -1.0)
    token = lax.broadcasted_iota(jnp.int32, shape, 0).astype(F32)
    token_rows, gate_rows = [], []
    for c in range(CP):
        here = pos == c
        token_rows.append(jnp.max(jnp.where(here, token, -1.0), axis=0, keepdims=True))
        gate_rows.append(jnp.sum(jnp.where(here, gate, 0.0), axis=0, keepdims=True))
    table = jnp.concatenate(token_rows + gate_rows, axis=0).astype(BF16)
    table = jnp.concatenate([table[:, :128], table[:, 128:]], axis=0)
    codes_at = total - 4 * CP
    for j in range(chips):
        out_ref[j, codes_at:, :] = table
    copies = 4
    span = width // copies
    part = span // chips
    for p in range(copies):
        for n in range(span // 128):
            turned = grads_ref[:, p * span + n * 128 : p * span + (n + 1) * 128].T
            place_rows(out_ref, turned, n * 128, part, p * part)


def prepare(ids, gates, grads, chips):
    tokens, width = grads.shape
    return pl.pallas_call(
        prepare_kernel,
        out_shape=shape_of((chips, width // chips + 4 * CP, tokens), BF16),
        compiler_params=params(),
        name="prepare",
    )(ids.T, gates.T, grads)


def turn_kernel(copy_ref, q_ref, out_ref):
    for n in range(q_ref.shape[1] // 128):
        out_ref[n * 128 : (n + 1) * 128, :] = q_ref[:, n * 128 : (n + 1) * 128].T


def turned_part(copy, q, copies):
    rows, width = q.shape
    steps = 2
    columns = width // copies
    return pl.pallas_call(
        turn_kernel,
        grid_spec=pltpu.PrefetchScalarGridSpec(
            num_scalar_prefetch=1,
            grid=(steps,),
            in_specs=[pl.BlockSpec((rows, columns // steps), lambda i, c: (0, c[0] * steps + i))],
            out_specs=pl.BlockSpec((columns // steps, rows), lambda i, c: (i, 0)),
        ),
        out_shape=shape_of((columns, rows), BF16),
        compiler_params=params(),
        name="turned_part",
    )(copy, q)


def dispatch_kernel(core_ref, xt_ref, out_ref, *, half):
    core = core_ref[0]
    token = lax.broadcasted_iota(jnp.int32, (CP, 128), 1).astype(F32)
    group = 32
    width = out_ref.shape[2]
    start = pl.multiple_of(width + 2 * CP * core, 2 * CP)
    codes = []
    for i in range(2):
        table = xt_ref[i, pl.ds(start, 2 * CP), :].astype(F32)
        codes.append(table[:CP] + table[CP:])
    for g in range(128 // group):
        rows = []
        for i in range(2):
            parts = []
            for x in range(g * group, (g + 1) * group):
                u = codes[i][:, x : x + 1] - token
                parts.append(jnp.where((u > 0) & (u < 1), u, 0.0))
            picks = jnp.concatenate(parts, axis=0).astype(BF16)
            got = lax.dot_general(picks, xt_ref[i, :width], NT, preferred_element_type=F32)
            rows.append(got.reshape(group, CP, width))
        out_ref[g * group : (g + 1) * group] = jnp.concatenate(rows, axis=1).astype(BF16)


def dispatch(core, xt, half):
    chips, total, tokens = xt.shape
    width = total - 4 * CP

    def body(*refs):
        dispatch_kernel(*refs, half=half)

    return pl.pallas_call(
        body,
        grid_spec=pltpu.PrefetchScalarGridSpec(
            num_scalar_prefetch=1,
            grid=(chips // 2,),
            in_specs=[pl.BlockSpec((2, total, tokens), lambda i, _: (i, 0, 0))],
            out_specs=pl.BlockSpec((128, 2 * CP, width), lambda i, _: (0, i, 0)),
        ),
        out_shape=shape_of((128, chips * CP, width), BF16),
        compiler_params=params(),
        cost_estimate=pl.CostEstimate(
            flops=2 * 128 * CP * chips * tokens * width, bytes_accessed=128 * chips * CP * width * 2, transcendentals=0
        ),
        name=f"dispatch_{half}",
    )(core, xt)


def mix_kernel(at_ref, own_ref, sib_ref, *rest):
    q_refs, (out_ref, q_ref, tmp_ref) = rest[:-3], rest[-3:]
    core, copy = at_ref[0], at_ref[1]
    copies = len(q_refs)
    lanes = out_ref.shape[4]
    owner = lax.broadcasted_iota(jnp.int32, (128, lanes), 1) // 32
    for n in range(out_ref.shape[0]):
        part = q_refs[0].shape[1]
        for shift, ref in enumerate(q_refs):
            start = pl.multiple_of(part * ((copy + shift) % copies), 16)
            q_ref[pl.ds(start, part), :] = ref[n]
        for half, ref in enumerate((own_ref, sib_ref)):
            _, experts, rows, width = ref.shape
            got = lax.dot_general(
                ref[n].reshape(experts * rows, width), q_ref[...], NN, preferred_element_type=F32
            )
            acc = got[:rows]
            for x in range(1, experts):
                acc = jnp.where(owner == x, got[x * rows : (x + 1) * rows], acc)
            tmp_ref[...] = acc
            place = core if half == 0 else 1 - core
            for c in range(CAP):
                out_ref[n, c, place] = tmp_ref[pl.ds(c, 16, stride=CP), :].astype(BF16)


def mix(at, own, sib, q_parts, stream):
    chips, part, lanes = q_parts[0].shape
    lanes = lanes // STREAMS
    _, experts, rows, width = own.shape
    experts = experts // STREAMS
    step = 2
    block = pl.BlockSpec((step, experts, rows, width), lambda i, _: (i, stream, 0, 0))
    q_block = pl.BlockSpec((step, part, lanes), lambda i, _: (i, 0, stream))
    return pl.pallas_call(
        mix_kernel,
        grid_spec=pltpu.PrefetchScalarGridSpec(
            num_scalar_prefetch=1,
            grid=(chips // step,),
            in_specs=[block, block] + [q_block] * len(q_parts),
            out_specs=pl.BlockSpec((step, CAP, 2, 16, lanes), lambda i, _: (i, 0, 0, 0, 0)),
            scratch_shapes=[pltpu.VMEM((width, lanes), BF16), pltpu.VMEM((rows, lanes), F32)],
        ),
        out_shape=shape_of((chips, CAP, 2, 16, lanes), BF16),
        compiler_params=params(),
        cost_estimate=pl.CostEstimate(
            flops=4 * chips * experts * rows * width * 256,
            bytes_accessed=4 * chips * experts * rows * width,
            transcendentals=0,
        ),
        name=f"mix_{stream}",
    )(at, own, sib, *q_parts)


def factor_kernel(parts_ref, hidden_ref, out_ref, tmp_ref, lhs_ref):
    step = pl.program_id(0)
    here = hidden_ref.shape[0]

    @pl.when(step == 0)
    def _():
        for c in range(CAP):
            for k in range(2):
                total = parts_ref[0, c, k].astype(F32)
                for j in range(1, parts_ref.shape[0]):
                    total = total + parts_ref[j, c, k].astype(F32)
                tmp_ref[pl.ds(k * CAP + c, 16, stride=2 * CAP), :] = total
        lhs_ref[...] = tmp_ref[...].T.astype(BF16)

    for n in range(here):
        start = pl.multiple_of((step * here + n) * 32, 32)
        lhs = lhs_ref[pl.ds(start, 32), 0 : hidden_ref.shape[1]]
        out_ref[n] = lax.dot_general(lhs, hidden_ref[n], NN, preferred_element_type=F32).astype(BF16)


def first_factor(parts, hidden, stream):
    experts, slots, units = hidden.shape
    experts = experts // STREAMS
    lanes = parts.shape[4]
    step = 2
    first = stream * experts // step
    return pl.pallas_call(
        factor_kernel,
        grid=(experts // step,),
        in_specs=[
            pl.BlockSpec(parts.shape, lambda i: (0, 0, 0, 0, 0)),
            pl.BlockSpec((step, slots, units), lambda i: (first + i, 0, 0)),
        ],
        out_specs=pl.BlockSpec((step, 32, units), lambda i: (i, 0, 0)),
        out_shape=shape_of((experts, 32, units), BF16),
        scratch_shapes=[pltpu.VMEM((256, lanes), F32), pltpu.VMEM((lanes, 256), BF16)],
        compiler_params=params(),
        cost_estimate=pl.CostEstimate(
            flops=2 * experts * slots * units * 256, bytes_accessed=2 * experts * slots * units, transcendentals=0
        ),
        name=f"first_factor_{stream}",
    )(parts, hidden)


def ortho_kernel(parts_ref, out_ref):
    count = parts_ref.shape[1]
    factors, systems = [], []
    row = lax.broadcasted_iota(jnp.int32, (32, 32), 0)
    col = lax.broadcasted_iota(jnp.int32, (32, 32), 1)
    eye = jnp.where(row == col, 1.0, 0.0)
    for m in range(count):
        value = parts_ref[0, m].astype(F32)
        for p in range(1, parts_ref.shape[0]):
            value = value + parts_ref[p, m].astype(F32)
        factors.append(value)
        gram = lax.dot_general(value, value, NT, precision=HIGHEST, preferred_element_type=F32)
        systems.append(jnp.concatenate([gram, eye], axis=1))
    index = lax.broadcasted_iota(jnp.int32, (32, 64), 0)
    for k in range(32):
        for m in range(count):
            a = systems[m]
            inv = lax.rsqrt(a[k : k + 1, k : k + 1])
            pivot = a[k : k + 1, :] * inv
            lower = a[:, k : k + 1] * inv
            below = a - lower * pivot
            systems[m] = jnp.where(index > k, below, jnp.where(index == k, pivot, a))
    for m in range(count):
        inverse = systems[m][:, 32:]
        out_ref[m] = lax.dot_general(
            inverse, factors[m], NN, precision=HIGHEST, preferred_element_type=F32
        ).astype(BF16)


def ortho_of(parts, stream):
    _, count, rank, units = parts.shape
    return pl.pallas_call(
        ortho_kernel,
        out_shape=shape_of((count, rank, units), BF16),
        compiler_params=params(),
        cost_estimate=pl.CostEstimate(flops=5_000_000_000, bytes_accessed=4 * rank * units * 2, transcendentals=0),
        name=f"ortho_{stream}",
    )(parts)


def project_kernel(ortho_ref, hidden_ref, *refs):
    basis_ref, out_ref, rows_ref = refs[-3:]
    step = pl.program_id(0)
    here, slots, units = hidden_ref.shape
    start = pl.multiple_of(step * here * 32, 32)
    basis = ortho_ref[pl.ds(start, here * 32), :].astype(F32) * math.sqrt(units)
    basis_ref[...] = basis.reshape(here, 32, units)
    got = lax.dot_general(
        hidden_ref[...].reshape(here * slots, units), ortho_ref[...], NT, preferred_element_type=F32
    )
    owner = lax.broadcasted_iota(jnp.int32, (slots, ortho_ref.shape[0]), 1) // 32
    for n in range(here):
        value = got[n * slots : (n + 1) * slots]
        kept = rows_ref[...]
        rows_ref[...] = jnp.where(owner == step * here + n, value, kept)

    @pl.when(step == pl.num_programs(0) - 1)
    def _():
        for c in range(CAP):
            for k in range(2):
                out_ref[c, k] = rows_ref[pl.ds(k * CAP + c, 16, stride=2 * CAP), :].astype(BF16)


def project(ortho, hidden, stream, basis):
    every, slots, units = hidden.shape
    experts = every // STREAMS
    lanes = experts * 32
    step = 2
    first = stream * experts // step
    given = [] if basis is None else [basis]
    return pl.pallas_call(
        project_kernel,
        grid=(experts // step,),
        in_specs=[
            pl.BlockSpec((lanes, units), lambda i: (0, 0)),
            pl.BlockSpec((step, slots, units), lambda i: (first + i, 0, 0)),
        ]
        + [pl.BlockSpec(memory_space=pl.ANY)] * len(given),
        out_specs=[
            pl.BlockSpec((step, 32, units), lambda i: (first + i, 0, 0)),
            pl.BlockSpec((CAP, 2, 16, lanes), lambda i: (0, 0, 0, 0)),
        ],
        out_shape=[
            shape_of((every, 32, units), F32),
            shape_of((CAP, 2, 16, lanes), BF16),
        ],
        input_output_aliases={2: 0} if given else {},
        scratch_shapes=[pltpu.VMEM((slots, lanes), F32)],
        compiler_params=params(),
        cost_estimate=pl.CostEstimate(
            flops=2 * experts * slots * units * 256, bytes_accessed=2 * experts * slots * units, transcendentals=0
        ),
        name=f"project_{stream}",
    )(ortho, hidden, *given)


def terms_kernel(core_ref, own_ref, sib_ref, proj_ref, out_ref, rows_ref, sum_ref):
    core = core_ref[0]
    count, experts, rows, width = own_ref.shape
    part = width // 4

    @pl.when(pl.program_id(0) == 0)
    def _():
        rows_ref[...] = jnp.zeros_like(rows_ref)
        sum_ref[...] = jnp.zeros_like(sum_ref)

    for n in range(count):
        for half in range(2):
            place = core if half == 0 else 1 - core
            for c in range(CAP):
                rows_ref[pl.ds(half * 128 + c, 16, stride=CP), :] = proj_ref[n, c, place].astype(F32)
        turned = rows_ref[...].T.astype(BF16)
        for x in range(experts):
            both = jnp.concatenate([own_ref[n, x], sib_ref[n, x]], axis=0)
            got = lax.dot_general(turned[x * 32 : (x + 1) * 32], both, NN, preferred_element_type=F32)
            sum_ref[x * 32 : (x + 1) * 32, 0:width] = got
        for i in range(4):
            tall = min(width - i * 128, 128)
            back = sum_ref[:, i * 128 : (i + 1) * 128].T[:tall].astype(BF16)
            done = 0
            while done < tall:
                p, offset = divmod(i * 128 + done, part)
                step = min(tall - done, part - offset)
                out_ref[p, n, offset : offset + step, :] = back[done : done + step]
                done += step


def second_terms(core, own, sib, proj, stream):
    chips, _, _, _, lanes = proj.shape
    _, experts, rows, width = own.shape
    experts = experts // STREAMS
    step = 2
    block = pl.BlockSpec((step, experts, rows, width), lambda i, _: (i, stream, 0, 0))
    return pl.pallas_call(
        terms_kernel,
        grid_spec=pltpu.PrefetchScalarGridSpec(
            num_scalar_prefetch=1,
            grid=(chips // step,),
            in_specs=[block, block, pl.BlockSpec((step, CAP, 2, 16, lanes), lambda i, _: (i, 0, 0, 0, 0))],
            out_specs=pl.BlockSpec((4, step, width // 4, lanes), lambda i, _: (0, i, 0, 0)),
            scratch_shapes=[pltpu.VMEM((256, lanes), F32), pltpu.VMEM((lanes, 512), F32)],
        ),
        out_shape=shape_of((4, chips, width // 4, lanes), BF16),
        compiler_params=params(),
        cost_estimate=pl.CostEstimate(
            flops=4 * chips * experts * rows * width * 256,
            bytes_accessed=4 * chips * experts * rows * width,
            transcendentals=0,
        ),
        name=f"second_terms_{stream}",
    )(core, own, sib, proj)


def gather_kernel(parts_ref, *refs):
    out_ref = refs[-1]
    total = parts_ref[0].astype(F32)
    for p in range(1, parts_ref.shape[0]):
        total = total + parts_ref[p].astype(F32)
    out_ref[...] = total.T


def owned_columns(parts, stream, sums):
    copies, columns, rows = parts.shape
    given = [] if sums is None else [sums]
    wide = 896
    return pl.pallas_call(
        gather_kernel,
        grid=(columns // wide,),
        in_specs=[pl.BlockSpec((copies, wide, rows), lambda i: (0, i, 0))]
        + [pl.BlockSpec(memory_space=pl.ANY)] * len(given),
        out_specs=pl.BlockSpec((rows, wide), lambda i: (stream, i)),
        out_shape=shape_of((rows * STREAMS, columns), F32),
        input_output_aliases={1: 0} if given else {},
        compiler_params=params(),
        name=f"owned_columns_{stream}",
    )(parts, *given)


def exchange(values, axes):
    return lax.all_to_all(values, axes, split_axis=0, concat_axis=0, tiled=True)


def to_all(values, axis):
    return exchange(jnp.broadcast_to(values[None], (lax.axis_size(axis), *values.shape)), axis)


def around(part, copies):
    ahead = [(i, (i + 1) % copies) for i in range(copies)]
    back = [(i, (i - 1) % copies) for i in range(copies)]
    half = part.shape[0] // 2
    before = lax.ppermute(part, "dp", ahead)
    after = lax.ppermute(part, "dp", back)
    far_low = lax.ppermute(before[:half], "dp", ahead)
    far_high = lax.ppermute(after[half:], "dp", back)
    return [part, after, jnp.concatenate([far_low, far_high], axis=0), before]


def local(out_grads, expert_ids, gate_probs, hidden_acts, q_previous):
    chips = lax.axis_size("chip")
    copies = lax.axis_size("dp")
    core = lax.axis_index("core").astype(jnp.int32).reshape(1)
    copy = lax.axis_index("dp").astype(jnp.int32).reshape(1)
    at = jnp.concatenate([core, copy])
    hidden = hidden_acts[0]
    experts, rank, width = q_previous.shape
    units = hidden.shape[2]
    here = experts // STREAMS

    q_part = turned_part(copy, q_previous.reshape(experts * rank, width), copies)
    q_part = exchange(q_part.reshape(chips, -1, experts * rank), "chip")
    q_parts = around(q_part, copies)

    own_t = exchange(prepare(expert_ids[0], gate_probs[0], out_grads[0], chips), "chip")
    sib_t = lax.ppermute(own_t, "core", [(0, 1), (1, 0)])
    own = dispatch(core, own_t, 0)
    sib = dispatch(core, sib_t, 1)
    own = own.reshape(chips, experts, *own.shape[1:])
    sib = sib.reshape(chips, experts, *sib.shape[1:])

    basis, sums = None, None
    for s in range(STREAMS):
        mixed = exchange(mix(at, own, sib, q_parts, s), "chip")
        factor = exchange(first_factor(mixed, hidden, s), "dp")
        ortho = ortho_of(factor.reshape(copies, here // copies, rank, units), s)
        ortho = to_all(ortho, "dp").reshape(here * rank, units)
        basis, proj = project(ortho, hidden, s, basis)
        terms = second_terms(core, own, sib, to_all(proj, "chip"), s)
        terms = exchange(terms.reshape(copies * chips, -1, here * rank), ("dp", "chip"))
        sums = owned_columns(terms.reshape(copies, width // copies, here * rank), s, sums)
    return (basis, sums.reshape(experts, rank, width // copies))


def solution(mesh):
    at = mesh.axis_names.index("expert")
    shape = mesh.devices.shape
    devices = mesh.devices.reshape(*shape[:at], shape[at] // 2, 2, *shape[at + 1 :])
    names = (*mesh.axis_names[:at], "chip", "core", *mesh.axis_names[at + 1 :])
    expert = ("chip", "core")
    return jax.shard_map(
        local,
        mesh=Mesh(devices, names),
        in_specs=(
            P("dp", expert, None),
            P("dp", expert, None),
            P("dp", expert, None),
            P("dp", expert, None, None),
            P(expert, None, None),
        ),
        out_specs=(P(expert, None, None), P(expert, None, "dp")),
        check_vma=False,
    )
```

time: 309 us -> 298 us (0.964)
  blocking collectives: 127 us -> 0 us
  waiting for transfers between devices: 47.9 us -> 107 us
  starting transfers between devices: 21.7 us -> 77.9 us
    all_to_all x5 -> x0, blocking collectives: 127 us -> none  [exchange(): return lax.all_to_all(values, axes, split_axis=0, concat_axis=0, tiled=True)]
    all_to_all x3 -> x12, starting transfers between devices: 21.7 us -> 70.9 us  [exchange(): return lax.all_to_all(values, axes, split_axis=0, concat_axis=0, tiled=True)]
    all_to_all x3 -> x12, waiting for transfers between devices: 47.9 us -> 87.2 us  [exchange(): return lax.all_to_all(values, axes, split_axis=0, concat_axis=0, tiled=True)]
    ppermute x0 -> x4, waiting for transfers between devices: none -> 19.7 us  [the longest x1 19.7 us: around(): before = lax.ppermute(part, 'dp', ahead)]
    transpose x3 -> x0, local copies, waits for them, and re-layouts: 11.6 us -> none  [the longest x1 5.9 us: local(): q_t = for_chips(q_previous.reshape(experts * rank, width).T, chips, copies)]
    ppermute x0 -> x4, starting transfers between devices: none -> 7.03 us  [the longest x1 2.99 us: around(): far_high = lax.ppermute(after[half:], 'dp', back)]
    unnamed x3 -> x35, local copies, waits for them, and re-layouts: 6.13 us -> 11.7 us
    pallas_call x1 -> x2, Pallas kernels: 20.4 us -> 22.1 us  [mix(): pl.pallas_call(mix_kernel, grid_spec=pltpu.PrefetchScalarGridSpec(num_sca...]
  transfers between devices with their start and end apart: 4 -> 17, of which waited for: 3 -> 11; matrix products, arithmetic and copies ran while one was open for 5% -> 1% of each run, Pallas kernels for 6% -> 21%
where the time goes in v2:
time: 298 us; the launch traced here: 294 us
  waiting for transfers between devices  107 us (36%)
  Pallas kernels  90 us (30%)
  starting transfers between devices  77.9 us (26%)
  local copies, waits for them, and re-layouts  18.2 us (6%)
    all_to_all x12, waiting for transfers between devices, exchange(): return lax.all_to_all(values, axes, split_axis=0, concat_axis=0, tiled=True)  87.2 us
    all_to_all x12, starting transfers between devices, exchange(): return lax.all_to_all(values, axes, split_axis=0, concat_axis=0, tiled=True)  70.9 us
    pallas_call x2, Pallas kernels, mix(): pl.pallas_call(mix_kernel, grid_spec=pltpu.PrefetchScalarGridSpec(num_sca...  22.1 us
    pallas_call x2, Pallas kernels, dispatch(): pl.pallas_call(body, grid_spec=pltpu.PrefetchScalarGridSpec(num_scalar_pr...  20.4 us
    pallas_call x2, Pallas kernels, second_terms(): pl.pallas_call(terms_kernel, grid_spec=pltpu.PrefetchScalarGridSpec(num_s...  20 us
    ppermute x1, waiting for transfers between devices, around(): before = lax.ppermute(part, 'dp', ahead)  19.7 us
    unnamed x35, local copies, waits for them, and re-layouts  11.7 us
    pallas_call x2, Pallas kernels, ortho_of(): pl.pallas_call(ortho_kernel, out_shape=shape_of((count, rank, units), BF1...  7.43 us
  transfers between devices with their start and end apart: 17, of which 11 were waited for; matrix products, arithmetic and copies ran while one was open for 1% of the time, Pallas kernels for 21%

profile of v2, /device:TPU:6, one launch (start us, length us, event | category | flops | bytes accessed | tf_op | source)
XLA Modules:
  0.0 294.1 jit_solution(6919140578331118654)
XLA Ops:
  6.0 7.4 %all-to-all-start = ((bf16[16,480,128]{2,1,0:T(8,128)(2,1)}), bf16[16,480,128]{2,1,0:T(8,128)(2,1)S(1)}, u32[]{:S(2)}, u32[]{:S(2)}) async-start(bf16[16,480,128]{2,1,0:T(8,128)(2,1)} %prepare.1), calls=%async_computation | async-start | bytes 3932160 | tf_op jit(solution)/shard_map/all_to_all | solution.py:434
  16.9 22.6 %all-to-all-done.refs_1_ = bf16[16,480,128]{2,1,0:T(8,128)(2,1)S(1)} async-done(((bf16[16,480,128]{2,1,0:T(8,128)(2,1)}), bf16[16,480,128]{2,1,0:T(8,128)(2,1)S(1)}, u32[]{:S(2)}, u32[]{:S(2)}) %all-to-all-start) | async-done | bytes 1966112 | tf_op jit(solution)/shard_map/all_to_all | solution.py:434
  39.4 7.4 %all-to-all-start.1 = ((bf16[16,112,256]{2,1,0:T(8,128)(2,1)}), bf16[16,112,256]{2,1,0:T(8,128)(2,1)S(1)}, u32[]{:S(2)}, u32[]{:S(2)}) async-start(bf16[16,112,256]{2,1,0:T(8,128)(2,1)} %bitcast.28), calls=%async_computation.1 | async-start | bytes 1835008 | tf_op jit(solution)/shard_map/all_to_all | solution.py:434
  46.9 12.7 %all-to-all-done.1.rest_0_ = bf16[16,112,256]{2,1,0:T(8,128)(2,1)S(1)} async-done(((bf16[16,112,256]{2,1,0:T(8,128)(2,1)}), bf16[16,112,256]{2,1,0:T(8,128)(2,1)S(1)}, u32[]{:S(2)}, u32[]{:S(2)}) %all-to-all-start.1) | async-done | bytes 917536 | tf_op jit(solution)/shard_map/all_to_all | solution.py:434
  63.6 19.7 %collective-permute-done.2.rest_3_ = bf16[16,112,256]{2,1,0:T(8,128)(2,1)S(1)} collective-permute-done((bf16[16,112,256]{2,1,0:T(8,128)(2,1)S(1)}, bf16[16,112,256]{2,1,0:T(8,128)(2,1)S(1)}, u32[]{:S(2)}, u32[]{:S(2)}) %collective-permute-start.2) | collective-permute-done | bytes 917536 | tf_op jit(solution)/shard_map/ppermute | solution.py:445
  88.6 9.3 %dispatch_0.1 = bf16[128,128,448]{2,1,0:T(8,128)(2,1)} custom-call(s32[1]{0:T(128)} %bitcast.refs_0_.core_ref, bf16[16,480,128]{2,1,0:T(8,128)(2,1)S(1)} %all-to-all-done.refs_1_), custom_call_target="tpu_custom_call" | custom-call | flops 1879048192 | bytes 14680064 | tf_op jit(solution)/shard_map/dispatch_0/pallas_call | solution.py:141
  99.0 11.1 %dispatch_1.1 = bf16[128,128,448]{2,1,0:T(8,128)(2,1)} custom-call(s32[1]{0:T(128)} %bitcast.refs_0_.core_ref, bf16[16,480,128]{2,1,0:T(8,128)(2,1)} %collective-permute-done.refs_1_), custom_call_target="tpu_custom_call" | custom-call | flops 1879048192 | bytes 14680064 | tf_op jit(solution)/shard_map/dispatch_1/pallas_call | solution.py:141
  110.1 11.0 %mix_0.1 = bf16[16,6,2,16,128]{4,3,2,1,0:T(8,128)(2,1)S(1)} custom-call(s32[2]{0:T(128)S(1)} %pad_add_fusion.at_ref, bf16[16,8,128,448]{3,2,1,0:T(8,128)(2,1)} %bitcast.39, bf16[16,8,128,448]{3,2,1,0:T(8,128)(2,1)} %bitcast.43, bf16[16,112,256]{2,1,0:T(8,128)(2,1)S(1)} %all-to-all-done.1.rest_0_, bf16[16,112,256]{2,1,0:T(8,128)(2,1)S(1)} %copy-done.6, ...), custom_call_target="tpu_custom_call" | custom-call | flops 3758096384 | bytes 14680064 | tf_op jit(solution)/shard_map/mix_0/pallas_call | solution.py:191
  122.1 6.3 %all-to-all-start.5 = ((bf16[16,6,2,16,128]{4,3,2,1,0:T(8,128)(2,1)}), bf16[16,6,2,16,128]{4,3,2,1,0:T(8,128)(2,1)}, u32[]{:S(2)}, u32[]{:S(2)}) async-start(bf16[16,6,2,16,128]{4,3,2,1,0:T(8,128)(2,1)} %copy-done.13), calls=%async_computation.5 | async-start | bytes 1572864 | tf_op jit(solution)/shard_map/all_to_all | solution.py:434
  129.5 11.0 %mix_1.1 = bf16[16,6,2,16,128]{4,3,2,1,0:T(8,128)(2,1)S(1)} custom-call(s32[2]{0:T(128)S(1)} %pad_add_fusion.at_ref, bf16[16,8,128,448]{3,2,1,0:T(8,128)(2,1)} %bitcast.40, bf16[16,8,128,448]{3,2,1,0:T(8,128)(2,1)} %bitcast.44, bf16[16,112,256]{2,1,0:T(8,128)(2,1)S(1)} %all-to-all-done.1.rest_0_, bf16[16,112,256]{2,1,0:T(8,128)(2,1)S(1)} %copy-done.7, ...), custom_call_target="tpu_custom_call" | custom-call | flops 3758096384 | bytes 14680064 | tf_op jit(solution)/shard_map/mix_1/pallas_call | solution.py:191
  141.5 7.2 %all-to-all-start.2 = ((bf16[16,6,2,16,128]{4,3,2,1,0:T(8,128)(2,1)}), bf16[16,6,2,16,128]{4,3,2,1,0:T(8,128)(2,1)S(1)}, u32[]{:S(2)}, u32[]{:S(2)}) async-start(bf16[16,6,2,16,128]{4,3,2,1,0:T(8,128)(2,1)} %copy-done.12), calls=%async_computation.2 | async-start | bytes 1572864 | tf_op jit(solution)/shard_map/all_to_all | solution.py:434
  152.0 6.4 %all-to-all-done.2.parts_ref = bf16[16,6,2,16,128]{4,3,2,1,0:T(8,128)(2,1)S(1)} async-done(((bf16[16,6,2,16,128]{4,3,2,1,0:T(8,128)(2,1)}), bf16[16,6,2,16,128]{4,3,2,1,0:T(8,128)(2,1)S(1)}, u32[]{:S(2)}, u32[]{:S(2)}) %all-to-all-start.2) | async-done | bytes 786464 | tf_op jit(solution)/shard_map/all_to_all | solution.py:434
  165.6 4.9 %all-to-all-done.6 = bf16[4,32,2048]{2,1,0:T(8,128)(2,1)S(1)} async-done(((bf16[4,32,2048]{2,1,0:T(8,128)(2,1)}), bf16[4,32,2048]{2,1,0:T(8,128)(2,1)S(1)}, u32[]{:S(2)}, u32[]{:S(2)}) %all-to-all-start.6) | async-done | bytes 524320 | tf_op jit(solution)/shard_map/all_to_all | solution.py:434
  177.7 4.3 %all-to-all-done.3 = bf16[4,32,2048]{2,1,0:T(8,128)(2,1)S(1)} async-done(((bf16[4,32,2048]{2,1,0:T(8,128)(2,1)}), bf16[4,32,2048]{2,1,0:T(8,128)(2,1)S(1)}, u32[]{:S(2)}, u32[]{:S(2)}) %all-to-all-start.3) | async-done | bytes 524320 | tf_op jit(solution)/shard_map/all_to_all | solution.py:434
  202.2 4.6 %all-to-all-done.4 = bf16[4,1,32,2048]{3,2,1,0:T(8,128)(2,1)S(1)} async-done(((bf16[4,1,32,2048]{3,2,1,0:T(8,128)(2,1)}), bf16[4,1,32,2048]{3,2,1,0:T(8,128)(2,1)S(1)}, u32[]{:S(2)}, u32[]{:S(2)}) %all-to-all-start.4) | async-done | bytes 524320 | tf_op jit(solution)/shard_map/all_to_all | solution.py:434
  207.8 6.2 %all-to-all-start.10 = ((bf16[16,6,2,16,128]{4,3,2,1,0:T(8,128)(2,1)}), bf16[16,6,2,16,128]{4,3,2,1,0:T(8,128)(2,1)S(1)}, u32[]{:S(2)}, u32[]{:S(2)}) async-start(bf16[16,6,2,16,128]{4,3,2,1,0:T(8,128)(2,1)} %broadcast_in_dim.33), calls=%async_computation.10 | async-start | bytes 1572864 | tf_op jit(solution)/shard_map/all_to_all | solution.py:434
  217.5 5.5 %all-to-all-done.10.proj_ref = bf16[16,6,2,16,128]{4,3,2,1,0:T(8,128)(2,1)S(1)} async-done(((bf16[16,6,2,16,128]{4,3,2,1,0:T(8,128)(2,1)}), bf16[16,6,2,16,128]{4,3,2,1,0:T(8,128)(2,1)S(1)}, u32[]{:S(2)}, u32[]{:S(2)}) %all-to-all-start.10) | async-done | bytes 786464 | tf_op jit(solution)/shard_map/all_to_all | solution.py:434
  224.1 6.3 %all-to-all-start.8 = ((bf16[16,6,2,16,128]{4,3,2,1,0:T(8,128)(2,1)}), bf16[16,6,2,16,128]{4,3,2,1,0:T(8,128)(2,1)S(1)}, u32[]{:S(2)}, u32[]{:S(2)}) async-start(bf16[16,6,2,16,128]{4,3,2,1,0:T(8,128)(2,1)} %broadcast_in_dim.32), calls=%async_computation.8 | async-start | bytes 1572864 | tf_op jit(solution)/shard_map/all_to_all | solution.py:434
  230.4 10.0 %second_terms_0.1 = bf16[4,16,112,128]{3,2,1,0:T(8,128)(2,1)S(1)} custom-call(s32[1]{0:T(128)} %bitcast.refs_0_.core_ref, bf16[16,8,128,448]{3,2,1,0:T(8,128)(2,1)} %bitcast.41, bf16[16,8,128,448]{3,2,1,0:T(8,128)(2,1)} %bitcast.45, bf16[16,6,2,16,128]{4,3,2,1,0:T(8,128)(2,1)S(1)} %all-to-all-done.10.proj_ref), custom_call_target="tpu_custom_call" | custom-call | flops 3758096384 | bytes 14680064 | tf_op jit(solution)/shard_map/second_terms_0/pallas_call | solution.py:388
  241.6 8.4 %all-to-all-start.11 = ((bf16[64,112,128]{2,1,0:T(8,128)(2,1)}), bf16[64,112,128]{2,1,0:T(8,128)(2,1)S(1)}, u32[]{:S(2)}, u32[]{:S(2)}) async-start(bf16[64,112,128]{2,1,0:T(8,128)(2,1)} %bitcast.26), calls=%async_computation.11 | async-start | bytes 3670016 | tf_op jit(solution)/shard_map/all_to_all | solution.py:434
  250.1 10.0 %second_terms_1.1 = bf16[4,16,112,128]{3,2,1,0:T(8,128)(2,1)S(1)} custom-call(s32[1]{0:T(128)} %bitcast.refs_0_.core_ref, bf16[16,8,128,448]{3,2,1,0:T(8,128)(2,1)} %bitcast.42, bf16[16,8,128,448]{3,2,1,0:T(8,128)(2,1)} %bitcast.46, bf16[16,6,2,16,128]{4,3,2,1,0:T(8,128)(2,1)S(1)} %all-to-all-done.8.proj_ref), custom_call_target="tpu_custom_call" | custom-call | flops 3758096384 | bytes 14680064 | tf_op jit(solution)/shard_map/second_terms_1/pallas_call | solution.py:388
  261.3 5.9 %all-to-all-done.11 = bf16[64,112,128]{2,1,0:T(8,128)(2,1)S(1)} async-done(((bf16[64,112,128]{2,1,0:T(8,128)(2,1)}), bf16[64,112,128]{2,1,0:T(8,128)(2,1)S(1)}, u32[]{:S(2)}, u32[]{:S(2)}) %all-to-all-start.11) | async-done | bytes 1835040 | tf_op jit(solution)/shard_map/all_to_all | solution.py:434
  267.2 7.2 %all-to-all-start.9 = ((bf16[64,112,128]{2,1,0:T(8,128)(2,1)}), bf16[64,112,128]{2,1,0:T(8,128)(2,1)}, u32[]{:S(2)}, u32[]{:S(2)}) async-start(bf16[64,112,128]{2,1,0:T(8,128)(2,1)} %bitcast.27), calls=%async_computation.9 | async-start | bytes 3670016 | tf_op jit(solution)/shard_map/all_to_all | solution.py:434
  275.8 15.9 %all-to-all-done.9 = bf16[64,112,128]{2,1,0:T(8,128)(2,1)} async-done(((bf16[64,112,128]{2,1,0:T(8,128)(2,1)}), bf16[64,112,128]{2,1,0:T(8,128)(2,1)}, u32[]{:S(2)}, u32[]{:S(2)}) %all-to-all-start.9) | async-done | bytes 1835040 | tf_op jit(solution)/shard_map/all_to_all | solution.py:434
  (69 shorter events, 71.6 us)
Async XLA Ops:
  0.6 1.5 copy-start.14
  6.0 33.5 %all-to-all-start = ((bf16[16,480,128]{2,1,0:T(8,128)(2,1)}), bf16[16,480,128]{2,1,0:T(8,128)(2,1)S(1)}, u32[]{:S(2)}, u32[]{:S(2)}) async-start(bf16[16,480,128]{2,1,0:T(8,128)(2,1)} %prepare.1), calls=%async_computation | async-start | bytes 3932160 | tf_op jit(solution)/shard_map/all_to_all | solution.py:434
  13.4 2.0 copy-start.11
  39.4 20.1 %all-to-all-start.1 = ((bf16[16,112,256]{2,1,0:T(8,128)(2,1)}), bf16[16,112,256]{2,1,0:T(8,128)(2,1)S(1)}, u32[]{:S(2)}, u32[]{:S(2)}) async-start(bf16[16,112,256]{2,1,0:T(8,128)(2,1)} %bitcast.28), calls=%async_computation.1 | async-start | bytes 1835008 | tf_op jit(solution)/shard_map/all_to_all | solution.py:434
  46.9 52.1 %collective-permute-start = (bf16[16,480,128]{2,1,0:T(8,128)(2,1)S(1)}, bf16[16,480,128]{2,1,0:T(8,128)(2,1)}, u32[]{:S(2)}, u32[]{:S(2)}) collective-permute-start(bf16[16,480,128]{2,1,0:T(8,128)(2,1)S(1)} %all-to-all-done.refs_1_), channel_id=1, source_target_pairs={{0,4},{4,0},{1,5},{5,1},{2,6},{6,2},{3,7},{7,3},{8,12},{12,8},{9,1... | collective-permute-start | bytes 5898248 | tf_op jit(solution)/shard_map/ppermute | solution.py:468
  59.6 23.8 %collective-permute-start.2 = (bf16[16,112,256]{2,1,0:T(8,128)(2,1)S(1)}, bf16[16,112,256]{2,1,0:T(8,128)(2,1)S(1)}, u32[]{:S(2)}, u32[]{:S(2)}) collective-permute-start(bf16[16,112,256]{2,1,0:T(8,128)(2,1)S(1)} %all-to-all-done.1.rest_0_), channel_id=1, source_target_pairs={{0,1},{1,2},{2,3},{3,0},{4,5},{5,6},{6,7},{7,4},{8,9},{9,10},{10,1... | collective-permute-start | bytes 2752520 | tf_op jit(solution)/shard_map/ppermute | solution.py:445
  61.5 22.7 %collective-permute-start.1 = (bf16[16,112,256]{2,1,0:T(8,128)(2,1)S(1)}, bf16[16,112,256]{2,1,0:T(8,128)(2,1)S(1)}, u32[]{:S(2)}, u32[]{:S(2)}) collective-permute-start(bf16[16,112,256]{2,1,0:T(8,128)(2,1)S(1)} %all-to-all-done.1.rest_0_), channel_id=1, source_target_pairs={{0,3},{1,0},{2,1},{3,2},{4,7},{5,4},{6,5},{7,6},{8,11},{9,8},{10,9... | collective-permute-start | bytes 2752520 | tf_op jit(solution)/shard_map/ppermute | solution.py:446
  84.2 13.7 %collective-permute-start.3 = (bf16[8,112,256]{2,1,0:T(8,128)(2,1)}, bf16[8,112,256]{2,1,0:T(8,128)(2,1)S(1)}, u32[]{:S(2)}, u32[]{:S(2)}) collective-permute-start(bf16[8,112,256]{2,1,0:T(8,128)(2,1)} %slice.8), channel_id=1, source_target_pairs={{0,1},{1,2},{2,3},{3,0},{4,5},{5,6},{6,7},{7,4},{8,9},{9,10},{10,1... | collective-permute-start | bytes 1376264 | tf_op jit(solution)/shard_map/ppermute | solution.py:447
  85.5 12.4 %collective-permute-start.4 = (bf16[8,112,256]{2,1,0:T(8,128)(2,1)}, bf16[8,112,256]{2,1,0:T(8,128)(2,1)}, u32[]{:S(2)}, u32[]{:S(2)}) collective-permute-start(bf16[8,112,256]{2,1,0:T(8,128)(2,1)} %slice.9), channel_id=1, source_target_pairs={{0,3},{1,0},{2,1},{3,2},{4,7},{5,4},{6,5},{7,6},{8,11},{9,8},{10,9... | collective-permute-start | bytes 1376264 | tf_op jit(solution)/shard_map/ppermute | solution.py:448
  99.0 11.1 %copy-start.8 = (bf16[16,112,256]{2,1,0:T(8,128)(2,1)}, bf16[16,112,256]{2,1,0:T(8,128)(2,1)S(1)}, u32[]{:S(2)}) copy-start(bf16[16,112,256]{2,1,0:T(8,128)(2,1)S(1)} %constant_dynamic-update-slice_fusion.rest_2_) | copy-start | bytes 2752516
  99.0 11.1 %copy-start.3 = (bf16[16,112,256]{2,1,0:T(8,128)(2,1)S(1)}, bf16[16,112,256]{2,1,0:T(8,128)(2,1)}, u32[]{:S(2)}) copy-start(bf16[16,112,256]{2,1,0:T(8,128)(2,1)} %copy-done.2) | copy-start | bytes 2752516
  99.0 11.1 %copy-start.6 = (bf16[16,112,256]{2,1,0:T(8,128)(2,1)S(1)}, bf16[16,112,256]{2,1,0:T(8,128)(2,1)}, u32[]{:S(2)}) copy-start(bf16[16,112,256]{2,1,0:T(8,128)(2,1)} %copy-done.5) | copy-start | bytes 2752516
  110.1 18.2 %copy-start.7 = (bf16[16,112,256]{2,1,0:T(8,128)(2,1)S(1)}, bf16[16,112,256]{2,1,0:T(8,128)(2,1)}, u32[]{:S(2)}) copy-start(bf16[16,112,256]{2,1,0:T(8,128)(2,1)} %copy-done.5) | copy-start | bytes 2752516
  122.1 6.3 %copy-start.4 = (bf16[16,112,256]{2,1,0:T(8,128)(2,1)S(1)}, bf16[16,112,256]{2,1,0:T(8,128)(2,1)}, u32[]{:S(2)}) copy-start(bf16[16,112,256]{2,1,0:T(8,128)(2,1)} %copy-done.2) | copy-start | bytes 2752516
  122.1 19.4 %all-to-all-start.5 = ((bf16[16,6,2,16,128]{4,3,2,1,0:T(8,128)(2,1)}), bf16[16,6,2,16,128]{4,3,2,1,0:T(8,128)(2,1)}, u32[]{:S(2)}, u32[]{:S(2)}) async-start(bf16[16,6,2,16,128]{4,3,2,1,0:T(8,128)(2,1)} %copy-done.13), calls=%async_computation.5 | async-start | bytes 1572864 | tf_op jit(solution)/shard_map/all_to_all | solution.py:434
  141.5 17.0 %all-to-all-start.2 = ((bf16[16,6,2,16,128]{4,3,2,1,0:T(8,128)(2,1)}), bf16[16,6,2,16,128]{4,3,2,1,0:T(8,128)(2,1)S(1)}, u32[]{:S(2)}, u32[]{:S(2)}) async-start(bf16[16,6,2,16,128]{4,3,2,1,0:T(8,128)(2,1)} %copy-done.12), calls=%async_computation.2 | async-start | bytes 1572864 | tf_op jit(solution)/shard_map/all_to_all | solution.py:434
  158.5 12.1 %all-to-all-start.6 = ((bf16[4,32,2048]{2,1,0:T(8,128)(2,1)}), bf16[4,32,2048]{2,1,0:T(8,128)(2,1)S(1)}, u32[]{:S(2)}, u32[]{:S(2)}) async-start(bf16[4,32,2048]{2,1,0:T(8,128)(2,1)} %first_factor_0.1), calls=%async_computation.6 | async-start | bytes 1048576 | tf_op jit(solution)/shard_map/all_to_all | solution.py:434
  170.5 11.5 %all-to-all-start.3 = ((bf16[4,32,2048]{2,1,0:T(8,128)(2,1)}), bf16[4,32,2048]{2,1,0:T(8,128)(2,1)S(1)}, u32[]{:S(2)}, u32[]{:S(2)}) async-start(bf16[4,32,2048]{2,1,0:T(8,128)(2,1)} %first_factor_1.1), calls=%async_computation.3 | async-start | bytes 1048576 | tf_op jit(solution)/shard_map/all_to_all | solution.py:434
  182.9 11.5 %all-to-all-start.7 = ((bf16[4,1,32,2048]{3,2,1,0:T(8,128)(2,1)}), bf16[4,1,32,2048]{3,2,1,0:T(8,128)(2,1)S(1)}, u32[]{:S(2)}, u32[]{:S(2)}) async-start(bf16[4,1,32,2048]{3,2,1,0:T(8,128)(2,1)} %broadcast_in_dim.15), calls=%async_computation.7 | async-start | bytes 1048576 | tf_op jit(solution)/shard_map/all_to_all | solution.py:434
  195.3 11.5 %all-to-all-start.4 = ((bf16[4,1,32,2048]{3,2,1,0:T(8,128)(2,1)}), bf16[4,1,32,2048]{3,2,1,0:T(8,128)(2,1)S(1)}, u32[]{:S(2)}, u32[]{:S(2)}) async-start(bf16[4,1,32,2048]{3,2,1,0:T(8,128)(2,1)} %broadcast_in_dim.13), calls=%async_computation.4 | async-start | bytes 1048576 | tf_op jit(solution)/shard_map/all_to_all | solution.py:434
  207.8 15.2 %all-to-all-start.10 = ((bf16[16,6,2,16,128]{4,3,2,1,0:T(8,128)(2,1)}), bf16[16,6,2,16,128]{4,3,2,1,0:T(8,128)(2,1)S(1)}, u32[]{:S(2)}, u32[]{:S(2)}) async-start(bf16[16,6,2,16,128]{4,3,2,1,0:T(8,128)(2,1)} %broadcast_in_dim.33), calls=%async_computation.10 | async-start | bytes 1572864 | tf_op jit(solution)/shard_map/all_to_all | solution.py:434
  224.1 17.5 %all-to-all-start.8 = ((bf16[16,6,2,16,128]{4,3,2,1,0:T(8,128)(2,1)}), bf16[16,6,2,16,128]{4,3,2,1,0:T(8,128)(2,1)S(1)}, u32[]{:S(2)}, u32[]{:S(2)}) async-start(bf16[16,6,2,16,128]{4,3,2,1,0:T(8,128)(2,1)} %broadcast_in_dim.32), calls=%async_computation.8 | async-start | bytes 1572864 | tf_op jit(solution)/shard_map/all_to_all | solution.py:434
  241.6 25.6 %all-to-all-start.11 = ((bf16[64,112,128]{2,1,0:T(8,128)(2,1)}), bf16[64,112,128]{2,1,0:T(8,128)(2,1)S(1)}, u32[]{:S(2)}, u32[]{:S(2)}) async-start(bf16[64,112,128]{2,1,0:T(8,128)(2,1)} %bitcast.26), calls=%async_computation.11 | async-start | bytes 3670016 | tf_op jit(solution)/shard_map/all_to_all | solution.py:434
  267.2 24.4 %all-to-all-start.9 = ((bf16[64,112,128]{2,1,0:T(8,128)(2,1)}), bf16[64,112,128]{2,1,0:T(8,128)(2,1)}, u32[]{:S(2)}, u32[]{:S(2)}) async-start(bf16[64,112,128]{2,1,0:T(8,128)(2,1)} %bitcast.27), calls=%async_computation.9 | async-start | bytes 3670016 | tf_op jit(solution)/shard_map/all_to_all | solution.py:434
  (10 other events, 9.9 us)

commit v3 on v2

--- a/solution.py
+++ b/solution.py
@@ -6,6 +6,7 @@
 from jax.experimental import pallas as pl
 from jax.experimental.pallas import tpu as pltpu
 from jax.sharding import Mesh, PartitionSpec as P
+
 
 F32 = jnp.float32
 BF16 = jnp.bfloat16
@@ -23,6 +24,14 @@
 
 def shape_of(shape, dtype):
     return jax.ShapeDtypeStruct(shape, dtype)
+
+
+def in_hbm(shape, dtype):
+    return pltpu.HBM(shape, dtype)
+
+
+def from_hbm(value):
+    return pltpu.with_memory_space_constraint(value, pltpu.HBM)
 
 
 def place_rows(out_ref, turned, first, part_rows, base):
@@ -79,10 +88,10 @@
     tokens, width = grads.shape
     return pl.pallas_call(
         prepare_kernel,
-        out_shape=shape_of((chips, width // chips + 4 * CP, tokens), BF16),
+        out_shape=in_hbm((chips, width // chips + 4 * CP, tokens), BF16),
         compiler_params=params(),
         name="prepare",
-    )(ids.T, gates.T, grads)
+    )(from_hbm(ids.T), from_hbm(gates.T), from_hbm(grads))
 
 
 def turn_kernel(copy_ref, q_ref, out_ref):
@@ -102,13 +111,13 @@
             in_specs=[pl.BlockSpec((rows, columns // steps), lambda i, c: (0, c[0] * steps + i))],
             out_specs=pl.BlockSpec((columns // steps, rows), lambda i, c: (i, 0)),
         ),
-        out_shape=shape_of((columns, rows), BF16),
+        out_shape=in_hbm((columns, rows), BF16),
         compiler_params=params(),
         name="turned_part",
-    )(copy, q)
-
-
-def dispatch_kernel(core_ref, xt_ref, out_ref, *, half):
+    )(copy, from_hbm(q))
+
+
+def dispatch_kernel(core_ref, xt_ref, out_ref):
     core = core_ref[0]
     token = lax.broadcasted_iota(jnp.int32, (CP, 128), 1).astype(F32)
     group = 32
@@ -131,12 +140,12 @@
         out_ref[g * group : (g + 1) * group] = jnp.concatenate(rows, axis=1).astype(BF16)
 
 
-def dispatch(core, xt, half):
+def dispatch(core, xt):
     chips, total, tokens = xt.shape
     width = total - 4 * CP
 
     def body(*refs):
-        dispatch_kernel(*refs, half=half)
+        dispatch_kernel(*refs)
 
     return pl.pallas_call(
         body,
@@ -151,7 +160,6 @@
         cost_estimate=pl.CostEstimate(
             flops=2 * 128 * CP * chips * tokens * width, bytes_accessed=128 * chips * CP * width * 2, transcendentals=0
         ),
-        name=f"dispatch_{half}",
     )(core, xt)
 
 
@@ -197,18 +205,19 @@
             out_specs=pl.BlockSpec((step, CAP, 2, 16, lanes), lambda i, _: (i, 0, 0, 0, 0)),
             scratch_shapes=[pltpu.VMEM((width, lanes), BF16), pltpu.VMEM((rows, lanes), F32)],
         ),
-        out_shape=shape_of((chips, CAP, 2, 16, lanes), BF16),
+        out_shape=in_hbm((chips, CAP, 2, 16, lanes), BF16),
         compiler_params=params(),
         cost_estimate=pl.CostEstimate(
             flops=4 * chips * experts * rows * width * 256,
             bytes_accessed=4 * chips * experts * rows * width,
             transcendentals=0,
         ),
-        name=f"mix_{stream}",
     )(at, own, sib, *q_parts)
 
 
-def factor_kernel(parts_ref, hidden_ref, out_ref, tmp_ref, lhs_ref):
+def factor_kernel(copy_ref, parts_ref, hidden_ref, *refs):
+    out_refs, (tmp_ref, lhs_ref) = refs[:-2], refs[-2:]
+    copies = len(out_refs)
     step = pl.program_id(0)
     here = hidden_ref.shape[0]
 
@@ -225,10 +234,16 @@
     for n in range(here):
         start = pl.multiple_of((step * here + n) * 32, 32)
         lhs = lhs_ref[pl.ds(start, 32), 0 : hidden_ref.shape[1]]
-        out_ref[n] = lax.dot_general(lhs, hidden_ref[n], NN, preferred_element_type=F32).astype(BF16)
-
-
-def first_factor(parts, hidden, stream):
+        value = lax.dot_general(lhs, hidden_ref[n], NN, preferred_element_type=F32).astype(BF16)
+        ahead = (step * here + n - copy_ref[0] + copies) % copies
+        for k, out_ref in enumerate(out_refs):
+
+            @pl.when(ahead == k)
+            def _():
+                out_ref[...] = value
+
+
+def first_factor(copy, parts, hidden, stream, copies):
     experts, slots, units = hidden.shape
     experts = experts // STREAMS
     lanes = parts.shape[4]
@@ -236,66 +251,67 @@
     first = stream * experts // step
     return pl.pallas_call(
         factor_kernel,
-        grid=(experts // step,),
-        in_specs=[
-            pl.BlockSpec(parts.shape, lambda i: (0, 0, 0, 0, 0)),
-            pl.BlockSpec((step, slots, units), lambda i: (first + i, 0, 0)),
-        ],
-        out_specs=pl.BlockSpec((step, 32, units), lambda i: (i, 0, 0)),
-        out_shape=shape_of((experts, 32, units), BF16),
-        scratch_shapes=[pltpu.VMEM((256, lanes), F32), pltpu.VMEM((lanes, 256), BF16)],
+        grid_spec=pltpu.PrefetchScalarGridSpec(
+            num_scalar_prefetch=1,
+            grid=(experts // step,),
+            in_specs=[
+                pl.BlockSpec(parts.shape, lambda i, _: (0, 0, 0, 0, 0)),
+                pl.BlockSpec((step, slots, units), lambda i, _: (first + i, 0, 0)),
+            ],
+            out_specs=[pl.BlockSpec((32, units), lambda i, _: (0, 0))] * copies,
+            scratch_shapes=[pltpu.VMEM((256, lanes), F32), pltpu.VMEM((lanes, 256), BF16)],
+        ),
+        out_shape=[shape_of((32, units), BF16)] * copies,
         compiler_params=params(),
         cost_estimate=pl.CostEstimate(
             flops=2 * experts * slots * units * 256, bytes_accessed=2 * experts * slots * units, transcendentals=0
         ),
-        name=f"first_factor_{stream}",
-    )(parts, hidden)
-
-
-def ortho_kernel(parts_ref, out_ref):
-    count = parts_ref.shape[1]
-    factors, systems = [], []
+    )(copy, parts, hidden)
+
+
+def ortho_kernel(*refs):
+    parts_refs, out_ref = refs[:-1], refs[-1]
     row = lax.broadcasted_iota(jnp.int32, (32, 32), 0)
     col = lax.broadcasted_iota(jnp.int32, (32, 32), 1)
-    eye = jnp.where(row == col, 1.0, 0.0)
-    for m in range(count):
-        value = parts_ref[0, m].astype(F32)
-        for p in range(1, parts_ref.shape[0]):
-            value = value + parts_ref[p, m].astype(F32)
-        factors.append(value)
-        gram = lax.dot_general(value, value, NT, precision=HIGHEST, preferred_element_type=F32)
-        systems.append(jnp.concatenate([gram, eye], axis=1))
+    value = parts_refs[0][...].astype(F32)
+    for ref in parts_refs[1:]:
+        value = value + ref[...].astype(F32)
+    gram = lax.dot_general(value, value, NT, precision=HIGHEST, preferred_element_type=F32)
+    a = jnp.concatenate([gram, jnp.where(row == col, 1.0, 0.0)], axis=1)
     index = lax.broadcasted_iota(jnp.int32, (32, 64), 0)
     for k in range(32):
-        for m in range(count):
-            a = systems[m]
-            inv = lax.rsqrt(a[k : k + 1, k : k + 1])
-            pivot = a[k : k + 1, :] * inv
-            lower = a[:, k : k + 1] * inv
-            below = a - lower * pivot
-            systems[m] = jnp.where(index > k, below, jnp.where(index == k, pivot, a))
-    for m in range(count):
-        inverse = systems[m][:, 32:]
-        out_ref[m] = lax.dot_general(
-            inverse, factors[m], NN, precision=HIGHEST, preferred_element_type=F32
-        ).astype(BF16)
-
-
-def ortho_of(parts, stream):
-    _, count, rank, units = parts.shape
+        inv = lax.rsqrt(a[k : k + 1, k : k + 1])
+        pivot = a[k : k + 1, :] * inv
+        lower = a[:, k : k + 1] * inv
+        below = a - lower * pivot
+        a = jnp.where(index > k, below, jnp.where(index == k, pivot, a))
+    out_ref[...] = lax.dot_general(
+        a[:, 32:], value, NN, precision=HIGHEST, preferred_element_type=F32
+    ).astype(BF16)
+
+
+def ortho_of(parts):
+    rank, units = parts[0].shape
     return pl.pallas_call(
         ortho_kernel,
-        out_shape=shape_of((count, rank, units), BF16),
+        out_shape=shape_of((rank, units), BF16),
         compiler_params=params(),
         cost_estimate=pl.CostEstimate(flops=5_000_000_000, bytes_accessed=4 * rank * units * 2, transcendentals=0),
-        name=f"ortho_{stream}",
-    )(parts)
-
-
-def project_kernel(ortho_ref, hidden_ref, *refs):
-    basis_ref, out_ref, rows_ref = refs[-3:]
+    )(*parts)
+
+
+def project_kernel(copy_ref, *refs, copies):
+    part_refs, hidden_ref = refs[:copies], refs[copies]
+    basis_ref, out_ref, ortho_ref, rows_ref = refs[-4:]
     step = pl.program_id(0)
     here, slots, units = hidden_ref.shape
+
+    @pl.when(step == 0)
+    def _():
+        for k, ref in enumerate(part_refs):
+            place = pl.multiple_of(32 * ((copy_ref[0] - k + copies) % copies), 32)
+            ortho_ref[pl.ds(place, 32), :] = ref[...]
+
     start = pl.multiple_of(step * here * 32, 32)
     basis = ortho_ref[pl.ds(start, here * 32), :].astype(F32) * math.sqrt(units)
     basis_ref[...] = basis.reshape(here, 32, units)
@@ -312,45 +328,52 @@
     def _():
         for c in range(CAP):
             for k in range(2):
-                out_ref[c, k] = rows_ref[pl.ds(k * CAP + c, 16, stride=2 * CAP), :].astype(BF16)
-
-
-def project(ortho, hidden, stream, basis):
+                value = rows_ref[pl.ds(k * CAP + c, 16, stride=2 * CAP), :].astype(BF16)
+                for j in range(out_ref.shape[0]):
+                    out_ref[j, c, k] = value
+
+
+def project(copy, parts, hidden, stream, basis, chips):
     every, slots, units = hidden.shape
     experts = every // STREAMS
+    copies = len(parts)
     lanes = experts * 32
     step = 2
     first = stream * experts // step
     given = [] if basis is None else [basis]
-    return pl.pallas_call(
-        project_kernel,
-        grid=(experts // step,),
-        in_specs=[
-            pl.BlockSpec((lanes, units), lambda i: (0, 0)),
-            pl.BlockSpec((step, slots, units), lambda i: (first + i, 0, 0)),
-        ]
-        + [pl.BlockSpec(memory_space=pl.ANY)] * len(given),
-        out_specs=[
-            pl.BlockSpec((step, 32, units), lambda i: (first + i, 0, 0)),
-            pl.BlockSpec((CAP, 2, 16, lanes), lambda i: (0, 0, 0, 0)),
-        ],
+
+    def body(*refs):
+        project_kernel(*refs, copies=copies)
+
+    return pl.pallas_call(
+        body,
+        grid_spec=pltpu.PrefetchScalarGridSpec(
+            num_scalar_prefetch=1,
+            grid=(experts // step,),
+            in_specs=[pl.BlockSpec((32, units), lambda i, _: (0, 0))] * copies
+            + [pl.BlockSpec((step, slots, units), lambda i, _: (first + i, 0, 0))]
+            + [pl.BlockSpec(memory_space=pl.ANY)] * len(given),
+            out_specs=[
+                pl.BlockSpec((step, 32, units), lambda i, _: (first + i, 0, 0)),
+                pl.BlockSpec((chips, CAP, 2, 16, lanes), lambda i, _: (0, 0, 0, 0, 0)),
+            ],
+            scratch_shapes=[pltpu.VMEM((lanes, units), BF16), pltpu.VMEM((slots, lanes), F32)],
+        ),
         out_shape=[
             shape_of((every, 32, units), F32),
-            shape_of((CAP, 2, 16, lanes), BF16),
+            in_hbm((chips, CAP, 2, 16, lanes), BF16),
         ],
-        input_output_aliases={2: 0} if given else {},
-        scratch_shapes=[pltpu.VMEM((slots, lanes), F32)],
+        input_output_aliases={copies + 2: 0} if given else {},
         compiler_params=params(),
         cost_estimate=pl.CostEstimate(
             flops=2 * experts * slots * units * 256, bytes_accessed=2 * experts * slots * units, transcendentals=0
         ),
-        name=f"project_{stream}",
-    )(ortho, hidden, *given)
+    )(copy, *parts, hidden, *given)
 
 
 def terms_kernel(core_ref, own_ref, sib_ref, proj_ref, out_ref, rows_ref, sum_ref):
     core = core_ref[0]
-    count, experts, rows, width = own_ref.shape
+    count, experts, _, width = own_ref.shape
     part = width // 4
 
     @pl.when(pl.program_id(0) == 0)
@@ -394,14 +417,13 @@
             out_specs=pl.BlockSpec((4, step, width // 4, lanes), lambda i, _: (0, i, 0, 0)),
             scratch_shapes=[pltpu.VMEM((256, lanes), F32), pltpu.VMEM((lanes, 512), F32)],
         ),
-        out_shape=shape_of((4, chips, width // 4, lanes), BF16),
+        out_shape=in_hbm((4, chips, width // 4, lanes), BF16),
         compiler_params=params(),
         cost_estimate=pl.CostEstimate(
             flops=4 * chips * experts * rows * width * 256,
             bytes_accessed=4 * chips * experts * rows * width,
             transcendentals=0,
         ),
-        name=f"second_terms_{stream}",
     )(core, own, sib, proj)
 
 
@@ -426,7 +448,6 @@
         out_shape=shape_of((rows * STREAMS, columns), F32),
         input_output_aliases={1: 0} if given else {},
         compiler_params=params(),
-        name=f"owned_columns_{stream}",
     )(parts, *given)
 
 
@@ -434,22 +455,20 @@
     return lax.all_to_all(values, axes, split_axis=0, concat_axis=0, tiled=True)
 
 
-def to_all(values, axis):
-    return exchange(jnp.broadcast_to(values[None], (lax.axis_size(axis), *values.shape)), axis)
+def shift(value, step, copies):
+    return lax.ppermute(value, "dp", [(i, (i + step) % copies) for i in range(copies)])
 
 
 def around(part, copies):
-    ahead = [(i, (i + 1) % copies) for i in range(copies)]
-    back = [(i, (i - 1) % copies) for i in range(copies)]
     half = part.shape[0] // 2
-    before = lax.ppermute(part, "dp", ahead)
-    after = lax.ppermute(part, "dp", back)
-    far_low = lax.ppermute(before[:half], "dp", ahead)
-    far_high = lax.ppermute(after[half:], "dp", back)
+    before = shift(part, 1, copies)
+    after = shift(part, copies - 1, copies)
+    far_low = shift(before[:half], 1, copies)
+    far_high = shift(after[half:], copies - 1, copies)
     return [part, after, jnp.concatenate([far_low, far_high], axis=0), before]
 
 
-def local(out_grads, expert_ids, gate_probs, hidden_acts, q_previous):
+def whole(out_grads, expert_ids, gate_probs, hidden_acts, q_previous):
     chips = lax.axis_size("chip")
     copies = lax.axis_size("dp")
     core = lax.axis_index("core").astype(jnp.int32).reshape(1)
@@ -457,28 +476,29 @@
     at = jnp.concatenate([core, copy])
     hidden = hidden_acts[0]
     experts, rank, width = q_previous.shape
-    units = hidden.shape[2]
     here = experts // STREAMS
 
     q_part = turned_part(copy, q_previous.reshape(experts * rank, width), copies)
     q_part = exchange(q_part.reshape(chips, -1, experts * rank), "chip")
+    own_t = prepare(expert_ids[0], gate_probs[0], out_grads[0], chips)
+    q_part, own_t = lax.optimization_barrier((q_part, own_t))
     q_parts = around(q_part, copies)
-
-    own_t = exchange(prepare(expert_ids[0], gate_probs[0], out_grads[0], chips), "chip")
+    own_t = exchange(own_t, "chip")
     sib_t = lax.ppermute(own_t, "core", [(0, 1), (1, 0)])
-    own = dispatch(core, own_t, 0)
-    sib = dispatch(core, sib_t, 1)
+    own = dispatch(core, own_t)
+    sib = dispatch(core, sib_t)
     own = own.reshape(chips, experts, *own.shape[1:])
     sib = sib.reshape(chips, experts, *sib.shape[1:])
 
     basis, sums = None, None
     for s in range(STREAMS):
         mixed = exchange(mix(at, own, sib, q_parts, s), "chip")
-        factor = exchange(first_factor(mixed, hidden, s), "dp")
-        ortho = ortho_of(factor.reshape(copies, here // copies, rank, units), s)
-        ortho = to_all(ortho, "dp").reshape(here * rank, units)
-        basis, proj = project(ortho, hidden, s, basis)
-        terms = second_terms(core, own, sib, to_all(proj, "chip"), s)
+        factor = first_factor(copy, mixed, hidden, s, copies)
+        factor = [factor[0]] + [shift(factor[k], k, copies) for k in range(1, copies)]
+        ortho = ortho_of(factor)
+        ortho = [ortho] + [shift(ortho, k, copies) for k in range(1, copies)]
+        basis, proj = project(copy, ortho, hidden, s, basis, chips)
+        terms = second_terms(core, own, sib, exchange(proj, "chip"), s)
         terms = exchange(terms.reshape(copies * chips, -1, here * rank), ("dp", "chip"))
         sums = owned_columns(terms.reshape(copies, width // copies, here * rank), s, sums)
     return (basis, sums.reshape(experts, rank, width // copies))
@@ -491,7 +511,7 @@
     names = (*mesh.axis_names[:at], "chip", "core", *mesh.axis_names[at + 1 :])
     expert = ("chip", "core")
     return jax.shard_map(
-        local,
+        whole,
         mesh=Mesh(devices, names),
         in_specs=(
             P("dp", expert, None),

time: 298 us -> 285 us (0.956)
  waiting for transfers between devices: 107 us -> 75.8 us
  blocking collectives: 0 us -> 30 us
  local copies, waits for them, and re-layouts: 18.2 us -> 4.43 us
  Pallas kernels: 90 us -> 96.1 us
  starting transfers between devices: 77.9 us -> 74.5 us
    all_to_all x12 -> x7, waiting for transfers between devices: 87.2 us -> 33.4 us  [exchange(): return lax.all_to_all(values, axes, split_axis=0, concat_axis=0, tiled=True)]
    all_to_all x0 -> x1, blocking collectives: none -> 30 us  [exchange(): return lax.all_to_all(values, axes, split_axis=0, concat_axis=0, tiled=True)]
    ppermute x5 -> x17, waiting for transfers between devices: 19.7 us -> 42.3 us  [the longest x16 42.3 us: shift(): lax.ppermute(value, 'dp', [(i, (i + step) % copies) for i in range(copies)])]
    all_to_all x12 -> x7, starting transfers between devices: 70.9 us -> 51.2 us  [exchange(): return lax.all_to_all(values, axes, split_axis=0, concat_axis=0, tiled=True)]
    ppermute x5 -> x17, starting transfers between devices: 7.03 us -> 23.3 us  [the longest x16 23.3 us: shift(): lax.ppermute(value, 'dp', [(i, (i + step) % copies) for i in range(copies)])]
    unnamed x35 -> x17, local copies, waits for them, and re-layouts: 11.7 us -> 1.7 us
    broadcast_in_dim x4 -> x0, local copies, waits for them, and re-layouts: 3.78 us -> none  [to_all(): jnp.broadcast_to(values[None], (lax.axis_size(axis), *values.shape))]
  transfers between devices with their start and end apart: 17 -> 24, of which waited for: 11 -> 12; matrix products, arithmetic and copies ran while one was open for 1% -> 1% of each run, Pallas kernels for 21% -> 24%
where the time goes in v3:
time: 285 us; the launch traced here: 282 us
  Pallas kernels  96.1 us (34%)
  waiting for transfers between devices  75.8 us (27%)
  starting transfers between devices  74.5 us (26%)
  blocking collectives  30 us (11%)
  local copies, waits for them, and re-layouts  4.43 us (2%)
    all_to_all x7, starting transfers between devices, exchange(): return lax.all_to_all(values, axes, split_axis=0, concat_axis=0, tiled=True)  51.2 us
    ppermute x16, waiting for transfers between devices, shift(): lax.ppermute(value, 'dp', [(i, (i + step) % copies) for i in range(copies)])  42.3 us
    all_to_all x7, waiting for transfers between devices, exchange(): return lax.all_to_all(values, axes, split_axis=0, concat_axis=0, tiled=True)  33.4 us
    all_to_all x1, blocking collectives, exchange(): return lax.all_to_all(values, axes, split_axis=0, concat_axis=0, tiled=True)  30 us
    pallas_call x2, Pallas kernels, mix(): pl.pallas_call(mix_kernel, grid_spec=pltpu.PrefetchScalarGridSpec(num_sca...  23.6 us
    ppermute x16, starting transfers between devices, shift(): lax.ppermute(value, 'dp', [(i, (i + step) % copies) for i in range(copies)])  23.3 us
    pallas_call x2, Pallas kernels, second_terms(): pl.pallas_call(terms_kernel, grid_spec=pltpu.PrefetchScalarGridSpec(num_s...  21.8 us
    pallas_call x2, Pallas kernels, dispatch(): pl.pallas_call(body, grid_spec=pltpu.PrefetchScalarGridSpec(num_scalar_pr...  20.1 us
  transfers between devices with their start and end apart: 24, of which 12 were waited for; matrix products, arithmetic and copies ran while one was open for 1% of the time, Pallas kernels for 24%

profile of v3, /device:TPU:6, one launch (start us, length us, event | category | flops | bytes accessed | tf_op | source)
XLA Modules:
  0.0 281.5 jit_solution(5609067603116820036)
XLA Ops:
  2.8 7.4 %all-to-all-start = ((bf16[16,112,256]{2,1,0:T(8,128)(2,1)}), bf16[16,112,256]{2,1,0:T(8,128)(2,1)S(1)}, u32[]{:S(2)}, u32[]{:S(2)}) async-start(bf16[16,112,256]{2,1,0:T(8,128)(2,1)} %bitcast.35), calls=%async_computation | async-start | bytes 1835008 | tf_op jit(solution)/shard_map/all_to_all | solution.py:455
  10.2 4.0 %prepare.1 = bf16[16,480,128]{2,1,0:T(8,128)(2,1)} custom-call(s32[8,128]{1,0:T(8,128)} %bitcast.38, f32[8,128]{1,0:T(8,128)} %bitcast.39, bf16[128,7168]{1,0:T(8,128)(2,1)} %bitcast.37), custom_call_target="tpu_custom_call" | custom-call | tf_op jit(solution)/shard_map/prepare/pallas_call | solution.py:89
  14.2 9.1 %all-to-all-done.rest_0_ = bf16[16,112,256]{2,1,0:T(8,128)(2,1)S(1)} async-done(((bf16[16,112,256]{2,1,0:T(8,128)(2,1)}), bf16[16,112,256]{2,1,0:T(8,128)(2,1)S(1)}, u32[]{:S(2)}, u32[]{:S(2)}) %all-to-all-start) | async-done | bytes 917536 | tf_op jit(solution)/shard_map/all_to_all | solution.py:455
  23.3 30.0 %all_to_all.40.refs_1_ = bf16[16,480,128]{2,1,0:T(8,128)(2,1)S(1)} all-to-all(bf16[16,480,128]{2,1,0:T(8,128)(2,1)} %prepare.1), channel_id=1, replica_groups=mesh['chip'=16,'core'=2,'dp'=4] {'chip'}, dimensions={0} | all-to-all | bytes 3932160 | tf_op jit(solution)/shard_map/all_to_all | solution.py:455
  57.3 21.0 %collective-permute-done.2.rest_3_ = bf16[16,112,256]{2,1,0:T(8,128)(2,1)S(1)} collective-permute-done((bf16[16,112,256]{2,1,0:T(8,128)(2,1)S(1)}, bf16[16,112,256]{2,1,0:T(8,128)(2,1)S(1)}, u32[]{:S(2)}, u32[]{:S(2)}) %collective-permute-start.2) | collective-permute-done | bytes 917536 | tf_op jit(solution)/shard_map/ppermute | solution.py:459
  83.6 9.4 %collective-permute-done.3 = bf16[8,112,256]{2,1,0:T(8,128)(2,1)S(1)} collective-permute-done((bf16[8,112,256]{2,1,0:T(8,128)(2,1)}, bf16[8,112,256]{2,1,0:T(8,128)(2,1)S(1)}, u32[]{:S(2)}, u32[]{:S(2)}) %collective-permute-start.3) | collective-permute-done | bytes 458784 | tf_op jit(solution)/shard_map/ppermute | solution.py:459
  94.5 9.3 %shard_map.68 = bf16[128,128,448]{2,1,0:T(8,128)(2,1)} custom-call(s32[1]{0:T(128)} %bitcast.1.refs_0_.core_ref, bf16[16,480,128]{2,1,0:T(8,128)(2,1)S(1)} %all_to_all.40.refs_1_), custom_call_target="tpu_custom_call" | custom-call | flops 1879048192 | bytes 14680064 | tf_op jit(solution)/shard_map/pallas_call | solution.py:150
  103.8 10.8 %shard_map.69 = bf16[128,128,448]{2,1,0:T(8,128)(2,1)} custom-call(s32[1]{0:T(128)} %bitcast.1.refs_0_.core_ref, bf16[16,480,128]{2,1,0:T(8,128)(2,1)} %collective-permute-done.refs_1_), custom_call_target="tpu_custom_call" | custom-call | flops 1879048192 | bytes 14680064 | tf_op jit(solution)/shard_map/pallas_call | solution.py:150
  114.6 11.8 %shard_map.73 = bf16[16,6,2,16,128]{4,3,2,1,0:T(8,128)(2,1)} custom-call(s32[2]{0:T(128)S(1)} %pad_add_fusion.at_ref, bf16[16,8,128,448]{3,2,1,0:T(8,128)(2,1)} %bitcast.20, bf16[16,8,128,448]{3,2,1,0:T(8,128)(2,1)} %bitcast.24, bf16[16,112,256]{2,1,0:T(8,128)(2,1)S(1)} %all-to-all-done.rest_0_, bf16[16,112,256]{2,1,0:T(8,128)(2,1)S(1)} %copy-done.4, ...), custom_call_target="tpu_custom_call" | custom-call | flops 3758096384 | bytes 14680064 | tf_op jit(solution)/shard_map/pallas_call | solution.py:199
  126.4 6.6 %all-to-all-start.3 = ((bf16[16,6,2,16,128]{4,3,2,1,0:T(8,128)(2,1)}), bf16[16,6,2,16,128]{4,3,2,1,0:T(8,128)(2,1)S(1)}, u32[]{:S(2)}, u32[]{:S(2)}) async-start(bf16[16,6,2,16,128]{4,3,2,1,0:T(8,128)(2,1)} %shard_map.73), calls=%async_computation.3 | async-start | bytes 1572864 | tf_op jit(solution)/shard_map/all_to_all | solution.py:455
  134.2 11.8 %shard_map.70 = bf16[16,6,2,16,128]{4,3,2,1,0:T(8,128)(2,1)} custom-call(s32[2]{0:T(128)S(1)} %pad_add_fusion.at_ref, bf16[16,8,128,448]{3,2,1,0:T(8,128)(2,1)} %bitcast.21, bf16[16,8,128,448]{3,2,1,0:T(8,128)(2,1)} %bitcast.25, bf16[16,112,256]{2,1,0:T(8,128)(2,1)S(1)} %all-to-all-done.rest_0_, bf16[16,112,256]{2,1,0:T(8,128)(2,1)S(1)} %copy-done.5, ...), custom_call_target="tpu_custom_call" | custom-call | flops 3758096384 | bytes 14680064 | tf_op jit(solution)/shard_map/pallas_call | solution.py:199
  146.0 7.3 %all-to-all-start.2 = ((bf16[16,6,2,16,128]{4,3,2,1,0:T(8,128)(2,1)}), bf16[16,6,2,16,128]{4,3,2,1,0:T(8,128)(2,1)S(1)}, u32[]{:S(2)}, u32[]{:S(2)}) async-start(bf16[16,6,2,16,128]{4,3,2,1,0:T(8,128)(2,1)} %shard_map.70), calls=%async_computation.2 | async-start | bytes 1572864 | tf_op jit(solution)/shard_map/all_to_all | solution.py:455
  156.7 4.6 %collective-permute-start.12 = (bf16[32,2048]{1,0:T(8,128)(2,1)S(1)}, bf16[32,2048]{1,0:T(8,128)(2,1)S(1)}, u32[]{:S(2)}, u32[]{:S(2)}) collective-permute-start(bf16[32,2048]{1,0:T(8,128)(2,1)S(1)} %get-tuple-element.24), channel_id=1, source_target_pairs={{0,2},{1,3},{2,0},{3,1},{4,6},{5,7},{6,4},{7,5},{8,10},{9,11},{10,... | collective-permute-start | bytes 393224 | tf_op jit(solution)/shard_map/ppermute | solution.py:459
  181.7 3.8 %shard_map.76 = (f32[8,32,2048]{2,1,0:T(8,128)}, bf16[16,6,2,16,128]{4,3,2,1,0:T(8,128)(2,1)}) custom-call(s32[1]{0:T(128)} %bitcast.copy_ref.refs_0_, bf16[32,2048]{1,0:T(8,128)(2,1)S(1)} %shard_map.75.refs_1_, bf16[32,2048]{1,0:T(8,128)(2,1)S(1)} %collective-permute-done.14.refs_2_, bf16[32,2048]{1,0:T(8,128)(2,1)S(1)} %collective-permute-done.15.refs_3_, ...), custom_call_target="tpu_custom_call" | custom-call | flops 805306368 | bytes 3145728 | tf_op jit(solution)/shard_map/pallas_call | solution.py:348
  185.5 7.2 %all-to-all-start.6 = ((bf16[16,6,2,16,128]{4,3,2,1,0:T(8,128)(2,1)}), bf16[16,6,2,16,128]{4,3,2,1,0:T(8,128)(2,1)S(1)}, u32[]{:S(2)}, u32[]{:S(2)}) async-start(bf16[16,6,2,16,128]{4,3,2,1,0:T(8,128)(2,1)} %get-tuple-element.29), calls=%async_computation.6 | async-start | bytes 1572864 | tf_op jit(solution)/shard_map/all_to_all | solution.py:455
  192.7 3.7 %shard_map.72.refs_1_ = bf16[32,2048]{1,0:T(8,128)(2,1)S(1)} custom-call(bf16[32,2048]{1,0:T(8,128)(2,1)S(1)} %get-tuple-element.18.refs_0_, bf16[32,2048]{1,0:T(8,128)(2,1)S(1)} %collective-permute-done.5.refs_1_, bf16[32,2048]{1,0:T(8,128)(2,1)S(1)} %collective-permute-done.6.refs_2_, bf16[32,2048]{1,0:T(8,128)(2,1)S(1)} %collective-permute-done.7.refs_3_), custom_call_target="tpu_custom_call" | custom-call | flops 5000000000 | bytes 524288 | tf_op jit(solution)/shard_map/pallas_call | solution.py:295
  205.1 3.9 %shard_map.77 = (f32[8,32,2048]{2,1,0:T(8,128)}, bf16[16,6,2,16,128]{4,3,2,1,0:T(8,128)(2,1)}) custom-call(s32[1]{0:T(128)} %bitcast.copy_ref.refs_0_, bf16[32,2048]{1,0:T(8,128)(2,1)S(1)} %shard_map.72.refs_1_, bf16[32,2048]{1,0:T(8,128)(2,1)S(1)} %collective-permute-done.8.refs_2_, ...), custom_call_target="tpu_custom_call", output_to_operand_aliasing={{0}: (6, {})} | custom-call | flops 805306368 | bytes 3145728 | tf_op jit(solution)/shard_map/pallas_call | solution.py:348
  208.9 7.2 %all-to-all-start.4 = ((bf16[16,6,2,16,128]{4,3,2,1,0:T(8,128)(2,1)}), bf16[16,6,2,16,128]{4,3,2,1,0:T(8,128)(2,1)S(1)}, u32[]{:S(2)}, u32[]{:S(2)}) async-start(bf16[16,6,2,16,128]{4,3,2,1,0:T(8,128)(2,1)} %get-tuple-element.28), calls=%async_computation.4 | async-start | bytes 1572864 | tf_op jit(solution)/shard_map/all_to_all | solution.py:455
  216.2 10.9 %shard_map.79 = bf16[4,16,112,128]{3,2,1,0:T(8,128)(2,1)} custom-call(s32[1]{0:T(128)} %bitcast.1.refs_0_.core_ref, bf16[16,8,128,448]{3,2,1,0:T(8,128)(2,1)} %bitcast.22, bf16[16,8,128,448]{3,2,1,0:T(8,128)(2,1)} %bitcast.26, bf16[16,6,2,16,128]{4,3,2,1,0:T(8,128)(2,1)S(1)} %all-to-all-done.6.proj_ref), custom_call_target="tpu_custom_call" | custom-call | flops 3758096384 | bytes 14680064 | tf_op jit(solution)/shard_map/pallas_call | solution.py:411
  227.1 8.5 %all-to-all-start.7 = ((bf16[64,112,128]{2,1,0:T(8,128)(2,1)}), bf16[64,112,128]{2,1,0:T(8,128)(2,1)S(1)}, u32[]{:S(2)}, u32[]{:S(2)}) async-start(bf16[64,112,128]{2,1,0:T(8,128)(2,1)} %bitcast.32), calls=%async_computation.7 | async-start | bytes 3670016 | tf_op jit(solution)/shard_map/all_to_all | solution.py:455
  235.6 10.9 %shard_map.78 = bf16[4,16,112,128]{3,2,1,0:T(8,128)(2,1)} custom-call(s32[1]{0:T(128)} %bitcast.1.refs_0_.core_ref, bf16[16,8,128,448]{3,2,1,0:T(8,128)(2,1)} %bitcast.23, bf16[16,8,128,448]{3,2,1,0:T(8,128)(2,1)} %bitcast.27, bf16[16,6,2,16,128]{4,3,2,1,0:T(8,128)(2,1)S(1)} %all-to-all-done.4.proj_ref), custom_call_target="tpu_custom_call" | custom-call | flops 3758096384 | bytes 14680064 | tf_op jit(solution)/shard_map/pallas_call | solution.py:411
  246.5 7.7 %all-to-all-done.7 = bf16[64,112,128]{2,1,0:T(8,128)(2,1)S(1)} async-done(((bf16[64,112,128]{2,1,0:T(8,128)(2,1)}), bf16[64,112,128]{2,1,0:T(8,128)(2,1)S(1)}, u32[]{:S(2)}, u32[]{:S(2)}) %all-to-all-start.7) | async-done | bytes 1835040 | tf_op jit(solution)/shard_map/all_to_all | solution.py:455
  254.2 7.0 %all-to-all-start.5 = ((bf16[64,112,128]{2,1,0:T(8,128)(2,1)}), bf16[64,112,128]{2,1,0:T(8,128)(2,1)}, u32[]{:S(2)}, u32[]{:S(2)}) async-start(bf16[64,112,128]{2,1,0:T(8,128)(2,1)} %bitcast.33), calls=%async_computation.5 | async-start | bytes 3670016 | tf_op jit(solution)/shard_map/all_to_all | solution.py:455
  262.5 16.6 %all-to-all-done.5 = bf16[64,112,128]{2,1,0:T(8,128)(2,1)} async-done(((bf16[64,112,128]{2,1,0:T(8,128)(2,1)}), bf16[64,112,128]{2,1,0:T(8,128)(2,1)}, u32[]{:S(2)}, u32[]{:S(2)}) %all-to-all-start.5) | async-done | bytes 1835040 | tf_op jit(solution)/shard_map/all_to_all | solution.py:455
  (62 shorter events, 50.2 us)
Async XLA Ops:
  2.8 20.5 %all-to-all-start = ((bf16[16,112,256]{2,1,0:T(8,128)(2,1)}), bf16[16,112,256]{2,1,0:T(8,128)(2,1)S(1)}, u32[]{:S(2)}, u32[]{:S(2)}) async-start(bf16[16,112,256]{2,1,0:T(8,128)(2,1)} %bitcast.35), calls=%async_computation | async-start | bytes 1835008 | tf_op jit(solution)/shard_map/all_to_all | solution.py:455
  53.3 50.5 %collective-permute-start = (bf16[16,480,128]{2,1,0:T(8,128)(2,1)S(1)}, bf16[16,480,128]{2,1,0:T(8,128)(2,1)}, u32[]{:S(2)}, u32[]{:S(2)}) collective-permute-start(bf16[16,480,128]{2,1,0:T(8,128)(2,1)S(1)} %all_to_all.40.refs_1_), channel_id=1, source_target_pairs={{0,4},{4,0},{1,5},{5,1},{2,6},{6,2},{3,7},{7,3},{8,12},{12,8},{9,1... | collective-permute-start | bytes 5898248 | tf_op jit(solution)/shard_map/ppermute | solution.py:487
  53.3 25.1 %collective-permute-start.2 = (bf16[16,112,256]{2,1,0:T(8,128)(2,1)S(1)}, bf16[16,112,256]{2,1,0:T(8,128)(2,1)S(1)}, u32[]{:S(2)}, u32[]{:S(2)}) collective-permute-start(bf16[16,112,256]{2,1,0:T(8,128)(2,1)S(1)} %all-to-all-done.rest_0_), channel_id=1, source_target_pairs={{0,1},{1,2},{2,3},{3,0},{4,5},{5,6},{6,7},{7,4},{8,9},{9,10},{10,1... | collective-permute-start | bytes 2752520 | tf_op jit(solution)/shard_map/ppermute | solution.py:459
  55.2 24.0 %collective-permute-start.1 = (bf16[16,112,256]{2,1,0:T(8,128)(2,1)S(1)}, bf16[16,112,256]{2,1,0:T(8,128)(2,1)S(1)}, u32[]{:S(2)}, u32[]{:S(2)}) collective-permute-start(bf16[16,112,256]{2,1,0:T(8,128)(2,1)S(1)} %all-to-all-done.rest_0_), channel_id=1, source_target_pairs={{0,3},{1,0},{2,1},{3,2},{4,7},{5,4},{6,5},{7,6},{8,11},{9,8},{10,9... | collective-permute-start | bytes 2752520 | tf_op jit(solution)/shard_map/ppermute | solution.py:459
  79.2 13.8 %collective-permute-start.3 = (bf16[8,112,256]{2,1,0:T(8,128)(2,1)}, bf16[8,112,256]{2,1,0:T(8,128)(2,1)S(1)}, u32[]{:S(2)}, u32[]{:S(2)}) collective-permute-start(bf16[8,112,256]{2,1,0:T(8,128)(2,1)} %slice.8), channel_id=1, source_target_pairs={{0,1},{1,2},{2,3},{3,0},{4,5},{5,6},{6,7},{7,4},{8,9},{9,10},{10,1... | collective-permute-start | bytes 1376264 | tf_op jit(solution)/shard_map/ppermute | solution.py:459
  80.5 12.9 %collective-permute-start.4 = (bf16[8,112,256]{2,1,0:T(8,128)(2,1)}, bf16[8,112,256]{2,1,0:T(8,128)(2,1)}, u32[]{:S(2)}, u32[]{:S(2)}) collective-permute-start(bf16[8,112,256]{2,1,0:T(8,128)(2,1)} %slice.9), channel_id=1, source_target_pairs={{0,3},{1,0},{2,1},{3,2},{4,7},{5,4},{6,5},{7,6},{8,11},{9,8},{10,9... | collective-permute-start | bytes 1376264 | tf_op jit(solution)/shard_map/ppermute | solution.py:459
  126.4 19.6 %all-to-all-start.3 = ((bf16[16,6,2,16,128]{4,3,2,1,0:T(8,128)(2,1)}), bf16[16,6,2,16,128]{4,3,2,1,0:T(8,128)(2,1)S(1)}, u32[]{:S(2)}, u32[]{:S(2)}) async-start(bf16[16,6,2,16,128]{4,3,2,1,0:T(8,128)(2,1)} %shard_map.73), calls=%async_computation.3 | async-start | bytes 1572864 | tf_op jit(solution)/shard_map/all_to_all | solution.py:455
  146.0 26.9 %all-to-all-start.2 = ((bf16[16,6,2,16,128]{4,3,2,1,0:T(8,128)(2,1)}), bf16[16,6,2,16,128]{4,3,2,1,0:T(8,128)(2,1)S(1)}, u32[]{:S(2)}, u32[]{:S(2)}) async-start(bf16[16,6,2,16,128]{4,3,2,1,0:T(8,128)(2,1)} %shard_map.70), calls=%async_computation.2 | async-start | bytes 1572864 | tf_op jit(solution)/shard_map/all_to_all | solution.py:455
  156.1 8.0 %collective-permute-start.11 = (bf16[32,2048]{1,0:T(8,128)(2,1)S(1)}, bf16[32,2048]{1,0:T(8,128)(2,1)S(1)}, u32[]{:S(2)}, u32[]{:S(2)}) collective-permute-start(bf16[32,2048]{1,0:T(8,128)(2,1)S(1)} %get-tuple-element.23), channel_id=1, source_target_pairs={{0,1},{1,2},{2,3},{3,0},{4,5},{5,6},{6,7},{7,4},{8,9},{9,10},{10,1... | collective-permute-start | bytes 393224 | tf_op jit(solution)/shard_map/ppermute | solution.py:459
  156.7 9.0 %collective-permute-start.12 = (bf16[32,2048]{1,0:T(8,128)(2,1)S(1)}, bf16[32,2048]{1,0:T(8,128)(2,1)S(1)}, u32[]{:S(2)}, u32[]{:S(2)}) collective-permute-start(bf16[32,2048]{1,0:T(8,128)(2,1)S(1)} %get-tuple-element.24), channel_id=1, source_target_pairs={{0,2},{1,3},{2,0},{3,1},{4,6},{5,7},{6,4},{7,5},{8,10},{9,11},{10,... | collective-permute-start | bytes 393224 | tf_op jit(solution)/shard_map/ppermute | solution.py:459
  161.3 5.0 %collective-permute-start.13 = (bf16[32,2048]{1,0:T(8,128)(2,1)S(1)}, bf16[32,2048]{1,0:T(8,128)(2,1)S(1)}, u32[]{:S(2)}, u32[]{:S(2)}) collective-permute-start(bf16[32,2048]{1,0:T(8,128)(2,1)S(1)} %get-tuple-element.25), channel_id=1, source_target_pairs={{0,3},{1,0},{2,1},{3,2},{4,7},{5,4},{6,5},{7,6},{8,11},{9,8},{10,9... | collective-permute-start | bytes 393224 | tf_op jit(solution)/shard_map/ppermute | solution.py:459
  170.0 9.6 %collective-permute-start.16 = (bf16[32,2048]{1,0:T(8,128)(2,1)S(1)}, bf16[32,2048]{1,0:T(8,128)(2,1)S(1)}, u32[]{:S(2)}, u32[]{:S(2)}) collective-permute-start(bf16[32,2048]{1,0:T(8,128)(2,1)S(1)} %shard_map.75.refs_1_), channel_id=1, source_target_pairs={{0,3},{1,0},{2,1},{3,2},{4,7},{5,4},{6,5},{7,6},{8,11},{9,8},{10,9... | collective-permute-start | bytes 393224 | tf_op jit(solution)/shard_map/ppermute | solution.py:459
  171.9 9.7 %collective-permute-start.15 = (bf16[32,2048]{1,0:T(8,128)(2,1)S(1)}, bf16[32,2048]{1,0:T(8,128)(2,1)S(1)}, u32[]{:S(2)}, u32[]{:S(2)}) collective-permute-start(bf16[32,2048]{1,0:T(8,128)(2,1)S(1)} %shard_map.75.refs_1_), channel_id=1, source_target_pairs={{0,2},{1,3},{2,0},{3,1},{4,6},{5,7},{6,4},{7,5},{8,10},{9,11},{10,... | collective-permute-start | bytes 393224 | tf_op jit(solution)/shard_map/ppermute | solution.py:459
  172.0 9.7 %collective-permute-start.14 = (bf16[32,2048]{1,0:T(8,128)(2,1)S(1)}, bf16[32,2048]{1,0:T(8,128)(2,1)S(1)}, u32[]{:S(2)}, u32[]{:S(2)}) collective-permute-start(bf16[32,2048]{1,0:T(8,128)(2,1)S(1)} %shard_map.75.refs_1_), channel_id=1, source_target_pairs={{0,1},{1,2},{2,3},{3,0},{4,5},{5,6},{6,7},{7,4},{8,9},{9,10},{10,1... | collective-permute-start | bytes 393224 | tf_op jit(solution)/shard_map/ppermute | solution.py:459
  175.7 17.0 %collective-permute-start.5 = (bf16[32,2048]{1,0:T(8,128)(2,1)S(1)}, bf16[32,2048]{1,0:T(8,128)(2,1)S(1)}, u32[]{:S(2)}, u32[]{:S(2)}) collective-permute-start(bf16[32,2048]{1,0:T(8,128)(2,1)S(1)} %get-tuple-element.19), channel_id=1, source_target_pairs={{0,1},{1,2},{2,3},{3,0},{4,5},{5,6},{6,7},{7,4},{8,9},{9,10},{10,1... | collective-permute-start | bytes 393224 | tf_op jit(solution)/shard_map/ppermute | solution.py:459
  178.2 14.5 %collective-permute-start.6 = (bf16[32,2048]{1,0:T(8,128)(2,1)S(1)}, bf16[32,2048]{1,0:T(8,128)(2,1)S(1)}, u32[]{:S(2)}, u32[]{:S(2)}) collective-permute-start(bf16[32,2048]{1,0:T(8,128)(2,1)S(1)} %get-tuple-element.20), channel_id=1, source_target_pairs={{0,2},{1,3},{2,0},{3,1},{4,6},{5,7},{6,4},{7,5},{8,10},{9,11},{10,... | collective-permute-start | bytes 393224 | tf_op jit(solution)/shard_map/ppermute | solution.py:459
  179.5 13.2 %collective-permute-start.7 = (bf16[32,2048]{1,0:T(8,128)(2,1)S(1)}, bf16[32,2048]{1,0:T(8,128)(2,1)S(1)}, u32[]{:S(2)}, u32[]{:S(2)}) collective-permute-start(bf16[32,2048]{1,0:T(8,128)(2,1)S(1)} %get-tuple-element.21), channel_id=1, source_target_pairs={{0,3},{1,0},{2,1},{3,2},{4,7},{5,4},{6,5},{7,6},{8,11},{9,8},{10,9... | collective-permute-start | bytes 393224 | tf_op jit(solution)/shard_map/ppermute | solution.py:459
  185.5 23.4 %all-to-all-start.6 = ((bf16[16,6,2,16,128]{4,3,2,1,0:T(8,128)(2,1)}), bf16[16,6,2,16,128]{4,3,2,1,0:T(8,128)(2,1)S(1)}, u32[]{:S(2)}, u32[]{:S(2)}) async-start(bf16[16,6,2,16,128]{4,3,2,1,0:T(8,128)(2,1)} %get-tuple-element.29), calls=%async_computation.6 | async-start | bytes 1572864 | tf_op jit(solution)/shard_map/all_to_all | solution.py:455
  196.5 5.0 %collective-permute-start.10 = (bf16[32,2048]{1,0:T(8,128)(2,1)S(1)}, bf16[32,2048]{1,0:T(8,128)(2,1)S(1)}, u32[]{:S(2)}, u32[]{:S(2)}) collective-permute-start(bf16[32,2048]{1,0:T(8,128)(2,1)S(1)} %shard_map.72.refs_1_), channel_id=1, source_target_pairs={{0,3},{1,0},{2,1},{3,2},{4,7},{5,4},{6,5},{7,6},{8,11},{9,8},{10,9... | collective-permute-start | bytes 393224 | tf_op jit(solution)/shard_map/ppermute | solution.py:459
  197.2 6.5 %collective-permute-start.9 = (bf16[32,2048]{1,0:T(8,128)(2,1)S(1)}, bf16[32,2048]{1,0:T(8,128)(2,1)S(1)}, u32[]{:S(2)}, u32[]{:S(2)}) collective-permute-start(bf16[32,2048]{1,0:T(8,128)(2,1)S(1)} %shard_map.72.refs_1_), channel_id=1, source_target_pairs={{0,2},{1,3},{2,0},{3,1},{4,6},{5,7},{6,4},{7,5},{8,10},{9,11},{10,... | collective-permute-start | bytes 393224 | tf_op jit(solution)/shard_map/ppermute | solution.py:459
  198.5 6.6 %collective-permute-start.8 = (bf16[32,2048]{1,0:T(8,128)(2,1)S(1)}, bf16[32,2048]{1,0:T(8,128)(2,1)S(1)}, u32[]{:S(2)}, u32[]{:S(2)}) collective-permute-start(bf16[32,2048]{1,0:T(8,128)(2,1)S(1)} %shard_map.72.refs_1_), channel_id=1, source_target_pairs={{0,1},{1,2},{2,3},{3,0},{4,5},{5,6},{6,7},{7,4},{8,9},{9,10},{10,1... | collective-permute-start | bytes 393224 | tf_op jit(solution)/shard_map/ppermute | solution.py:459
  208.9 18.1 %all-to-all-start.4 = ((bf16[16,6,2,16,128]{4,3,2,1,0:T(8,128)(2,1)}), bf16[16,6,2,16,128]{4,3,2,1,0:T(8,128)(2,1)S(1)}, u32[]{:S(2)}, u32[]{:S(2)}) async-start(bf16[16,6,2,16,128]{4,3,2,1,0:T(8,128)(2,1)} %get-tuple-element.28), calls=%async_computation.4 | async-start | bytes 1572864 | tf_op jit(solution)/shard_map/all_to_all | solution.py:455
  227.1 27.1 %all-to-all-start.7 = ((bf16[64,112,128]{2,1,0:T(8,128)(2,1)}), bf16[64,112,128]{2,1,0:T(8,128)(2,1)S(1)}, u32[]{:S(2)}, u32[]{:S(2)}) async-start(bf16[64,112,128]{2,1,0:T(8,128)(2,1)} %bitcast.32), calls=%async_computation.7 | async-start | bytes 3670016 | tf_op jit(solution)/shard_map/all_to_all | solution.py:455
  254.2 24.9 %all-to-all-start.5 = ((bf16[64,112,128]{2,1,0:T(8,128)(2,1)}), bf16[64,112,128]{2,1,0:T(8,128)(2,1)}, u32[]{:S(2)}, u32[]{:S(2)}) async-start(bf16[64,112,128]{2,1,0:T(8,128)(2,1)} %bitcast.33), calls=%async_computation.5 | async-start | bytes 3670016 | tf_op jit(solution)/shard_map/all_to_all | solution.py:455
  (8 other events, 70.0 us)

commit v4 on v3

--- a/solution.py
+++ b/solution.py
@@ -16,6 +16,8 @@
 CP = 8
 CAP = 6
 STREAMS = 2
+STEP = 2
+AHEAD = 3
 
 
 def params(limit_mib=48, **kw):
@@ -163,8 +165,36 @@
     )(core, xt)
 
 
-def mix_kernel(at_ref, own_ref, sib_ref, *rest):
-    q_refs, (out_ref, q_ref, tmp_ref) = rest[:-3], rest[-3:]
+def arrived_rows(sources, rows_ref, sems, stream):
+    step = pl.program_id(0)
+    _, every, count, experts, _, _ = rows_ref.shape
+
+    def copy(half, i):
+        return pltpu.make_async_copy(
+            sources[half].at[pl.ds(i * count, count), stream * experts : (stream + 1) * experts],
+            rows_ref.at[half, i],
+            sems.at[half, i],
+        )
+
+    @pl.when(step == 0)
+    def _():
+        for i in range(AHEAD):
+            for half in range(2):
+                copy(half, i).start()
+
+    @pl.when(step + AHEAD < every)
+    def _():
+        for half in range(2):
+            copy(half, step + AHEAD).start()
+
+    for half in range(2):
+        copy(half, step).wait()
+    return rows_ref.at[0, step], rows_ref.at[1, step]
+
+
+def mix_kernel(at_ref, own_ref, sib_ref, *rest, stream):
+    q_refs, (out_ref, q_ref, tmp_ref, rows_ref, sems) = rest[:-5], rest[-5:]
+    own_ref, sib_ref = arrived_rows((own_ref, sib_ref), rows_ref, sems, stream)
     core, copy = at_ref[0], at_ref[1]
     copies = len(q_refs)
     lanes = out_ref.shape[4]
@@ -193,17 +223,26 @@
     lanes = lanes // STREAMS
     _, experts, rows, width = own.shape
     experts = experts // STREAMS
-    step = 2
-    block = pl.BlockSpec((step, experts, rows, width), lambda i, _: (i, stream, 0, 0))
+    step = STEP
+    block = pl.BlockSpec(memory_space=pl.ANY)
+
+    def body(*refs):
+        mix_kernel(*refs, stream=stream)
+
     q_block = pl.BlockSpec((step, part, lanes), lambda i, _: (i, 0, stream))
     return pl.pallas_call(
-        mix_kernel,
+        body,
         grid_spec=pltpu.PrefetchScalarGridSpec(
             num_scalar_prefetch=1,
             grid=(chips // step,),
             in_specs=[block, block] + [q_block] * len(q_parts),
             out_specs=pl.BlockSpec((step, CAP, 2, 16, lanes), lambda i, _: (i, 0, 0, 0, 0)),
-            scratch_shapes=[pltpu.VMEM((width, lanes), BF16), pltpu.VMEM((rows, lanes), F32)],
+            scratch_shapes=[
+                pltpu.VMEM((width, lanes), BF16),
+                pltpu.VMEM((rows, lanes), F32),
+                pltpu.VMEM((2, chips // step, step, experts, rows, width), BF16),
+                pltpu.SemaphoreType.DMA((2, chips // step)),
+            ],
         ),
         out_shape=in_hbm((chips, CAP, 2, 16, lanes), BF16),
         compiler_params=params(),
@@ -371,8 +410,9 @@
     )(copy, *parts, hidden, *given)
 
 
-def terms_kernel(core_ref, own_ref, sib_ref, proj_ref, out_ref, rows_ref, sum_ref):
+def terms_kernel(core_ref, own_ref, sib_ref, proj_ref, out_ref, rows_ref, sum_ref, held_ref, sems, *, stream):
     core = core_ref[0]
+    own_ref, sib_ref = arrived_rows((own_ref, sib_ref), held_ref, sems, stream)
     count, experts, _, width = own_ref.shape
     part = width // 4
 
@@ -406,16 +446,25 @@
     chips, _, _, _, lanes = proj.shape
     _, experts, rows, width = own.shape
     experts = experts // STREAMS
-    step = 2
-    block = pl.BlockSpec((step, experts, rows, width), lambda i, _: (i, stream, 0, 0))
-    return pl.pallas_call(
-        terms_kernel,
+    step = STEP
+    block = pl.BlockSpec(memory_space=pl.ANY)
+
+    def body(*refs):
+        terms_kernel(*refs, stream=stream)
+
+    return pl.pallas_call(
+        body,
         grid_spec=pltpu.PrefetchScalarGridSpec(
             num_scalar_prefetch=1,
             grid=(chips // step,),
             in_specs=[block, block, pl.BlockSpec((step, CAP, 2, 16, lanes), lambda i, _: (i, 0, 0, 0, 0))],
             out_specs=pl.BlockSpec((4, step, width // 4, lanes), lambda i, _: (0, i, 0, 0)),
-            scratch_shapes=[pltpu.VMEM((256, lanes), F32), pltpu.VMEM((lanes, 512), F32)],
+            scratch_shapes=[
+                pltpu.VMEM((256, lanes), F32),
+                pltpu.VMEM((lanes, 512), F32),
+                pltpu.VMEM((2, chips // step, step, experts, rows, width), BF16),
+                pltpu.SemaphoreType.DMA((2, chips // step)),
+            ],
         ),
         out_shape=in_hbm((4, chips, width // 4, lanes), BF16),
         compiler_params=params(),

time: 285 us -> 277 us (0.972)
  Pallas kernels: 96.1 us -> 85.8 us
  waiting for transfers between devices: 75.8 us -> 79.9 us
    pallas_call x4, Pallas kernels: 45.5 us -> 35.2 us  [the longest x2 19.2 us: mix(): pl.pallas_call(body, grid_spec=pltpu.PrefetchScalarGridSpec(num_scalar_pr...]
    all_to_all x7, waiting for transfers between devices: 33.4 us -> 37.5 us  [exchange(): return lax.all_to_all(values, axes, split_axis=0, concat_axis=0, tiled=True)]
  transfers between devices with their start and end apart: 24 -> 24, of which waited for: 12 -> 14; matrix products, arithmetic and copies ran while one was open for 1% -> 1% of each run, Pallas kernels for 24% -> 22%
where the time goes in v4:
time: 277 us; the launch traced here: 274 us
  Pallas kernels  85.8 us (31%)
  waiting for transfers between devices  79.9 us (29%)
  starting transfers between devices  73.3 us (26%)
  blocking collectives  30 us (11%)
  local copies, waits for them, and re-layouts  4.43 us (2%)
    all_to_all x7, starting transfers between devices, exchange(): return lax.all_to_all(values, axes, split_axis=0, concat_axis=0, tiled=True)  50 us
    ppermute x16, waiting for transfers between devices, shift(): lax.ppermute(value, 'dp', [(i, (i + step) % copies) for i in range(copies)])  42.3 us
    all_to_all x7, waiting for transfers between devices, exchange(): return lax.all_to_all(values, axes, split_axis=0, concat_axis=0, tiled=True)  37.5 us
    all_to_all x1, blocking collectives, exchange(): return lax.all_to_all(values, axes, split_axis=0, concat_axis=0, tiled=True)  30 us
    ppermute x16, starting transfers between devices, shift(): lax.ppermute(value, 'dp', [(i, (i + step) % copies) for i in range(copies)])  23.3 us
    pallas_call x2, Pallas kernels, dispatch(): pl.pallas_call(body, grid_spec=pltpu.PrefetchScalarGridSpec(num_scalar_pr...  20.1 us
    pallas_call x2, Pallas kernels, mix(): pl.pallas_call(body, grid_spec=pltpu.PrefetchScalarGridSpec(num_scalar_pr...  19.2 us
    pallas_call x2, Pallas kernels, second_terms(): pl.pallas_call(body, grid_spec=pltpu.PrefetchScalarGridSpec(num_scalar_pr...  16 us
  transfers between devices with their start and end apart: 24, of which 14 were waited for; matrix products, arithmetic and copies ran while one was open for 1% of the time, Pallas kernels for 22%

profile of v4, /device:TPU:6, one launch (start us, length us, event | category | flops | bytes accessed | tf_op | source)
XLA Modules:
  0.0 274.2 jit_solution(2448379430945659969)
XLA Ops:
  2.8 7.4 %all-to-all-start = ((bf16[16,112,256]{2,1,0:T(8,128)(2,1)}), bf16[16,112,256]{2,1,0:T(8,128)(2,1)S(1)}, u32[]{:S(2)}, u32[]{:S(2)}) async-start(bf16[16,112,256]{2,1,0:T(8,128)(2,1)} %bitcast.35), calls=%async_computation | async-start | bytes 1835008 | tf_op jit(solution)/shard_map/all_to_all | solution.py:504
  10.2 4.0 %prepare.1 = bf16[16,480,128]{2,1,0:T(8,128)(2,1)} custom-call(s32[8,128]{1,0:T(8,128)} %bitcast.38, f32[8,128]{1,0:T(8,128)} %bitcast.39, bf16[128,7168]{1,0:T(8,128)(2,1)} %bitcast.37), custom_call_target="tpu_custom_call" | custom-call | tf_op jit(solution)/shard_map/prepare/pallas_call | solution.py:91
  14.2 9.1 %all-to-all-done.refs_3_ = bf16[16,112,256]{2,1,0:T(8,128)(2,1)S(1)} async-done(((bf16[16,112,256]{2,1,0:T(8,128)(2,1)}), bf16[16,112,256]{2,1,0:T(8,128)(2,1)S(1)}, u32[]{:S(2)}, u32[]{:S(2)}) %all-to-all-start) | async-done | bytes 917536 | tf_op jit(solution)/shard_map/all_to_all | solution.py:504
  23.3 30.0 %all_to_all.40.refs_1_ = bf16[16,480,128]{2,1,0:T(8,128)(2,1)S(1)} all-to-all(bf16[16,480,128]{2,1,0:T(8,128)(2,1)} %prepare.1), channel_id=1, replica_groups=mesh['chip'=16,'core'=2,'dp'=4] {'chip'}, dimensions={0} | all-to-all | bytes 3932160 | tf_op jit(solution)/shard_map/all_to_all | solution.py:504
  57.3 21.0 %collective-permute-done.2.refs_6_ = bf16[16,112,256]{2,1,0:T(8,128)(2,1)S(1)} collective-permute-done((bf16[16,112,256]{2,1,0:T(8,128)(2,1)S(1)}, bf16[16,112,256]{2,1,0:T(8,128)(2,1)S(1)}, u32[]{:S(2)}, u32[]{:S(2)}) %collective-permute-start.2) | collective-permute-done | bytes 917536 | tf_op jit(solution)/shard_map/ppermute | solution.py:508
  83.6 9.4 %collective-permute-done.3 = bf16[8,112,256]{2,1,0:T(8,128)(2,1)S(1)} collective-permute-done((bf16[8,112,256]{2,1,0:T(8,128)(2,1)}, bf16[8,112,256]{2,1,0:T(8,128)(2,1)S(1)}, u32[]{:S(2)}, u32[]{:S(2)}) %collective-permute-start.3) | collective-permute-done | bytes 458784 | tf_op jit(solution)/shard_map/ppermute | solution.py:508
  94.5 9.3 %shard_map.68 = bf16[128,128,448]{2,1,0:T(8,128)(2,1)} custom-call(s32[1]{0:T(128)} %bitcast.1.refs_0_, bf16[16,480,128]{2,1,0:T(8,128)(2,1)S(1)} %all_to_all.40.refs_1_), custom_call_target="tpu_custom_call" | custom-call | flops 1879048192 | bytes 14680064 | tf_op jit(solution)/shard_map/pallas_call | solution.py:152
  103.8 10.8 %shard_map.69 = bf16[128,128,448]{2,1,0:T(8,128)(2,1)} custom-call(s32[1]{0:T(128)} %bitcast.1.refs_0_, bf16[16,480,128]{2,1,0:T(8,128)(2,1)} %collective-permute-done.refs_1_), custom_call_target="tpu_custom_call" | custom-call | flops 1879048192 | bytes 14680064 | tf_op jit(solution)/shard_map/pallas_call | solution.py:152
  114.6 9.6 %shard_map.73 = bf16[16,6,2,16,128]{4,3,2,1,0:T(8,128)(2,1)} custom-call(s32[2]{0:T(128)S(1)} %pad_add_fusion.refs_0_, bf16[16,8,128,448]{3,2,1,0:T(8,128)(2,1)} %bitcast.20, bf16[16,8,128,448]{3,2,1,0:T(8,128)(2,1)} %bitcast.24, bf16[16,112,256]{2,1,0:T(8,128)(2,1)S(1)} %all-to-all-done.refs_3_, bf16[16,112,256]{2,1,0:T(8,128)(2,1)S(1)} %copy-done.4, ...), custom_call_target="tpu_custom_call" | custom-call | flops 3758096384 | bytes 14680064 | tf_op jit(solution)/shard_map/pallas_call | solution.py:233
  124.2 6.6 %all-to-all-start.3 = ((bf16[16,6,2,16,128]{4,3,2,1,0:T(8,128)(2,1)}), bf16[16,6,2,16,128]{4,3,2,1,0:T(8,128)(2,1)S(1)}, u32[]{:S(2)}, u32[]{:S(2)}) async-start(bf16[16,6,2,16,128]{4,3,2,1,0:T(8,128)(2,1)} %shard_map.73), calls=%async_computation.3 | async-start | bytes 1572864 | tf_op jit(solution)/shard_map/all_to_all | solution.py:504
  132.0 9.6 %shard_map.70 = bf16[16,6,2,16,128]{4,3,2,1,0:T(8,128)(2,1)} custom-call(s32[2]{0:T(128)S(1)} %pad_add_fusion.refs_0_, bf16[16,8,128,448]{3,2,1,0:T(8,128)(2,1)} %bitcast.21, bf16[16,8,128,448]{3,2,1,0:T(8,128)(2,1)} %bitcast.25, bf16[16,112,256]{2,1,0:T(8,128)(2,1)S(1)} %all-to-all-done.refs_3_, bf16[16,112,256]{2,1,0:T(8,128)(2,1)S(1)} %copy-done.5, ...), custom_call_target="tpu_custom_call" | custom-call | flops 3758096384 | bytes 14680064 | tf_op jit(solution)/shard_map/pallas_call | solution.py:233
  141.9 7.0 %all-to-all-start.2 = ((bf16[16,6,2,16,128]{4,3,2,1,0:T(8,128)(2,1)}), bf16[16,6,2,16,128]{4,3,2,1,0:T(8,128)(2,1)S(1)}, u32[]{:S(2)}, u32[]{:S(2)}) async-start(bf16[16,6,2,16,128]{4,3,2,1,0:T(8,128)(2,1)} %shard_map.70), calls=%async_computation.2 | async-start | bytes 1572864 | tf_op jit(solution)/shard_map/all_to_all | solution.py:504
  152.3 4.6 %collective-permute-start.12 = (bf16[32,2048]{1,0:T(8,128)(2,1)S(1)}, bf16[32,2048]{1,0:T(8,128)(2,1)S(1)}, u32[]{:S(2)}, u32[]{:S(2)}) collective-permute-start(bf16[32,2048]{1,0:T(8,128)(2,1)S(1)} %get-tuple-element.24), channel_id=1, source_target_pairs={{0,2},{1,3},{2,0},{3,1},{4,6},{5,7},{6,4},{7,5},{8,10},{9,11},{10,... | collective-permute-start | bytes 393224 | tf_op jit(solution)/shard_map/ppermute | solution.py:508
  177.3 3.8 %shard_map.76 = (f32[8,32,2048]{2,1,0:T(8,128)}, bf16[16,6,2,16,128]{4,3,2,1,0:T(8,128)(2,1)}) custom-call(s32[1]{0:T(128)} %bitcast.copy_ref.refs_0_, bf16[32,2048]{1,0:T(8,128)(2,1)S(1)} %shard_map.75.refs_1_, bf16[32,2048]{1,0:T(8,128)(2,1)S(1)} %collective-permute-done.14.refs_2_, bf16[32,2048]{1,0:T(8,128)(2,1)S(1)} %collective-permute-done.15.refs_3_, ...), custom_call_target="tpu_custom_call" | custom-call | flops 805306368 | bytes 3145728 | tf_op jit(solution)/shard_map/pallas_call | solution.py:387
  181.1 7.2 %all-to-all-start.6 = ((bf16[16,6,2,16,128]{4,3,2,1,0:T(8,128)(2,1)}), bf16[16,6,2,16,128]{4,3,2,1,0:T(8,128)(2,1)S(1)}, u32[]{:S(2)}, u32[]{:S(2)}) async-start(bf16[16,6,2,16,128]{4,3,2,1,0:T(8,128)(2,1)} %get-tuple-element.29), calls=%async_computation.6 | async-start | bytes 1572864 | tf_op jit(solution)/shard_map/all_to_all | solution.py:504
  188.3 3.7 %shard_map.72.refs_1_ = bf16[32,2048]{1,0:T(8,128)(2,1)S(1)} custom-call(bf16[32,2048]{1,0:T(8,128)(2,1)S(1)} %get-tuple-element.18.refs_0_, bf16[32,2048]{1,0:T(8,128)(2,1)S(1)} %collective-permute-done.5.refs_1_, bf16[32,2048]{1,0:T(8,128)(2,1)S(1)} %collective-permute-done.6.refs_2_, bf16[32,2048]{1,0:T(8,128)(2,1)S(1)} %collective-permute-done.7.refs_3_), custom_call_target="tpu_custom_call" | custom-call | flops 5000000000 | bytes 524288 | tf_op jit(solution)/shard_map/pallas_call | solution.py:334
  200.7 3.9 %shard_map.77 = (f32[8,32,2048]{2,1,0:T(8,128)}, bf16[16,6,2,16,128]{4,3,2,1,0:T(8,128)(2,1)}) custom-call(s32[1]{0:T(128)} %bitcast.copy_ref.refs_0_, bf16[32,2048]{1,0:T(8,128)(2,1)S(1)} %shard_map.72.refs_1_, bf16[32,2048]{1,0:T(8,128)(2,1)S(1)} %collective-permute-done.8.refs_2_, ...), custom_call_target="tpu_custom_call", output_to_operand_aliasing={{0}: (6, {})} | custom-call | flops 805306368 | bytes 3145728 | tf_op jit(solution)/shard_map/pallas_call | solution.py:387
  204.5 7.2 %all-to-all-start.4 = ((bf16[16,6,2,16,128]{4,3,2,1,0:T(8,128)(2,1)}), bf16[16,6,2,16,128]{4,3,2,1,0:T(8,128)(2,1)S(1)}, u32[]{:S(2)}, u32[]{:S(2)}) async-start(bf16[16,6,2,16,128]{4,3,2,1,0:T(8,128)(2,1)} %get-tuple-element.28), calls=%async_computation.4 | async-start | bytes 1572864 | tf_op jit(solution)/shard_map/all_to_all | solution.py:504
  211.8 8.0 %shard_map.79 = bf16[4,16,112,128]{3,2,1,0:T(8,128)(2,1)} custom-call(s32[1]{0:T(128)} %bitcast.1.refs_0_, bf16[16,8,128,448]{3,2,1,0:T(8,128)(2,1)} %bitcast.22, bf16[16,8,128,448]{3,2,1,0:T(8,128)(2,1)} %bitcast.26, bf16[16,6,2,16,128]{4,3,2,1,0:T(8,128)(2,1)S(1)} %all-to-all-done.6.refs_3_), custom_call_target="tpu_custom_call" | custom-call | flops 3758096384 | bytes 14680064 | tf_op jit(solution)/shard_map/pallas_call | solution.py:455
  220.7 7.6 %all-to-all-start.7 = ((bf16[64,112,128]{2,1,0:T(8,128)(2,1)}), bf16[64,112,128]{2,1,0:T(8,128)(2,1)S(1)}, u32[]{:S(2)}, u32[]{:S(2)}) async-start(bf16[64,112,128]{2,1,0:T(8,128)(2,1)} %bitcast.32), calls=%async_computation.7 | async-start | bytes 3670016 | tf_op jit(solution)/shard_map/all_to_all | solution.py:504
  228.3 8.0 %shard_map.78 = bf16[4,16,112,128]{3,2,1,0:T(8,128)(2,1)} custom-call(s32[1]{0:T(128)} %bitcast.1.refs_0_, bf16[16,8,128,448]{3,2,1,0:T(8,128)(2,1)} %bitcast.23, bf16[16,8,128,448]{3,2,1,0:T(8,128)(2,1)} %bitcast.27, bf16[16,6,2,16,128]{4,3,2,1,0:T(8,128)(2,1)S(1)} %all-to-all-done.4.refs_3_), custom_call_target="tpu_custom_call" | custom-call | flops 3758096384 | bytes 14680064 | tf_op jit(solution)/shard_map/pallas_call | solution.py:455
  236.3 10.6 %all-to-all-done.7 = bf16[64,112,128]{2,1,0:T(8,128)(2,1)S(1)} async-done(((bf16[64,112,128]{2,1,0:T(8,128)(2,1)}), bf16[64,112,128]{2,1,0:T(8,128)(2,1)S(1)}, u32[]{:S(2)}, u32[]{:S(2)}) %all-to-all-start.7) | async-done | bytes 1835040 | tf_op jit(solution)/shard_map/all_to_all | solution.py:504
  246.9 7.0 %all-to-all-start.5 = ((bf16[64,112,128]{2,1,0:T(8,128)(2,1)}), bf16[64,112,128]{2,1,0:T(8,128)(2,1)}, u32[]{:S(2)}, u32[]{:S(2)}) async-start(bf16[64,112,128]{2,1,0:T(8,128)(2,1)} %bitcast.33), calls=%async_computation.5 | async-start | bytes 3670016 | tf_op jit(solution)/shard_map/all_to_all | solution.py:504
  255.2 16.6 %all-to-all-done.5 = bf16[64,112,128]{2,1,0:T(8,128)(2,1)} async-done(((bf16[64,112,128]{2,1,0:T(8,128)(2,1)}), bf16[64,112,128]{2,1,0:T(8,128)(2,1)}, u32[]{:S(2)}, u32[]{:S(2)}) %all-to-all-start.5) | async-done | bytes 1835040 | tf_op jit(solution)/shard_map/all_to_all | solution.py:504
  (62 shorter events, 51.4 us)
Async XLA Ops:
  2.8 20.5 %all-to-all-start = ((bf16[16,112,256]{2,1,0:T(8,128)(2,1)}), bf16[16,112,256]{2,1,0:T(8,128)(2,1)S(1)}, u32[]{:S(2)}, u32[]{:S(2)}) async-start(bf16[16,112,256]{2,1,0:T(8,128)(2,1)} %bitcast.35), calls=%async_computation | async-start | bytes 1835008 | tf_op jit(solution)/shard_map/all_to_all | solution.py:504
  53.3 50.5 %collective-permute-start = (bf16[16,480,128]{2,1,0:T(8,128)(2,1)S(1)}, bf16[16,480,128]{2,1,0:T(8,128)(2,1)}, u32[]{:S(2)}, u32[]{:S(2)}) collective-permute-start(bf16[16,480,128]{2,1,0:T(8,128)(2,1)S(1)} %all_to_all.40.refs_1_), channel_id=1, source_target_pairs={{0,4},{4,0},{1,5},{5,1},{2,6},{6,2},{3,7},{7,3},{8,12},{12,8},{9,1... | collective-permute-start | bytes 5898248 | tf_op jit(solution)/shard_map/ppermute | solution.py:536
  53.3 25.1 %collective-permute-start.2 = (bf16[16,112,256]{2,1,0:T(8,128)(2,1)S(1)}, bf16[16,112,256]{2,1,0:T(8,128)(2,1)S(1)}, u32[]{:S(2)}, u32[]{:S(2)}) collective-permute-start(bf16[16,112,256]{2,1,0:T(8,128)(2,1)S(1)} %all-to-all-done.refs_3_), channel_id=1, source_target_pairs={{0,1},{1,2},{2,3},{3,0},{4,5},{5,6},{6,7},{7,4},{8,9},{9,10},{10,1... | collective-permute-start | bytes 2752520 | tf_op jit(solution)/shard_map/ppermute | solution.py:508
  55.2 24.0 %collective-permute-start.1 = (bf16[16,112,256]{2,1,0:T(8,128)(2,1)S(1)}, bf16[16,112,256]{2,1,0:T(8,128)(2,1)S(1)}, u32[]{:S(2)}, u32[]{:S(2)}) collective-permute-start(bf16[16,112,256]{2,1,0:T(8,128)(2,1)S(1)} %all-to-all-done.refs_3_), channel_id=1, source_target_pairs={{0,3},{1,0},{2,1},{3,2},{4,7},{5,4},{6,5},{7,6},{8,11},{9,8},{10,9... | collective-permute-start | bytes 2752520 | tf_op jit(solution)/shard_map/ppermute | solution.py:508
  79.2 13.8 %collective-permute-start.3 = (bf16[8,112,256]{2,1,0:T(8,128)(2,1)}, bf16[8,112,256]{2,1,0:T(8,128)(2,1)S(1)}, u32[]{:S(2)}, u32[]{:S(2)}) collective-permute-start(bf16[8,112,256]{2,1,0:T(8,128)(2,1)} %slice.8), channel_id=1, source_target_pairs={{0,1},{1,2},{2,3},{3,0},{4,5},{5,6},{6,7},{7,4},{8,9},{9,10},{10,1... | collective-permute-start | bytes 1376264 | tf_op jit(solution)/shard_map/ppermute | solution.py:508
  80.5 12.9 %collective-permute-start.4 = (bf16[8,112,256]{2,1,0:T(8,128)(2,1)}, bf16[8,112,256]{2,1,0:T(8,128)(2,1)}, u32[]{:S(2)}, u32[]{:S(2)}) collective-permute-start(bf16[8,112,256]{2,1,0:T(8,128)(2,1)} %slice.9), channel_id=1, source_target_pairs={{0,3},{1,0},{2,1},{3,2},{4,7},{5,4},{6,5},{7,6},{8,11},{9,8},{10,9... | collective-permute-start | bytes 1376264 | tf_op jit(solution)/shard_map/ppermute | solution.py:508
  124.2 17.6 %all-to-all-start.3 = ((bf16[16,6,2,16,128]{4,3,2,1,0:T(8,128)(2,1)}), bf16[16,6,2,16,128]{4,3,2,1,0:T(8,128)(2,1)S(1)}, u32[]{:S(2)}, u32[]{:S(2)}) async-start(bf16[16,6,2,16,128]{4,3,2,1,0:T(8,128)(2,1)} %shard_map.73), calls=%async_computation.3 | async-start | bytes 1572864 | tf_op jit(solution)/shard_map/all_to_all | solution.py:504
  141.9 26.7 %all-to-all-start.2 = ((bf16[16,6,2,16,128]{4,3,2,1,0:T(8,128)(2,1)}), bf16[16,6,2,16,128]{4,3,2,1,0:T(8,128)(2,1)S(1)}, u32[]{:S(2)}, u32[]{:S(2)}) async-start(bf16[16,6,2,16,128]{4,3,2,1,0:T(8,128)(2,1)} %shard_map.70), calls=%async_computation.2 | async-start | bytes 1572864 | tf_op jit(solution)/shard_map/all_to_all | solution.py:504
  151.7 8.0 %collective-permute-start.11 = (bf16[32,2048]{1,0:T(8,128)(2,1)S(1)}, bf16[32,2048]{1,0:T(8,128)(2,1)S(1)}, u32[]{:S(2)}, u32[]{:S(2)}) collective-permute-start(bf16[32,2048]{1,0:T(8,128)(2,1)S(1)} %get-tuple-element.23), channel_id=1, source_target_pairs={{0,1},{1,2},{2,3},{3,0},{4,5},{5,6},{6,7},{7,4},{8,9},{9,10},{10,1... | collective-permute-start | bytes 393224 | tf_op jit(solution)/shard_map/ppermute | solution.py:508
  152.3 9.0 %collective-permute-start.12 = (bf16[32,2048]{1,0:T(8,128)(2,1)S(1)}, bf16[32,2048]{1,0:T(8,128)(2,1)S(1)}, u32[]{:S(2)}, u32[]{:S(2)}) collective-permute-start(bf16[32,2048]{1,0:T(8,128)(2,1)S(1)} %get-tuple-element.24), channel_id=1, source_target_pairs={{0,2},{1,3},{2,0},{3,1},{4,6},{5,7},{6,4},{7,5},{8,10},{9,11},{10,... | collective-permute-start | bytes 393224 | tf_op jit(solution)/shard_map/ppermute | solution.py:508
  156.9 5.0 %collective-permute-start.13 = (bf16[32,2048]{1,0:T(8,128)(2,1)S(1)}, bf16[32,2048]{1,0:T(8,128)(2,1)S(1)}, u32[]{:S(2)}, u32[]{:S(2)}) collective-permute-start(bf16[32,2048]{1,0:T(8,128)(2,1)S(1)} %get-tuple-element.25), channel_id=1, source_target_pairs={{0,3},{1,0},{2,1},{3,2},{4,7},{5,4},{6,5},{7,6},{8,11},{9,8},{10,9... | collective-permute-start | bytes 393224 | tf_op jit(solution)/shard_map/ppermute | solution.py:508
  165.6 9.5 %collective-permute-start.16 = (bf16[32,2048]{1,0:T(8,128)(2,1)S(1)}, bf16[32,2048]{1,0:T(8,128)(2,1)S(1)}, u32[]{:S(2)}, u32[]{:S(2)}) collective-permute-start(bf16[32,2048]{1,0:T(8,128)(2,1)S(1)} %shard_map.75.refs_1_), channel_id=1, source_target_pairs={{0,3},{1,0},{2,1},{3,2},{4,7},{5,4},{6,5},{7,6},{8,11},{9,8},{10,9... | collective-permute-start | bytes 393224 | tf_op jit(solution)/shard_map/ppermute | solution.py:508
  167.5 9.7 %collective-permute-start.15 = (bf16[32,2048]{1,0:T(8,128)(2,1)S(1)}, bf16[32,2048]{1,0:T(8,128)(2,1)S(1)}, u32[]{:S(2)}, u32[]{:S(2)}) collective-permute-start(bf16[32,2048]{1,0:T(8,128)(2,1)S(1)} %shard_map.75.refs_1_), channel_id=1, source_target_pairs={{0,2},{1,3},{2,0},{3,1},{4,6},{5,7},{6,4},{7,5},{8,10},{9,11},{10,... | collective-permute-start | bytes 393224 | tf_op jit(solution)/shard_map/ppermute | solution.py:508
  167.6 9.7 %collective-permute-start.14 = (bf16[32,2048]{1,0:T(8,128)(2,1)S(1)}, bf16[32,2048]{1,0:T(8,128)(2,1)S(1)}, u32[]{:S(2)}, u32[]{:S(2)}) collective-permute-start(bf16[32,2048]{1,0:T(8,128)(2,1)S(1)} %shard_map.75.refs_1_), channel_id=1, source_target_pairs={{0,1},{1,2},{2,3},{3,0},{4,5},{5,6},{6,7},{7,4},{8,9},{9,10},{10,1... | collective-permute-start | bytes 393224 | tf_op jit(solution)/shard_map/ppermute | solution.py:508
  171.3 17.0 %collective-permute-start.5 = (bf16[32,2048]{1,0:T(8,128)(2,1)S(1)}, bf16[32,2048]{1,0:T(8,128)(2,1)S(1)}, u32[]{:S(2)}, u32[]{:S(2)}) collective-permute-start(bf16[32,2048]{1,0:T(8,128)(2,1)S(1)} %get-tuple-element.19), channel_id=1, source_target_pairs={{0,1},{1,2},{2,3},{3,0},{4,5},{5,6},{6,7},{7,4},{8,9},{9,10},{10,1... | collective-permute-start | bytes 393224 | tf_op jit(solution)/shard_map/ppermute | solution.py:508
  173.9 14.5 %collective-permute-start.6 = (bf16[32,2048]{1,0:T(8,128)(2,1)S(1)}, bf16[32,2048]{1,0:T(8,128)(2,1)S(1)}, u32[]{:S(2)}, u32[]{:S(2)}) collective-permute-start(bf16[32,2048]{1,0:T(8,128)(2,1)S(1)} %get-tuple-element.20), channel_id=1, source_target_pairs={{0,2},{1,3},{2,0},{3,1},{4,6},{5,7},{6,4},{7,5},{8,10},{9,11},{10,... | collective-permute-start | bytes 393224 | tf_op jit(solution)/shard_map/ppermute | solution.py:508
  175.1 13.2 %collective-permute-start.7 = (bf16[32,2048]{1,0:T(8,128)(2,1)S(1)}, bf16[32,2048]{1,0:T(8,128)(2,1)S(1)}, u32[]{:S(2)}, u32[]{:S(2)}) collective-permute-start(bf16[32,2048]{1,0:T(8,128)(2,1)S(1)} %get-tuple-element.21), channel_id=1, source_target_pairs={{0,3},{1,0},{2,1},{3,2},{4,7},{5,4},{6,5},{7,6},{8,11},{9,8},{10,9... | collective-permute-start | bytes 393224 | tf_op jit(solution)/shard_map/ppermute | solution.py:508
  181.1 23.4 %all-to-all-start.6 = ((bf16[16,6,2,16,128]{4,3,2,1,0:T(8,128)(2,1)}), bf16[16,6,2,16,128]{4,3,2,1,0:T(8,128)(2,1)S(1)}, u32[]{:S(2)}, u32[]{:S(2)}) async-start(bf16[16,6,2,16,128]{4,3,2,1,0:T(8,128)(2,1)} %get-tuple-element.29), calls=%async_computation.6 | async-start | bytes 1572864 | tf_op jit(solution)/shard_map/all_to_all | solution.py:504
  192.1 5.0 %collective-permute-start.10 = (bf16[32,2048]{1,0:T(8,128)(2,1)S(1)}, bf16[32,2048]{1,0:T(8,128)(2,1)S(1)}, u32[]{:S(2)}, u32[]{:S(2)}) collective-permute-start(bf16[32,2048]{1,0:T(8,128)(2,1)S(1)} %shard_map.72.refs_1_), channel_id=1, source_target_pairs={{0,3},{1,0},{2,1},{3,2},{4,7},{5,4},{6,5},{7,6},{8,11},{9,8},{10,9... | collective-permute-start | bytes 393224 | tf_op jit(solution)/shard_map/ppermute | solution.py:508
  192.8 6.5 %collective-permute-start.9 = (bf16[32,2048]{1,0:T(8,128)(2,1)S(1)}, bf16[32,2048]{1,0:T(8,128)(2,1)S(1)}, u32[]{:S(2)}, u32[]{:S(2)}) collective-permute-start(bf16[32,2048]{1,0:T(8,128)(2,1)S(1)} %shard_map.72.refs_1_), channel_id=1, source_target_pairs={{0,2},{1,3},{2,0},{3,1},{4,6},{5,7},{6,4},{7,5},{8,10},{9,11},{10,... | collective-permute-start | bytes 393224 | tf_op jit(solution)/shard_map/ppermute | solution.py:508
  194.1 6.6 %collective-permute-start.8 = (bf16[32,2048]{1,0:T(8,128)(2,1)S(1)}, bf16[32,2048]{1,0:T(8,128)(2,1)S(1)}, u32[]{:S(2)}, u32[]{:S(2)}) collective-permute-start(bf16[32,2048]{1,0:T(8,128)(2,1)S(1)} %shard_map.72.refs_1_), channel_id=1, source_target_pairs={{0,1},{1,2},{2,3},{3,0},{4,5},{5,6},{6,7},{7,4},{8,9},{9,10},{10,1... | collective-permute-start | bytes 393224 | tf_op jit(solution)/shard_map/ppermute | solution.py:508
  204.5 16.2 %all-to-all-start.4 = ((bf16[16,6,2,16,128]{4,3,2,1,0:T(8,128)(2,1)}), bf16[16,6,2,16,128]{4,3,2,1,0:T(8,128)(2,1)S(1)}, u32[]{:S(2)}, u32[]{:S(2)}) async-start(bf16[16,6,2,16,128]{4,3,2,1,0:T(8,128)(2,1)} %get-tuple-element.28), calls=%async_computation.4 | async-start | bytes 1572864 | tf_op jit(solution)/shard_map/all_to_all | solution.py:504
  220.7 26.2 %all-to-all-start.7 = ((bf16[64,112,128]{2,1,0:T(8,128)(2,1)}), bf16[64,112,128]{2,1,0:T(8,128)(2,1)S(1)}, u32[]{:S(2)}, u32[]{:S(2)}) async-start(bf16[64,112,128]{2,1,0:T(8,128)(2,1)} %bitcast.32), calls=%async_computation.7 | async-start | bytes 3670016 | tf_op jit(solution)/shard_map/all_to_all | solution.py:504
  246.9 24.9 %all-to-all-start.5 = ((bf16[64,112,128]{2,1,0:T(8,128)(2,1)}), bf16[64,112,128]{2,1,0:T(8,128)(2,1)}, u32[]{:S(2)}, u32[]{:S(2)}) async-start(bf16[64,112,128]{2,1,0:T(8,128)(2,1)} %bitcast.33), calls=%async_computation.5 | async-start | bytes 3670016 | tf_op jit(solution)/shard_map/all_to_all | solution.py:504
  (8 other events, 67.9 us)

commit v5 on v4

--- a/solution.py
+++ b/solution.py
@@ -410,8 +410,16 @@
     )(copy, *parts, hidden, *given)
 
 
-def terms_kernel(core_ref, own_ref, sib_ref, proj_ref, out_ref, rows_ref, sum_ref, held_ref, sems, *, stream):
-    core = core_ref[0]
+def terms_kernel(at_ref, own_ref, sib_ref, proj_ref, *refs, stream):
+    low_refs, high_refs, (rows_ref, sum_ref, held_ref, sems, sort_ref) = refs[:2], refs[2:4], refs[4:]
+    core, copy = at_ref[0], at_ref[1]
+    low = pl.program_id(0) < pl.num_programs(0) // 2
+
+    def slot(p):
+        apart = jnp.bitwise_xor(copy, p)
+        mixed = jnp.where(low, jnp.where(apart == 1, 0, 3), jnp.where(apart == 1, 3, 0))
+        return jnp.where(apart == 0, 2, jnp.where(apart == 2, 1, mixed))
+
     own_ref, sib_ref = arrived_rows((own_ref, sib_ref), held_ref, sems, stream)
     count, experts, _, width = own_ref.shape
     part = width // 4
@@ -438,15 +446,22 @@
             while done < tall:
                 p, offset = divmod(i * 128 + done, part)
                 step = min(tall - done, part - offset)
-                out_ref[p, n, offset : offset + step, :] = back[done : done + step]
+                sort_ref[slot(p), n, offset : offset + step, :] = back[done : done + step]
                 done += step
-
-
-def second_terms(core, own, sib, proj, stream):
+    for here, out_refs in ((low, low_refs), (jnp.logical_not(low), high_refs)):
+
+        @pl.when(here)
+        def _():
+            out_refs[0][...] = sort_ref[0:2]
+            out_refs[1][...] = sort_ref[2:4]
+
+
+def second_terms(at, own, sib, proj, stream):
     chips, _, _, _, lanes = proj.shape
     _, experts, rows, width = own.shape
     experts = experts // STREAMS
     step = STEP
+    half = chips // step // 2
     block = pl.BlockSpec(memory_space=pl.ANY)
 
     def body(*refs):
@@ -458,22 +473,28 @@
             num_scalar_prefetch=1,
             grid=(chips // step,),
             in_specs=[block, block, pl.BlockSpec((step, CAP, 2, 16, lanes), lambda i, _: (i, 0, 0, 0, 0))],
-            out_specs=pl.BlockSpec((4, step, width // 4, lanes), lambda i, _: (0, i, 0, 0)),
+            out_specs=[
+                pl.BlockSpec((2, step, width // 4, lanes), lambda i, _: (0, jnp.minimum(i, half - 1), 0, 0)),
+                pl.BlockSpec((2, step, width // 4, lanes), lambda i, _: (0, jnp.minimum(i, half - 1), 0, 0)),
+                pl.BlockSpec((2, step, width // 4, lanes), lambda i, _: (0, jnp.maximum(i - half, 0), 0, 0)),
+                pl.BlockSpec((2, step, width // 4, lanes), lambda i, _: (0, jnp.maximum(i - half, 0), 0, 0)),
+            ],
             scratch_shapes=[
                 pltpu.VMEM((256, lanes), F32),
                 pltpu.VMEM((lanes, 512), F32),
                 pltpu.VMEM((2, chips // step, step, experts, rows, width), BF16),
                 pltpu.SemaphoreType.DMA((2, chips // step)),
+                pltpu.VMEM((4, step, width // 4, lanes), BF16),
             ],
         ),
-        out_shape=in_hbm((4, chips, width // 4, lanes), BF16),
+        out_shape=[shape_of((2, chips // 2, width // 4, lanes), BF16)] * 4,
         compiler_params=params(),
         cost_estimate=pl.CostEstimate(
             flops=4 * chips * experts * rows * width * 256,
             bytes_accessed=4 * chips * experts * rows * width,
             transcendentals=0,
         ),
-    )(core, own, sib, proj)
+    )(at, own, sib, proj)
 
 
 def gather_kernel(parts_ref, *refs):
@@ -506,6 +527,35 @@
 
 def shift(value, step, copies):
     return lax.ppermute(value, "dp", [(i, (i + step) % copies) for i in range(copies)])
+
+
+def first_sum_kernel(low_ref, low_got_ref, high_ref, high_got_ref, *out_refs):
+    for k, (kept_ref, got_ref) in enumerate(((low_ref, low_got_ref), (high_ref, high_got_ref))):
+        out_refs[2 * k][...] = kept_ref[0].astype(F32) + got_ref[0].astype(F32)
+        out_refs[2 * k + 1][...] = (kept_ref[1].astype(F32) + got_ref[1].astype(F32)).astype(BF16)
+
+
+def last_sum_kernel(low_ref, low_got_ref, high_ref, high_got_ref, out_ref):
+    half = low_ref.shape[0]
+    out_ref[:half] = (low_ref[...] + low_got_ref[...].astype(F32)).astype(BF16)
+    out_ref[half:] = (high_ref[...] + high_got_ref[...].astype(F32)).astype(BF16)
+
+
+def summed_over_copies(low_sent, low_kept, high_sent, high_kept, copies):
+    near = [(i, i ^ 1) for i in range(copies)]
+    far = [(i, i ^ 3) for i in range(copies)]
+    _, chips, columns, lanes = low_kept.shape
+    shape = (chips, columns, lanes)
+    low_got = lax.ppermute(low_sent, "dp", near)
+    high_got = lax.ppermute(high_sent, "dp", far)
+    low, low_sent, high, high_sent = pl.pallas_call(
+        first_sum_kernel, out_shape=[shape_of(shape, F32), shape_of(shape, BF16)] * 2, compiler_params=params()
+    )(low_kept, low_got, high_kept, high_got)
+    low_got = lax.ppermute(low_sent, "dp", far)
+    high_got = lax.ppermute(high_sent, "dp", near)
+    return pl.pallas_call(
+        last_sum_kernel, out_shape=in_hbm((2 * chips, columns, lanes), BF16), compiler_params=params()
+    )(low, low_got, high, high_got)
 
 
 def around(part, copies):
@@ -547,9 +597,11 @@
         ortho = ortho_of(factor)
         ortho = [ortho] + [shift(ortho, k, copies) for k in range(1, copies)]
         basis, proj = project(copy, ortho, hidden, s, basis, chips)
-        terms = second_terms(core, own, sib, exchange(proj, "chip"), s)
-        terms = exchange(terms.reshape(copies * chips, -1, here * rank), ("dp", "chip"))
-        sums = owned_columns(terms.reshape(copies, width // copies, here * rank), s, sums)
+        proj = exchange(proj, "chip")
+        terms = second_terms(at, own, sib, proj, s)
+        terms = summed_over_copies(*terms, copies)
+        terms = exchange(terms, "chip")
+        sums = owned_columns(terms.reshape(1, width // copies, here * rank), s, sums)
     return (basis, sums.reshape(experts, rank, width // copies))
 
 

time: 277 us -> 282 us (1.018)
  starting transfers between devices: 73.3 us -> 85.2 us
  waiting for transfers between devices: 79.9 us -> 69.2 us
  Pallas kernels: 85.8 us -> 89.1 us
    all_to_all x7, waiting for transfers between devices: 37.5 us -> 15.5 us  [exchange(): return lax.all_to_all(values, axes, split_axis=0, concat_axis=0, tiled=True)]
    ppermute x0 -> x8, waiting for transfers between devices: none -> 13.6 us  [the longest x2 13 us: summed_over_copies(): low_got = lax.ppermute(low_sent, 'dp', far)]
    ppermute x0 -> x8, starting transfers between devices: none -> 9.9 us  [the longest x2 4.65 us: summed_over_copies(): low_got = lax.ppermute(low_sent, 'dp', far)]
    pallas_call x0 -> x4, Pallas kernels: none -> 3.17 us  [the longest x2 1.75 us: summed_over_copies(): pl.pallas_call(last_sum_kernel, out_shape=in_hbm((2 * chips, columns, lan...]
  transfers between devices with their start and end apart: 24 -> 32, of which waited for: 14 -> 14; matrix products, arithmetic and copies ran while one was open for 1% -> 1% of each run, Pallas kernels for 22% -> 23%
where the time goes in v5:
time: 282 us; the launch traced here: 279 us
  Pallas kernels  89.1 us (32%)
  starting transfers between devices  85.2 us (30%)
  waiting for transfers between devices  69.2 us (25%)
  blocking collectives  30 us (11%)
  local copies, waits for them, and re-layouts  4.43 us (2%)
    all_to_all x7, starting transfers between devices, exchange(): return lax.all_to_all(values, axes, split_axis=0, concat_axis=0, tiled=True)  50 us
    ppermute x16, waiting for transfers between devices, shift(): lax.ppermute(value, 'dp', [(i, (i + step) % copies) for i in range(copies)])  40.1 us
    all_to_all x1, blocking collectives, exchange(): return lax.all_to_all(values, axes, split_axis=0, concat_axis=0, tiled=True)  30 us
    ppermute x16, starting transfers between devices, shift(): lax.ppermute(value, 'dp', [(i, (i + step) % copies) for i in range(copies)])  25.4 us
    pallas_call x2, Pallas kernels, dispatch(): pl.pallas_call(body, grid_spec=pltpu.PrefetchScalarGridSpec(num_scalar_pr...  20.2 us
    pallas_call x2, Pallas kernels, mix(): pl.pallas_call(body, grid_spec=pltpu.PrefetchScalarGridSpec(num_scalar_pr...  19.2 us
    pallas_call x2, Pallas kernels, second_terms(): pl.pallas_call(body, grid_spec=pltpu.PrefetchScalarGridSpec(num_scalar_pr...  17.6 us
    all_to_all x7, waiting for transfers between devices, exchange(): return lax.all_to_all(values, axes, split_axis=0, concat_axis=0, tiled=True)  15.5 us
  transfers between devices with their start and end apart: 32, of which 14 were waited for; matrix products, arithmetic and copies ran while one was open for 1% of the time, Pallas kernels for 23%

profile of v5, /device:TPU:6, one launch (start us, length us, event | category | flops | bytes accessed | tf_op | source)
XLA Modules:
  0.0 278.8 jit_solution(16651877309042327555)
XLA Ops:
  2.8 7.4 %all-to-all-start = ((bf16[16,112,256]{2,1,0:T(8,128)(2,1)}), bf16[16,112,256]{2,1,0:T(8,128)(2,1)S(1)}, u32[]{:S(2)}, u32[]{:S(2)}) async-start(bf16[16,112,256]{2,1,0:T(8,128)(2,1)} %bitcast.32), calls=%async_computation | async-start | bytes 1835008 | tf_op jit(solution)/shard_map/all_to_all | solution.py:525
  10.2 4.0 %prepare.1 = bf16[16,480,128]{2,1,0:T(8,128)(2,1)} custom-call(s32[8,128]{1,0:T(8,128)} %bitcast.35, f32[8,128]{1,0:T(8,128)} %bitcast.36, bf16[128,7168]{1,0:T(8,128)(2,1)} %bitcast.34), custom_call_target="tpu_custom_call" | custom-call | tf_op jit(solution)/shard_map/prepare/pallas_call | solution.py:91
  14.2 9.1 %all-to-all-done.refs_3_ = bf16[16,112,256]{2,1,0:T(8,128)(2,1)S(1)} async-done(((bf16[16,112,256]{2,1,0:T(8,128)(2,1)}), bf16[16,112,256]{2,1,0:T(8,128)(2,1)S(1)}, u32[]{:S(2)}, u32[]{:S(2)}) %all-to-all-start) | async-done | bytes 917536 | tf_op jit(solution)/shard_map/all_to_all | solution.py:525
  23.3 30.0 %all_to_all.40.refs_1_ = bf16[16,480,128]{2,1,0:T(8,128)(2,1)S(1)} all-to-all(bf16[16,480,128]{2,1,0:T(8,128)(2,1)} %prepare.1), channel_id=1, replica_groups=mesh['chip'=16,'core'=2,'dp'=4] {'chip'}, dimensions={0} | all-to-all | bytes 3932160 | tf_op jit(solution)/shard_map/all_to_all | solution.py:525
  57.3 21.0 %collective-permute-done.2.refs_6_ = bf16[16,112,256]{2,1,0:T(8,128)(2,1)S(1)} collective-permute-done((bf16[16,112,256]{2,1,0:T(8,128)(2,1)S(1)}, bf16[16,112,256]{2,1,0:T(8,128)(2,1)S(1)}, u32[]{:S(2)}, u32[]{:S(2)}) %collective-permute-start.2) | collective-permute-done | bytes 917536 | tf_op jit(solution)/shard_map/ppermute | solution.py:529
  83.6 9.4 %collective-permute-done.3 = bf16[8,112,256]{2,1,0:T(8,128)(2,1)S(1)} collective-permute-done((bf16[8,112,256]{2,1,0:T(8,128)(2,1)}, bf16[8,112,256]{2,1,0:T(8,128)(2,1)S(1)}, u32[]{:S(2)}, u32[]{:S(2)}) %collective-permute-start.3) | collective-permute-done | bytes 458784 | tf_op jit(solution)/shard_map/ppermute | solution.py:529
  94.5 9.3 %shard_map.68 = bf16[128,128,448]{2,1,0:T(8,128)(2,1)} custom-call(s32[1]{0:T(128)} %bitcast.1.refs_0_, bf16[16,480,128]{2,1,0:T(8,128)(2,1)S(1)} %all_to_all.40.refs_1_), custom_call_target="tpu_custom_call" | custom-call | flops 1879048192 | bytes 14680064 | tf_op jit(solution)/shard_map/pallas_call | solution.py:152
  103.8 10.9 %shard_map.69 = bf16[128,128,448]{2,1,0:T(8,128)(2,1)} custom-call(s32[1]{0:T(128)} %bitcast.1.refs_0_, bf16[16,480,128]{2,1,0:T(8,128)(2,1)} %collective-permute-done.refs_1_), custom_call_target="tpu_custom_call" | custom-call | flops 1879048192 | bytes 14680064 | tf_op jit(solution)/shard_map/pallas_call | solution.py:152
  114.7 9.6 %shard_map.73 = bf16[16,6,2,16,128]{4,3,2,1,0:T(8,128)(2,1)} custom-call(s32[2]{0:T(128)S(1)} %pad_add_fusion.refs_0_, bf16[16,8,128,448]{3,2,1,0:T(8,128)(2,1)} %bitcast.19, bf16[16,8,128,448]{3,2,1,0:T(8,128)(2,1)} %bitcast.23, bf16[16,112,256]{2,1,0:T(8,128)(2,1)S(1)} %all-to-all-done.refs_3_, bf16[16,112,256]{2,1,0:T(8,128)(2,1)S(1)} %copy-done.4, ...), custom_call_target="tpu_custom_call" | custom-call | flops 3758096384 | bytes 14680064 | tf_op jit(solution)/shard_map/pallas_call | solution.py:233
  124.3 6.6 %all-to-all-start.3 = ((bf16[16,6,2,16,128]{4,3,2,1,0:T(8,128)(2,1)}), bf16[16,6,2,16,128]{4,3,2,1,0:T(8,128)(2,1)S(1)}, u32[]{:S(2)}, u32[]{:S(2)}) async-start(bf16[16,6,2,16,128]{4,3,2,1,0:T(8,128)(2,1)} %shard_map.73), calls=%async_computation.3 | async-start | bytes 1572864 | tf_op jit(solution)/shard_map/all_to_all | solution.py:525
  132.1 9.6 %shard_map.70 = bf16[16,6,2,16,128]{4,3,2,1,0:T(8,128)(2,1)} custom-call(s32[2]{0:T(128)S(1)} %pad_add_fusion.refs_0_, bf16[16,8,128,448]{3,2,1,0:T(8,128)(2,1)} %bitcast.20, bf16[16,8,128,448]{3,2,1,0:T(8,128)(2,1)} %bitcast.24, bf16[16,112,256]{2,1,0:T(8,128)(2,1)S(1)} %all-to-all-done.refs_3_, bf16[16,112,256]{2,1,0:T(8,128)(2,1)S(1)} %copy-done.5, ...), custom_call_target="tpu_custom_call" | custom-call | flops 3758096384 | bytes 14680064 | tf_op jit(solution)/shard_map/pallas_call | solution.py:233
  142.0 7.1 %all-to-all-start.2 = ((bf16[16,6,2,16,128]{4,3,2,1,0:T(8,128)(2,1)}), bf16[16,6,2,16,128]{4,3,2,1,0:T(8,128)(2,1)S(1)}, u32[]{:S(2)}, u32[]{:S(2)}) async-start(bf16[16,6,2,16,128]{4,3,2,1,0:T(8,128)(2,1)} %shard_map.70), calls=%async_computation.2 | async-start | bytes 1572864 | tf_op jit(solution)/shard_map/all_to_all | solution.py:525
  152.4 4.6 %collective-permute-start.12 = (bf16[32,2048]{1,0:T(8,128)(2,1)S(1)}, bf16[32,2048]{1,0:T(8,128)(2,1)S(1)}, u32[]{:S(2)}, u32[]{:S(2)}) collective-permute-start(bf16[32,2048]{1,0:T(8,128)(2,1)S(1)} %get-tuple-element.40), channel_id=1, source_target_pairs={{0,2},{1,3},{2,0},{3,1},{4,6},{5,7},{6,4},{7,5},{8,10},{9,11},{10,... | collective-permute-start | bytes 393224 | tf_op jit(solution)/shard_map/ppermute | solution.py:529
  177.4 3.8 %shard_map.76 = (f32[8,32,2048]{2,1,0:T(8,128)}, bf16[16,6,2,16,128]{4,3,2,1,0:T(8,128)(2,1)}) custom-call(s32[1]{0:T(128)} %bitcast.copy_ref.refs_0_, bf16[32,2048]{1,0:T(8,128)(2,1)S(1)} %shard_map.75.refs_1_, bf16[32,2048]{1,0:T(8,128)(2,1)S(1)} %collective-permute-done.14.refs_2_, bf16[32,2048]{1,0:T(8,128)(2,1)S(1)} %collective-permute-done.15.refs_3_, ...), custom_call_target="tpu_custom_call" | custom-call | flops 805306368 | bytes 3145728 | tf_op jit(solution)/shard_map/pallas_call | solution.py:387
  181.2 7.2 %all-to-all-start.6 = ((bf16[16,6,2,16,128]{4,3,2,1,0:T(8,128)(2,1)}), bf16[16,6,2,16,128]{4,3,2,1,0:T(8,128)(2,1)S(1)}, u32[]{:S(2)}, u32[]{:S(2)}) async-start(bf16[16,6,2,16,128]{4,3,2,1,0:T(8,128)(2,1)} %get-tuple-element.53), calls=%async_computation.6 | async-start | bytes 1572864 | tf_op jit(solution)/shard_map/all_to_all | solution.py:525
  200.7 3.8 %shard_map.77 = (f32[8,32,2048]{2,1,0:T(8,128)}, bf16[16,6,2,16,128]{4,3,2,1,0:T(8,128)(2,1)}) custom-call(s32[1]{0:T(128)} %bitcast.copy_ref.refs_0_, bf16[32,2048]{1,0:T(8,128)(2,1)S(1)} %shard_map.72.refs_1_, bf16[32,2048]{1,0:T(8,128)(2,1)S(1)} %collective-permute-done.8.refs_2_, ...), custom_call_target="tpu_custom_call", output_to_operand_aliasing={{0}: (6, {})} | custom-call | flops 805306368 | bytes 3145728 | tf_op jit(solution)/shard_map/pallas_call | solution.py:387
  204.5 7.2 %all-to-all-start.4 = ((bf16[16,6,2,16,128]{4,3,2,1,0:T(8,128)(2,1)}), bf16[16,6,2,16,128]{4,3,2,1,0:T(8,128)(2,1)S(1)}, u32[]{:S(2)}, u32[]{:S(2)}) async-start(bf16[16,6,2,16,128]{4,3,2,1,0:T(8,128)(2,1)} %get-tuple-element.44), calls=%async_computation.4 | async-start | bytes 1572864 | tf_op jit(solution)/shard_map/all_to_all | solution.py:525
  211.7 8.8 %shard_map.81 = (bf16[2,8,112,128]{3,2,1,0:T(8,128)(2,1)}, bf16[2,8,112,128]{3,2,1,0:T(8,128)(2,1)S(1)}, bf16[2,8,112,128]{3,2,1,0:T(8,128)(2,1)}, bf16[2,8,112,128]{3,2,1,0:T(8,128)(2,1)S(1)}) custom-call(s32[2]{0:T(128)S(1)} %pad_add_fusion.refs_0_, bf16[16,8,128,448]{3,2,1,0:T(8,128)(2,1)} %bitcast.21, bf16[16,8,128,448]{3,2,1,0:T(8,128)(2,1)} %bitcast.25, ...), custom_call_target="tpu_custom_call" | custom-call | flops 3758096384 | bytes 14680064 | tf_op jit(solution)/shard_map/pallas_call | solution.py:470
  223.4 8.8 %shard_map.78 = (bf16[2,8,112,128]{3,2,1,0:T(8,128)(2,1)}, bf16[2,8,112,128]{3,2,1,0:T(8,128)(2,1)S(1)}, bf16[2,8,112,128]{3,2,1,0:T(8,128)(2,1)}, bf16[2,8,112,128]{3,2,1,0:T(8,128)(2,1)S(1)}) custom-call(s32[2]{0:T(128)S(1)} %pad_add_fusion.refs_0_, bf16[16,8,128,448]{3,2,1,0:T(8,128)(2,1)} %bitcast.22, bf16[16,8,128,448]{3,2,1,0:T(8,128)(2,1)} %bitcast.26, ...), custom_call_target="tpu_custom_call" | custom-call | flops 3758096384 | bytes 14680064 | tf_op jit(solution)/shard_map/pallas_call | solution.py:470
  238.5 7.7 %collective-permute-done.23.low_got_ref = bf16[8,112,128]{2,1,0:T(8,128)(2,1)S(1)} collective-permute-done((bf16[8,112,128]{2,1,0:T(8,128)(2,1)S(1)}, bf16[8,112,128]{2,1,0:T(8,128)(2,1)S(1)}, u32[]{:S(2)}, u32[]{:S(2)}) %collective-permute-start.23) | collective-permute-done | bytes 229408 | tf_op jit(solution)/shard_map/ppermute | solution.py:554
  247.0 7.2 %all-to-all-start.7 = ((bf16[16,112,128]{2,1,0:T(8,128)(2,1)}), bf16[16,112,128]{2,1,0:T(8,128)(2,1)S(1)}, u32[]{:S(2)}, u32[]{:S(2)}) async-start(bf16[16,112,128]{2,1,0:T(8,128)(2,1)} %shard_map.83), calls=%async_computation.7 | async-start | bytes 917504 | tf_op jit(solution)/shard_map/all_to_all | solution.py:525
  256.6 5.2 %collective-permute-done.19.low_got_ref = bf16[8,112,128]{2,1,0:T(8,128)(2,1)S(1)} collective-permute-done((bf16[8,112,128]{2,1,0:T(8,128)(2,1)S(1)}, bf16[8,112,128]{2,1,0:T(8,128)(2,1)S(1)}, u32[]{:S(2)}, u32[]{:S(2)}) %collective-permute-start.19) | collective-permute-done | bytes 229408 | tf_op jit(solution)/shard_map/ppermute | solution.py:554
  263.4 7.2 %all-to-all-start.5 = ((bf16[16,112,128]{2,1,0:T(8,128)(2,1)}), bf16[16,112,128]{2,1,0:T(8,128)(2,1)S(1)}, u32[]{:S(2)}, u32[]{:S(2)}) async-start(bf16[16,112,128]{2,1,0:T(8,128)(2,1)} %shard_map.80), calls=%async_computation.5 | async-start | bytes 917504 | tf_op jit(solution)/shard_map/all_to_all | solution.py:525
  271.7 6.1 %all-to-all-done.5 = bf16[16,112,128]{2,1,0:T(8,128)(2,1)S(1)} async-done(((bf16[16,112,128]{2,1,0:T(8,128)(2,1)}), bf16[16,112,128]{2,1,0:T(8,128)(2,1)S(1)}, u32[]{:S(2)}, u32[]{:S(2)}) %all-to-all-start.5) | async-done | bytes 458784 | tf_op jit(solution)/shard_map/all_to_all | solution.py:525
  (82 shorter events, 66.2 us)
Async XLA Ops:
  2.8 20.5 %all-to-all-start = ((bf16[16,112,256]{2,1,0:T(8,128)(2,1)}), bf16[16,112,256]{2,1,0:T(8,128)(2,1)S(1)}, u32[]{:S(2)}, u32[]{:S(2)}) async-start(bf16[16,112,256]{2,1,0:T(8,128)(2,1)} %bitcast.32), calls=%async_computation | async-start | bytes 1835008 | tf_op jit(solution)/shard_map/all_to_all | solution.py:525
  53.3 50.5 %collective-permute-start = (bf16[16,480,128]{2,1,0:T(8,128)(2,1)S(1)}, bf16[16,480,128]{2,1,0:T(8,128)(2,1)}, u32[]{:S(2)}, u32[]{:S(2)}) collective-permute-start(bf16[16,480,128]{2,1,0:T(8,128)(2,1)S(1)} %all_to_all.40.refs_1_), channel_id=1, source_target_pairs={{0,4},{4,0},{1,5},{5,1},{2,6},{6,2},{3,7},{7,3},{8,12},{12,8},{9,1... | collective-permute-start | bytes 5898248 | tf_op jit(solution)/shard_map/ppermute | solution.py:586
  53.3 25.1 %collective-permute-start.2 = (bf16[16,112,256]{2,1,0:T(8,128)(2,1)S(1)}, bf16[16,112,256]{2,1,0:T(8,128)(2,1)S(1)}, u32[]{:S(2)}, u32[]{:S(2)}) collective-permute-start(bf16[16,112,256]{2,1,0:T(8,128)(2,1)S(1)} %all-to-all-done.refs_3_), channel_id=1, source_target_pairs={{0,1},{1,2},{2,3},{3,0},{4,5},{5,6},{6,7},{7,4},{8,9},{9,10},{10,1... | collective-permute-start | bytes 2752520 | tf_op jit(solution)/shard_map/ppermute | solution.py:529
  55.2 24.0 %collective-permute-start.1 = (bf16[16,112,256]{2,1,0:T(8,128)(2,1)S(1)}, bf16[16,112,256]{2,1,0:T(8,128)(2,1)S(1)}, u32[]{:S(2)}, u32[]{:S(2)}) collective-permute-start(bf16[16,112,256]{2,1,0:T(8,128)(2,1)S(1)} %all-to-all-done.refs_3_), channel_id=1, source_target_pairs={{0,3},{1,0},{2,1},{3,2},{4,7},{5,4},{6,5},{7,6},{8,11},{9,8},{10,9... | collective-permute-start | bytes 2752520 | tf_op jit(solution)/shard_map/ppermute | solution.py:529
  79.2 13.8 %collective-permute-start.3 = (bf16[8,112,256]{2,1,0:T(8,128)(2,1)}, bf16[8,112,256]{2,1,0:T(8,128)(2,1)S(1)}, u32[]{:S(2)}, u32[]{:S(2)}) collective-permute-start(bf16[8,112,256]{2,1,0:T(8,128)(2,1)} %slice.8), channel_id=1, source_target_pairs={{0,1},{1,2},{2,3},{3,0},{4,5},{5,6},{6,7},{7,4},{8,9},{9,10},{10,1... | collective-permute-start | bytes 1376264 | tf_op jit(solution)/shard_map/ppermute | solution.py:529
  80.5 12.9 %collective-permute-start.4 = (bf16[8,112,256]{2,1,0:T(8,128)(2,1)}, bf16[8,112,256]{2,1,0:T(8,128)(2,1)}, u32[]{:S(2)}, u32[]{:S(2)}) collective-permute-start(bf16[8,112,256]{2,1,0:T(8,128)(2,1)} %slice.9), channel_id=1, source_target_pairs={{0,3},{1,0},{2,1},{3,2},{4,7},{5,4},{6,5},{7,6},{8,11},{9,8},{10,9... | collective-permute-start | bytes 1376264 | tf_op jit(solution)/shard_map/ppermute | solution.py:529
  124.3 17.6 %all-to-all-start.3 = ((bf16[16,6,2,16,128]{4,3,2,1,0:T(8,128)(2,1)}), bf16[16,6,2,16,128]{4,3,2,1,0:T(8,128)(2,1)S(1)}, u32[]{:S(2)}, u32[]{:S(2)}) async-start(bf16[16,6,2,16,128]{4,3,2,1,0:T(8,128)(2,1)} %shard_map.73), calls=%async_computation.3 | async-start | bytes 1572864 | tf_op jit(solution)/shard_map/all_to_all | solution.py:525
  142.0 27.9 %all-to-all-start.2 = ((bf16[16,6,2,16,128]{4,3,2,1,0:T(8,128)(2,1)}), bf16[16,6,2,16,128]{4,3,2,1,0:T(8,128)(2,1)S(1)}, u32[]{:S(2)}, u32[]{:S(2)}) async-start(bf16[16,6,2,16,128]{4,3,2,1,0:T(8,128)(2,1)} %shard_map.70), calls=%async_computation.2 | async-start | bytes 1572864 | tf_op jit(solution)/shard_map/all_to_all | solution.py:525
  152.4 9.0 %collective-permute-start.12 = (bf16[32,2048]{1,0:T(8,128)(2,1)S(1)}, bf16[32,2048]{1,0:T(8,128)(2,1)S(1)}, u32[]{:S(2)}, u32[]{:S(2)}) collective-permute-start(bf16[32,2048]{1,0:T(8,128)(2,1)S(1)} %get-tuple-element.40), channel_id=1, source_target_pairs={{0,2},{1,3},{2,0},{3,1},{4,6},{5,7},{6,4},{7,5},{8,10},{9,11},{10,... | collective-permute-start | bytes 393224 | tf_op jit(solution)/shard_map/ppermute | solution.py:529
  165.7 9.1 %collective-permute-start.14 = (bf16[32,2048]{1,0:T(8,128)(2,1)S(1)}, bf16[32,2048]{1,0:T(8,128)(2,1)S(1)}, u32[]{:S(2)}, u32[]{:S(2)}) collective-permute-start(bf16[32,2048]{1,0:T(8,128)(2,1)S(1)} %shard_map.75.refs_1_), channel_id=1, source_target_pairs={{0,1},{1,2},{2,3},{3,0},{4,5},{5,6},{6,7},{7,4},{8,9},{9,10},{10,1... | collective-permute-start | bytes 393224 | tf_op jit(solution)/shard_map/ppermute | solution.py:529
  165.8 11.6 %collective-permute-start.15 = (bf16[32,2048]{1,0:T(8,128)(2,1)S(1)}, bf16[32,2048]{1,0:T(8,128)(2,1)S(1)}, u32[]{:S(2)}, u32[]{:S(2)}) collective-permute-start(bf16[32,2048]{1,0:T(8,128)(2,1)S(1)} %shard_map.75.refs_1_), channel_id=1, source_target_pairs={{0,2},{1,3},{2,0},{3,1},{4,6},{5,7},{6,4},{7,5},{8,10},{9,11},{10,... | collective-permute-start | bytes 393224 | tf_op jit(solution)/shard_map/ppermute | solution.py:529
  169.1 8.3 %collective-permute-start.16 = (bf16[32,2048]{1,0:T(8,128)(2,1)S(1)}, bf16[32,2048]{1,0:T(8,128)(2,1)S(1)}, u32[]{:S(2)}, u32[]{:S(2)}) collective-permute-start(bf16[32,2048]{1,0:T(8,128)(2,1)S(1)} %shard_map.75.refs_1_), channel_id=1, source_target_pairs={{0,3},{1,0},{2,1},{3,2},{4,7},{5,4},{6,5},{7,6},{8,11},{9,8},{10,9... | collective-permute-start | bytes 393224 | tf_op jit(solution)/shard_map/ppermute | solution.py:529
  172.6 15.8 %collective-permute-start.5 = (bf16[32,2048]{1,0:T(8,128)(2,1)S(1)}, bf16[32,2048]{1,0:T(8,128)(2,1)S(1)}, u32[]{:S(2)}, u32[]{:S(2)}) collective-permute-start(bf16[32,2048]{1,0:T(8,128)(2,1)S(1)} %get-tuple-element.35), channel_id=1, source_target_pairs={{0,1},{1,2},{2,3},{3,0},{4,5},{5,6},{6,7},{7,4},{8,9},{9,10},{10,1... | collective-permute-start | bytes 393224 | tf_op jit(solution)/shard_map/ppermute | solution.py:529
  174.0 14.5 %collective-permute-start.6 = (bf16[32,2048]{1,0:T(8,128)(2,1)S(1)}, bf16[32,2048]{1,0:T(8,128)(2,1)S(1)}, u32[]{:S(2)}, u32[]{:S(2)}) collective-permute-start(bf16[32,2048]{1,0:T(8,128)(2,1)S(1)} %get-tuple-element.36), channel_id=1, source_target_pairs={{0,2},{1,3},{2,0},{3,1},{4,6},{5,7},{6,4},{7,5},{8,10},{9,11},{10,... | collective-permute-start | bytes 393224 | tf_op jit(solution)/shard_map/ppermute | solution.py:529
  174.8 13.6 %collective-permute-start.7 = (bf16[32,2048]{1,0:T(8,128)(2,1)S(1)}, bf16[32,2048]{1,0:T(8,128)(2,1)S(1)}, u32[]{:S(2)}, u32[]{:S(2)}) collective-permute-start(bf16[32,2048]{1,0:T(8,128)(2,1)S(1)} %get-tuple-element.37), channel_id=1, source_target_pairs={{0,3},{1,0},{2,1},{3,2},{4,7},{5,4},{6,5},{7,6},{8,11},{9,8},{10,9... | collective-permute-start | bytes 393224 | tf_op jit(solution)/shard_map/ppermute | solution.py:529
  181.2 23.3 %all-to-all-start.6 = ((bf16[16,6,2,16,128]{4,3,2,1,0:T(8,128)(2,1)}), bf16[16,6,2,16,128]{4,3,2,1,0:T(8,128)(2,1)S(1)}, u32[]{:S(2)}, u32[]{:S(2)}) async-start(bf16[16,6,2,16,128]{4,3,2,1,0:T(8,128)(2,1)} %get-tuple-element.53), calls=%async_computation.6 | async-start | bytes 1572864 | tf_op jit(solution)/shard_map/all_to_all | solution.py:525
  204.5 18.9 %all-to-all-start.4 = ((bf16[16,6,2,16,128]{4,3,2,1,0:T(8,128)(2,1)}), bf16[16,6,2,16,128]{4,3,2,1,0:T(8,128)(2,1)S(1)}, u32[]{:S(2)}, u32[]{:S(2)}) async-start(bf16[16,6,2,16,128]{4,3,2,1,0:T(8,128)(2,1)} %get-tuple-element.44), calls=%async_computation.4 | async-start | bytes 1572864 | tf_op jit(solution)/shard_map/all_to_all | solution.py:525
  220.6 13.7 %collective-permute-start.21 = (bf16[2,8,112,128]{3,2,1,0:T(8,128)(2,1)}, bf16[2,8,112,128]{3,2,1,0:T(8,128)(2,1)S(1)}, u32[]{:S(2)}, u32[]{:S(2)}) collective-permute-start(bf16[2,8,112,128]{3,2,1,0:T(8,128)(2,1)} %get-tuple-element.55), channel_id=1, source_target_pairs={{0,1},{1,0},{2,3},{3,2},{4,5},{5,4},{6,7},{7,6},{8,9},{9,8},{10,11... | collective-permute-start | bytes 1376264 | tf_op jit(solution)/shard_map/ppermute | solution.py:549
  221.5 12.7 %collective-permute-start.22 = (bf16[2,8,112,128]{3,2,1,0:T(8,128)(2,1)}, bf16[2,8,112,128]{3,2,1,0:T(8,128)(2,1)}, u32[]{:S(2)}, u32[]{:S(2)}) collective-permute-start(bf16[2,8,112,128]{3,2,1,0:T(8,128)(2,1)} %get-tuple-element.57), channel_id=1, source_target_pairs={{0,3},{1,2},{2,1},{3,0},{4,7},{5,6},{6,5},{7,4},{8,11},{9,10},{10,... | collective-permute-start | bytes 1376264 | tf_op jit(solution)/shard_map/ppermute | solution.py:550
  232.2 22.0 %collective-permute-start.17 = (bf16[2,8,112,128]{3,2,1,0:T(8,128)(2,1)}, bf16[2,8,112,128]{3,2,1,0:T(8,128)(2,1)S(1)}, u32[]{:S(2)}, u32[]{:S(2)}) collective-permute-start(bf16[2,8,112,128]{3,2,1,0:T(8,128)(2,1)} %get-tuple-element.46), channel_id=1, source_target_pairs={{0,1},{1,0},{2,3},{3,2},{4,5},{5,4},{6,7},{7,6},{8,9},{9,8},{10,11... | collective-permute-start | bytes 1376264 | tf_op jit(solution)/shard_map/ppermute | solution.py:549
  233.6 20.6 %collective-permute-start.18 = (bf16[2,8,112,128]{3,2,1,0:T(8,128)(2,1)}, bf16[2,8,112,128]{3,2,1,0:T(8,128)(2,1)S(1)}, u32[]{:S(2)}, u32[]{:S(2)}) collective-permute-start(bf16[2,8,112,128]{3,2,1,0:T(8,128)(2,1)} %get-tuple-element.48), channel_id=1, source_target_pairs={{0,3},{1,2},{2,1},{3,0},{4,7},{5,6},{6,5},{7,4},{8,11},{9,10},{10,... | collective-permute-start | bytes 1376264 | tf_op jit(solution)/shard_map/ppermute | solution.py:550
  235.5 10.7 %collective-permute-start.23 = (bf16[8,112,128]{2,1,0:T(8,128)(2,1)S(1)}, bf16[8,112,128]{2,1,0:T(8,128)(2,1)S(1)}, u32[]{:S(2)}, u32[]{:S(2)}) collective-permute-start(bf16[8,112,128]{2,1,0:T(8,128)(2,1)S(1)} %get-tuple-element.59), channel_id=1, source_target_pairs={{0,3},{1,2},{2,1},{3,0},{4,7},{5,6},{6,5},{7,4},{8,11},{9,10},{10,... | collective-permute-start | bytes 688136 | tf_op jit(solution)/shard_map/ppermute | solution.py:554
  247.0 16.3 %all-to-all-start.7 = ((bf16[16,112,128]{2,1,0:T(8,128)(2,1)}), bf16[16,112,128]{2,1,0:T(8,128)(2,1)S(1)}, u32[]{:S(2)}, u32[]{:S(2)}) async-start(bf16[16,112,128]{2,1,0:T(8,128)(2,1)} %shard_map.83), calls=%async_computation.7 | async-start | bytes 917504 | tf_op jit(solution)/shard_map/all_to_all | solution.py:525
  263.4 14.4 %all-to-all-start.5 = ((bf16[16,112,128]{2,1,0:T(8,128)(2,1)}), bf16[16,112,128]{2,1,0:T(8,128)(2,1)S(1)}, u32[]{:S(2)}, u32[]{:S(2)}) async-start(bf16[16,112,128]{2,1,0:T(8,128)(2,1)} %shard_map.80), calls=%async_computation.5 | async-start | bytes 917504 | tf_op jit(solution)/shard_map/all_to_all | solution.py:525
  (16 other events, 123.1 us)

commit v6 on v5

--- a/solution.py
+++ b/solution.py
@@ -16,7 +16,10 @@
 CP = 8
 CAP = 6
 STREAMS = 2
-STEP = 2
+BLOCKS = 4
+GROUP = 32
+MIX_STEP = 4
+TERMS_STEP = 2
 AHEAD = 3
 
 
@@ -122,16 +125,17 @@
 def dispatch_kernel(core_ref, xt_ref, out_ref):
     core = core_ref[0]
     token = lax.broadcasted_iota(jnp.int32, (CP, 128), 1).astype(F32)
-    group = 32
+    group = GROUP
+    count = xt_ref.shape[0]
     width = out_ref.shape[2]
     start = pl.multiple_of(width + 2 * CP * core, 2 * CP)
     codes = []
-    for i in range(2):
+    for i in range(count):
         table = xt_ref[i, pl.ds(start, 2 * CP), :].astype(F32)
         codes.append(table[:CP] + table[CP:])
     for g in range(128 // group):
         rows = []
-        for i in range(2):
+        for i in range(count):
             parts = []
             for x in range(g * group, (g + 1) * group):
                 u = codes[i][:, x : x + 1] - token
@@ -153,9 +157,9 @@
         body,
         grid_spec=pltpu.PrefetchScalarGridSpec(
             num_scalar_prefetch=1,
-            grid=(chips // 2,),
-            in_specs=[pl.BlockSpec((2, total, tokens), lambda i, _: (i, 0, 0))],
-            out_specs=pl.BlockSpec((128, 2 * CP, width), lambda i, _: (0, i, 0)),
+            grid=(chips // BLOCKS,),
+            in_specs=[pl.BlockSpec((BLOCKS, total, tokens), lambda i, _: (i, 0, 0))],
+            out_specs=pl.BlockSpec((128, BLOCKS * CP, width), lambda i, _: (0, i, 0)),
         ),
         out_shape=shape_of((128, chips * CP, width), BF16),
         compiler_params=params(),
@@ -203,7 +207,7 @@
         part = q_refs[0].shape[1]
         for shift, ref in enumerate(q_refs):
             start = pl.multiple_of(part * ((copy + shift) % copies), 16)
-            q_ref[pl.ds(start, part), :] = ref[n]
+            q_ref[pl.ds(start, part), :] = ref[n, :, stream * lanes : (stream + 1) * lanes]
         for half, ref in enumerate((own_ref, sib_ref)):
             _, experts, rows, width = ref.shape
             got = lax.dot_general(
@@ -223,13 +227,13 @@
     lanes = lanes // STREAMS
     _, experts, rows, width = own.shape
     experts = experts // STREAMS
-    step = STEP
+    step = MIX_STEP
     block = pl.BlockSpec(memory_space=pl.ANY)
 
     def body(*refs):
         mix_kernel(*refs, stream=stream)
 
-    q_block = pl.BlockSpec((step, part, lanes), lambda i, _: (i, 0, stream))
+    q_block = pl.BlockSpec((step, part, lanes * STREAMS), lambda i, _: (i, 0, 0))
     return pl.pallas_call(
         body,
         grid_spec=pltpu.PrefetchScalarGridSpec(
@@ -460,7 +464,7 @@
     chips, _, _, _, lanes = proj.shape
     _, experts, rows, width = own.shape
     experts = experts // STREAMS
-    step = STEP
+    step = TERMS_STEP
     half = chips // step // 2
     block = pl.BlockSpec(memory_space=pl.ANY)
 

time: 282 us -> 278 us (0.986)
  Pallas kernels: 89.1 us -> 85 us
where the time goes in v6:
time: 278 us; the launch traced here: 275 us
  Pallas kernels  85 us (31%)
  starting transfers between devices  84.8 us (31%)
  waiting for transfers between devices  69.8 us (25%)
  blocking collectives  30 us (11%)
  local copies, waits for them, and re-layouts  4.43 us (2%)
    all_to_all x7, starting transfers between devices, exchange(): return lax.all_to_all(values, axes, split_axis=0, concat_axis=0, tiled=True)  49.3 us
    ppermute x16, waiting for transfers between devices, shift(): lax.ppermute(value, 'dp', [(i, (i + step) % copies) for i in range(copies)])  40.1 us
    all_to_all x1, blocking collectives, exchange(): return lax.all_to_all(values, axes, split_axis=0, concat_axis=0, tiled=True)  30 us
    ppermute x16, starting transfers between devices, shift(): lax.ppermute(value, 'dp', [(i, (i + step) % copies) for i in range(copies)])  25.5 us
    pallas_call x2, Pallas kernels, mix(): pl.pallas_call(body, grid_spec=pltpu.PrefetchScalarGridSpec(num_scalar_pr...  17.9 us
    pallas_call x2, Pallas kernels, second_terms(): pl.pallas_call(body, grid_spec=pltpu.PrefetchScalarGridSpec(num_scalar_pr...  17.6 us
    pallas_call x2, Pallas kernels, dispatch(): pl.pallas_call(body, grid_spec=pltpu.PrefetchScalarGridSpec(num_scalar_pr...  17.4 us
    all_to_all x7, waiting for transfers between devices, exchange(): return lax.all_to_all(values, axes, split_axis=0, concat_axis=0, tiled=True)  16.1 us
  transfers between devices with their start and end apart: 32, of which 14 were waited for; matrix products, arithmetic and copies ran while one was open for 1% of the time, Pallas kernels for 23%

profile of v6, /device:TPU:6, one launch (start us, length us, event | category | flops | bytes accessed | tf_op | source)
XLA Modules:
  0.0 274.9 jit_solution(3750265072103077114)
XLA Ops:
  2.8 7.4 %all-to-all-start = ((bf16[16,112,256]{2,1,0:T(8,128)(2,1)}), bf16[16,112,256]{2,1,0:T(8,128)(2,1)S(1)}, u32[]{:S(2)}, u32[]{:S(2)}) async-start(bf16[16,112,256]{2,1,0:T(8,128)(2,1)} %bitcast.32), calls=%async_computation | async-start | bytes 1835008 | tf_op jit(solution)/shard_map/all_to_all | solution.py:529
  10.2 4.0 %prepare.1 = bf16[16,480,128]{2,1,0:T(8,128)(2,1)} custom-call(s32[8,128]{1,0:T(8,128)} %bitcast.35, f32[8,128]{1,0:T(8,128)} %bitcast.36, bf16[128,7168]{1,0:T(8,128)(2,1)} %bitcast.34), custom_call_target="tpu_custom_call" | custom-call | tf_op jit(solution)/shard_map/prepare/pallas_call | solution.py:94
  14.2 9.1 %all-to-all-done.refs_3_ = bf16[16,112,256]{2,1,0:T(8,128)(2,1)S(1)} async-done(((bf16[16,112,256]{2,1,0:T(8,128)(2,1)}), bf16[16,112,256]{2,1,0:T(8,128)(2,1)S(1)}, u32[]{:S(2)}, u32[]{:S(2)}) %all-to-all-start) | async-done | bytes 917536 | tf_op jit(solution)/shard_map/all_to_all | solution.py:529
  23.3 30.0 %all_to_all.40.refs_1_ = bf16[16,480,128]{2,1,0:T(8,128)(2,1)S(1)} all-to-all(bf16[16,480,128]{2,1,0:T(8,128)(2,1)} %prepare.1), channel_id=1, replica_groups=mesh['chip'=16,'core'=2,'dp'=4] {'chip'}, dimensions={0} | all-to-all | bytes 3932160 | tf_op jit(solution)/shard_map/all_to_all | solution.py:529
  57.3 21.0 %collective-permute-done.2.refs_6_ = bf16[16,112,256]{2,1,0:T(8,128)(2,1)S(1)} collective-permute-done((bf16[16,112,256]{2,1,0:T(8,128)(2,1)S(1)}, bf16[16,112,256]{2,1,0:T(8,128)(2,1)S(1)}, u32[]{:S(2)}, u32[]{:S(2)}) %collective-permute-start.2) | collective-permute-done | bytes 917536 | tf_op jit(solution)/shard_map/ppermute | solution.py:533
  83.6 9.4 %collective-permute-done.3 = bf16[8,112,256]{2,1,0:T(8,128)(2,1)S(1)} collective-permute-done((bf16[8,112,256]{2,1,0:T(8,128)(2,1)}, bf16[8,112,256]{2,1,0:T(8,128)(2,1)S(1)}, u32[]{:S(2)}, u32[]{:S(2)}) %collective-permute-start.3) | collective-permute-done | bytes 458784 | tf_op jit(solution)/shard_map/ppermute | solution.py:533
  94.5 8.1 %shard_map.68 = bf16[128,128,448]{2,1,0:T(8,128)(2,1)} custom-call(s32[1]{0:T(128)} %bitcast.1.refs_0_, bf16[16,480,128]{2,1,0:T(8,128)(2,1)S(1)} %all_to_all.40.refs_1_), custom_call_target="tpu_custom_call" | custom-call | flops 1879048192 | bytes 14680064 | tf_op jit(solution)/shard_map/pallas_call | solution.py:156
  102.6 9.3 %shard_map.69 = bf16[128,128,448]{2,1,0:T(8,128)(2,1)} custom-call(s32[1]{0:T(128)} %bitcast.1.refs_0_, bf16[16,480,128]{2,1,0:T(8,128)(2,1)} %collective-permute-done.refs_1_), custom_call_target="tpu_custom_call" | custom-call | flops 1879048192 | bytes 14680064 | tf_op jit(solution)/shard_map/pallas_call | solution.py:156
  111.9 9.0 %shard_map.73 = bf16[16,6,2,16,128]{4,3,2,1,0:T(8,128)(2,1)} custom-call(s32[2]{0:T(128)S(1)} %pad_add_fusion.refs_0_, bf16[16,8,128,448]{3,2,1,0:T(8,128)(2,1)} %bitcast.19, bf16[16,8,128,448]{3,2,1,0:T(8,128)(2,1)} %bitcast.23, bf16[16,112,256]{2,1,0:T(8,128)(2,1)S(1)} %all-to-all-done.refs_3_, bf16[16,112,256]{2,1,0:T(8,128)(2,1)S(1)} %copy-done.4, ...), custom_call_target="tpu_custom_call" | custom-call | flops 3758096384 | bytes 14680064 | tf_op jit(solution)/shard_map/pallas_call | solution.py:237
  120.9 6.6 %all-to-all-start.3 = ((bf16[16,6,2,16,128]{4,3,2,1,0:T(8,128)(2,1)}), bf16[16,6,2,16,128]{4,3,2,1,0:T(8,128)(2,1)S(1)}, u32[]{:S(2)}, u32[]{:S(2)}) async-start(bf16[16,6,2,16,128]{4,3,2,1,0:T(8,128)(2,1)} %shard_map.73), calls=%async_computation.3 | async-start | bytes 1572864 | tf_op jit(solution)/shard_map/all_to_all | solution.py:529
  128.7 9.0 %shard_map.70 = bf16[16,6,2,16,128]{4,3,2,1,0:T(8,128)(2,1)} custom-call(s32[2]{0:T(128)S(1)} %pad_add_fusion.refs_0_, bf16[16,8,128,448]{3,2,1,0:T(8,128)(2,1)} %bitcast.20, bf16[16,8,128,448]{3,2,1,0:T(8,128)(2,1)} %bitcast.24, bf16[16,112,256]{2,1,0:T(8,128)(2,1)S(1)} %all-to-all-done.refs_3_, bf16[16,112,256]{2,1,0:T(8,128)(2,1)S(1)} %copy-done.5, ...), custom_call_target="tpu_custom_call" | custom-call | flops 3758096384 | bytes 14680064 | tf_op jit(solution)/shard_map/pallas_call | solution.py:237
  138.5 6.4 %all-to-all-start.2 = ((bf16[16,6,2,16,128]{4,3,2,1,0:T(8,128)(2,1)}), bf16[16,6,2,16,128]{4,3,2,1,0:T(8,128)(2,1)S(1)}, u32[]{:S(2)}, u32[]{:S(2)}) async-start(bf16[16,6,2,16,128]{4,3,2,1,0:T(8,128)(2,1)} %shard_map.70), calls=%async_computation.2 | async-start | bytes 1572864 | tf_op jit(solution)/shard_map/all_to_all | solution.py:529
  148.3 4.6 %collective-permute-start.12 = (bf16[32,2048]{1,0:T(8,128)(2,1)S(1)}, bf16[32,2048]{1,0:T(8,128)(2,1)S(1)}, u32[]{:S(2)}, u32[]{:S(2)}) collective-permute-start(bf16[32,2048]{1,0:T(8,128)(2,1)S(1)} %get-tuple-element.40), channel_id=1, source_target_pairs={{0,2},{1,3},{2,0},{3,1},{4,6},{5,7},{6,4},{7,5},{8,10},{9,11},{10,... | collective-permute-start | bytes 393224 | tf_op jit(solution)/shard_map/ppermute | solution.py:533
  173.5 3.8 %shard_map.76 = (f32[8,32,2048]{2,1,0:T(8,128)}, bf16[16,6,2,16,128]{4,3,2,1,0:T(8,128)(2,1)}) custom-call(s32[1]{0:T(128)} %bitcast.copy_ref.refs_0_, bf16[32,2048]{1,0:T(8,128)(2,1)S(1)} %shard_map.75.refs_1_, bf16[32,2048]{1,0:T(8,128)(2,1)S(1)} %collective-permute-done.14.refs_2_, bf16[32,2048]{1,0:T(8,128)(2,1)S(1)} %collective-permute-done.15.refs_3_, ...), custom_call_target="tpu_custom_call" | custom-call | flops 805306368 | bytes 3145728 | tf_op jit(solution)/shard_map/pallas_call | solution.py:391
  177.3 7.2 %all-to-all-start.6 = ((bf16[16,6,2,16,128]{4,3,2,1,0:T(8,128)(2,1)}), bf16[16,6,2,16,128]{4,3,2,1,0:T(8,128)(2,1)S(1)}, u32[]{:S(2)}, u32[]{:S(2)}) async-start(bf16[16,6,2,16,128]{4,3,2,1,0:T(8,128)(2,1)} %get-tuple-element.53), calls=%async_computation.6 | async-start | bytes 1572864 | tf_op jit(solution)/shard_map/all_to_all | solution.py:529
  196.7 3.8 %shard_map.77 = (f32[8,32,2048]{2,1,0:T(8,128)}, bf16[16,6,2,16,128]{4,3,2,1,0:T(8,128)(2,1)}) custom-call(s32[1]{0:T(128)} %bitcast.copy_ref.refs_0_, bf16[32,2048]{1,0:T(8,128)(2,1)S(1)} %shard_map.72.refs_1_, bf16[32,2048]{1,0:T(8,128)(2,1)S(1)} %collective-permute-done.8.refs_2_, ...), custom_call_target="tpu_custom_call", output_to_operand_aliasing={{0}: (6, {})} | custom-call | flops 805306368 | bytes 3145728 | tf_op jit(solution)/shard_map/pallas_call | solution.py:391
  200.6 7.2 %all-to-all-start.4 = ((bf16[16,6,2,16,128]{4,3,2,1,0:T(8,128)(2,1)}), bf16[16,6,2,16,128]{4,3,2,1,0:T(8,128)(2,1)S(1)}, u32[]{:S(2)}, u32[]{:S(2)}) async-start(bf16[16,6,2,16,128]{4,3,2,1,0:T(8,128)(2,1)} %get-tuple-element.44), calls=%async_computation.4 | async-start | bytes 1572864 | tf_op jit(solution)/shard_map/all_to_all | solution.py:529
  207.8 8.8 %shard_map.81 = (bf16[2,8,112,128]{3,2,1,0:T(8,128)(2,1)}, bf16[2,8,112,128]{3,2,1,0:T(8,128)(2,1)S(1)}, bf16[2,8,112,128]{3,2,1,0:T(8,128)(2,1)}, bf16[2,8,112,128]{3,2,1,0:T(8,128)(2,1)S(1)}) custom-call(s32[2]{0:T(128)S(1)} %pad_add_fusion.refs_0_, bf16[16,8,128,448]{3,2,1,0:T(8,128)(2,1)} %bitcast.21, bf16[16,8,128,448]{3,2,1,0:T(8,128)(2,1)} %bitcast.25, ...), custom_call_target="tpu_custom_call" | custom-call | flops 3758096384 | bytes 14680064 | tf_op jit(solution)/shard_map/pallas_call | solution.py:474
  219.5 8.8 %shard_map.78 = (bf16[2,8,112,128]{3,2,1,0:T(8,128)(2,1)}, bf16[2,8,112,128]{3,2,1,0:T(8,128)(2,1)S(1)}, bf16[2,8,112,128]{3,2,1,0:T(8,128)(2,1)}, bf16[2,8,112,128]{3,2,1,0:T(8,128)(2,1)S(1)}) custom-call(s32[2]{0:T(128)S(1)} %pad_add_fusion.refs_0_, bf16[16,8,128,448]{3,2,1,0:T(8,128)(2,1)} %bitcast.22, bf16[16,8,128,448]{3,2,1,0:T(8,128)(2,1)} %bitcast.26, ...), custom_call_target="tpu_custom_call" | custom-call | flops 3758096384 | bytes 14680064 | tf_op jit(solution)/shard_map/pallas_call | solution.py:474
  234.5 7.7 %collective-permute-done.23.low_got_ref = bf16[8,112,128]{2,1,0:T(8,128)(2,1)S(1)} collective-permute-done((bf16[8,112,128]{2,1,0:T(8,128)(2,1)S(1)}, bf16[8,112,128]{2,1,0:T(8,128)(2,1)S(1)}, u32[]{:S(2)}, u32[]{:S(2)}) %collective-permute-start.23) | collective-permute-done | bytes 229408 | tf_op jit(solution)/shard_map/ppermute | solution.py:558
  243.1 7.2 %all-to-all-start.7 = ((bf16[16,112,128]{2,1,0:T(8,128)(2,1)}), bf16[16,112,128]{2,1,0:T(8,128)(2,1)S(1)}, u32[]{:S(2)}, u32[]{:S(2)}) async-start(bf16[16,112,128]{2,1,0:T(8,128)(2,1)} %shard_map.83), calls=%async_computation.7 | async-start | bytes 917504 | tf_op jit(solution)/shard_map/all_to_all | solution.py:529
  252.6 5.2 %collective-permute-done.19.low_got_ref = bf16[8,112,128]{2,1,0:T(8,128)(2,1)S(1)} collective-permute-done((bf16[8,112,128]{2,1,0:T(8,128)(2,1)S(1)}, bf16[8,112,128]{2,1,0:T(8,128)(2,1)S(1)}, u32[]{:S(2)}, u32[]{:S(2)}) %collective-permute-start.19) | collective-permute-done | bytes 229408 | tf_op jit(solution)/shard_map/ppermute | solution.py:558
  259.4 7.2 %all-to-all-start.5 = ((bf16[16,112,128]{2,1,0:T(8,128)(2,1)}), bf16[16,112,128]{2,1,0:T(8,128)(2,1)S(1)}, u32[]{:S(2)}, u32[]{:S(2)}) async-start(bf16[16,112,128]{2,1,0:T(8,128)(2,1)} %shard_map.80), calls=%async_computation.5 | async-start | bytes 917504 | tf_op jit(solution)/shard_map/all_to_all | solution.py:529
  267.8 6.1 %all-to-all-done.5 = bf16[16,112,128]{2,1,0:T(8,128)(2,1)S(1)} async-done(((bf16[16,112,128]{2,1,0:T(8,128)(2,1)}), bf16[16,112,128]{2,1,0:T(8,128)(2,1)S(1)}, u32[]{:S(2)}, u32[]{:S(2)}) %all-to-all-start.5) | async-done | bytes 458784 | tf_op jit(solution)/shard_map/all_to_all | solution.py:529
  (82 shorter events, 67.0 us)
Async XLA Ops:
  2.8 20.5 %all-to-all-start = ((bf16[16,112,256]{2,1,0:T(8,128)(2,1)}), bf16[16,112,256]{2,1,0:T(8,128)(2,1)S(1)}, u32[]{:S(2)}, u32[]{:S(2)}) async-start(bf16[16,112,256]{2,1,0:T(8,128)(2,1)} %bitcast.32), calls=%async_computation | async-start | bytes 1835008 | tf_op jit(solution)/shard_map/all_to_all | solution.py:529
  53.3 49.3 %collective-permute-start = (bf16[16,480,128]{2,1,0:T(8,128)(2,1)S(1)}, bf16[16,480,128]{2,1,0:T(8,128)(2,1)}, u32[]{:S(2)}, u32[]{:S(2)}) collective-permute-start(bf16[16,480,128]{2,1,0:T(8,128)(2,1)S(1)} %all_to_all.40.refs_1_), channel_id=1, source_target_pairs={{0,4},{4,0},{1,5},{5,1},{2,6},{6,2},{3,7},{7,3},{8,12},{12,8},{9,1... | collective-permute-start | bytes 5898248 | tf_op jit(solution)/shard_map/ppermute | solution.py:590
  53.3 25.1 %collective-permute-start.2 = (bf16[16,112,256]{2,1,0:T(8,128)(2,1)S(1)}, bf16[16,112,256]{2,1,0:T(8,128)(2,1)S(1)}, u32[]{:S(2)}, u32[]{:S(2)}) collective-permute-start(bf16[16,112,256]{2,1,0:T(8,128)(2,1)S(1)} %all-to-all-done.refs_3_), channel_id=1, source_target_pairs={{0,1},{1,2},{2,3},{3,0},{4,5},{5,6},{6,7},{7,4},{8,9},{9,10},{10,1... | collective-permute-start | bytes 2752520 | tf_op jit(solution)/shard_map/ppermute | solution.py:533
  55.2 24.0 %collective-permute-start.1 = (bf16[16,112,256]{2,1,0:T(8,128)(2,1)S(1)}, bf16[16,112,256]{2,1,0:T(8,128)(2,1)S(1)}, u32[]{:S(2)}, u32[]{:S(2)}) collective-permute-start(bf16[16,112,256]{2,1,0:T(8,128)(2,1)S(1)} %all-to-all-done.refs_3_), channel_id=1, source_target_pairs={{0,3},{1,0},{2,1},{3,2},{4,7},{5,4},{6,5},{7,6},{8,11},{9,8},{10,9... | collective-permute-start | bytes 2752520 | tf_op jit(solution)/shard_map/ppermute | solution.py:533
  79.2 13.8 %collective-permute-start.3 = (bf16[8,112,256]{2,1,0:T(8,128)(2,1)}, bf16[8,112,256]{2,1,0:T(8,128)(2,1)S(1)}, u32[]{:S(2)}, u32[]{:S(2)}) collective-permute-start(bf16[8,112,256]{2,1,0:T(8,128)(2,1)} %slice.8), channel_id=1, source_target_pairs={{0,1},{1,2},{2,3},{3,0},{4,5},{5,6},{6,7},{7,4},{8,9},{9,10},{10,1... | collective-permute-start | bytes 1376264 | tf_op jit(solution)/shard_map/ppermute | solution.py:533
  80.5 12.9 %collective-permute-start.4 = (bf16[8,112,256]{2,1,0:T(8,128)(2,1)}, bf16[8,112,256]{2,1,0:T(8,128)(2,1)}, u32[]{:S(2)}, u32[]{:S(2)}) collective-permute-start(bf16[8,112,256]{2,1,0:T(8,128)(2,1)} %slice.9), channel_id=1, source_target_pairs={{0,3},{1,0},{2,1},{3,2},{4,7},{5,4},{6,5},{7,6},{8,11},{9,8},{10,9... | collective-permute-start | bytes 1376264 | tf_op jit(solution)/shard_map/ppermute | solution.py:533
  120.9 17.6 %all-to-all-start.3 = ((bf16[16,6,2,16,128]{4,3,2,1,0:T(8,128)(2,1)}), bf16[16,6,2,16,128]{4,3,2,1,0:T(8,128)(2,1)S(1)}, u32[]{:S(2)}, u32[]{:S(2)}) async-start(bf16[16,6,2,16,128]{4,3,2,1,0:T(8,128)(2,1)} %shard_map.73), calls=%async_computation.3 | async-start | bytes 1572864 | tf_op jit(solution)/shard_map/all_to_all | solution.py:529
  138.5 27.4 %all-to-all-start.2 = ((bf16[16,6,2,16,128]{4,3,2,1,0:T(8,128)(2,1)}), bf16[16,6,2,16,128]{4,3,2,1,0:T(8,128)(2,1)S(1)}, u32[]{:S(2)}, u32[]{:S(2)}) async-start(bf16[16,6,2,16,128]{4,3,2,1,0:T(8,128)(2,1)} %shard_map.70), calls=%async_computation.2 | async-start | bytes 1572864 | tf_op jit(solution)/shard_map/all_to_all | solution.py:529
  148.3 9.0 %collective-permute-start.12 = (bf16[32,2048]{1,0:T(8,128)(2,1)S(1)}, bf16[32,2048]{1,0:T(8,128)(2,1)S(1)}, u32[]{:S(2)}, u32[]{:S(2)}) collective-permute-start(bf16[32,2048]{1,0:T(8,128)(2,1)S(1)} %get-tuple-element.40), channel_id=1, source_target_pairs={{0,2},{1,3},{2,0},{3,1},{4,6},{5,7},{6,4},{7,5},{8,10},{9,11},{10,... | collective-permute-start | bytes 393224 | tf_op jit(solution)/shard_map/ppermute | solution.py:533
  161.6 9.3 %collective-permute-start.14 = (bf16[32,2048]{1,0:T(8,128)(2,1)S(1)}, bf16[32,2048]{1,0:T(8,128)(2,1)S(1)}, u32[]{:S(2)}, u32[]{:S(2)}) collective-permute-start(bf16[32,2048]{1,0:T(8,128)(2,1)S(1)} %shard_map.75.refs_1_), channel_id=1, source_target_pairs={{0,1},{1,2},{2,3},{3,0},{4,5},{5,6},{6,7},{7,4},{8,9},{9,10},{10,1... | collective-permute-start | bytes 393224 | tf_op jit(solution)/shard_map/ppermute | solution.py:533
  161.8 11.6 %collective-permute-start.15 = (bf16[32,2048]{1,0:T(8,128)(2,1)S(1)}, bf16[32,2048]{1,0:T(8,128)(2,1)S(1)}, u32[]{:S(2)}, u32[]{:S(2)}) collective-permute-start(bf16[32,2048]{1,0:T(8,128)(2,1)S(1)} %shard_map.75.refs_1_), channel_id=1, source_target_pairs={{0,2},{1,3},{2,0},{3,1},{4,6},{5,7},{6,4},{7,5},{8,10},{9,11},{10,... | collective-permute-start | bytes 393224 | tf_op jit(solution)/shard_map/ppermute | solution.py:533
  165.2 8.3 %collective-permute-start.16 = (bf16[32,2048]{1,0:T(8,128)(2,1)S(1)}, bf16[32,2048]{1,0:T(8,128)(2,1)S(1)}, u32[]{:S(2)}, u32[]{:S(2)}) collective-permute-start(bf16[32,2048]{1,0:T(8,128)(2,1)S(1)} %shard_map.75.refs_1_), channel_id=1, source_target_pairs={{0,3},{1,0},{2,1},{3,2},{4,7},{5,4},{6,5},{7,6},{8,11},{9,8},{10,9... | collective-permute-start | bytes 393224 | tf_op jit(solution)/shard_map/ppermute | solution.py:533
  168.7 15.8 %collective-permute-start.5 = (bf16[32,2048]{1,0:T(8,128)(2,1)S(1)}, bf16[32,2048]{1,0:T(8,128)(2,1)S(1)}, u32[]{:S(2)}, u32[]{:S(2)}) collective-permute-start(bf16[32,2048]{1,0:T(8,128)(2,1)S(1)} %get-tuple-element.35), channel_id=1, source_target_pairs={{0,1},{1,2},{2,3},{3,0},{4,5},{5,6},{6,7},{7,4},{8,9},{9,10},{10,1... | collective-permute-start | bytes 393224 | tf_op jit(solution)/shard_map/ppermute | solution.py:533
  170.1 14.5 %collective-permute-start.6 = (bf16[32,2048]{1,0:T(8,128)(2,1)S(1)}, bf16[32,2048]{1,0:T(8,128)(2,1)S(1)}, u32[]{:S(2)}, u32[]{:S(2)}) collective-permute-start(bf16[32,2048]{1,0:T(8,128)(2,1)S(1)} %get-tuple-element.36), channel_id=1, source_target_pairs={{0,2},{1,3},{2,0},{3,1},{4,6},{5,7},{6,4},{7,5},{8,10},{9,11},{10,... | collective-permute-start | bytes 393224 | tf_op jit(solution)/shard_map/ppermute | solution.py:533
  170.9 13.6 %collective-permute-start.7 = (bf16[32,2048]{1,0:T(8,128)(2,1)S(1)}, bf16[32,2048]{1,0:T(8,128)(2,1)S(1)}, u32[]{:S(2)}, u32[]{:S(2)}) collective-permute-start(bf16[32,2048]{1,0:T(8,128)(2,1)S(1)} %get-tuple-element.37), channel_id=1, source_target_pairs={{0,3},{1,0},{2,1},{3,2},{4,7},{5,4},{6,5},{7,6},{8,11},{9,8},{10,9... | collective-permute-start | bytes 393224 | tf_op jit(solution)/shard_map/ppermute | solution.py:533
  177.3 23.3 %all-to-all-start.6 = ((bf16[16,6,2,16,128]{4,3,2,1,0:T(8,128)(2,1)}), bf16[16,6,2,16,128]{4,3,2,1,0:T(8,128)(2,1)S(1)}, u32[]{:S(2)}, u32[]{:S(2)}) async-start(bf16[16,6,2,16,128]{4,3,2,1,0:T(8,128)(2,1)} %get-tuple-element.53), calls=%async_computation.6 | async-start | bytes 1572864 | tf_op jit(solution)/shard_map/all_to_all | solution.py:529
  200.6 18.9 %all-to-all-start.4 = ((bf16[16,6,2,16,128]{4,3,2,1,0:T(8,128)(2,1)}), bf16[16,6,2,16,128]{4,3,2,1,0:T(8,128)(2,1)S(1)}, u32[]{:S(2)}, u32[]{:S(2)}) async-start(bf16[16,6,2,16,128]{4,3,2,1,0:T(8,128)(2,1)} %get-tuple-element.44), calls=%async_computation.4 | async-start | bytes 1572864 | tf_op jit(solution)/shard_map/all_to_all | solution.py:529
  216.6 13.7 %collective-permute-start.21 = (bf16[2,8,112,128]{3,2,1,0:T(8,128)(2,1)}, bf16[2,8,112,128]{3,2,1,0:T(8,128)(2,1)S(1)}, u32[]{:S(2)}, u32[]{:S(2)}) collective-permute-start(bf16[2,8,112,128]{3,2,1,0:T(8,128)(2,1)} %get-tuple-element.55), channel_id=1, source_target_pairs={{0,1},{1,0},{2,3},{3,2},{4,5},{5,4},{6,7},{7,6},{8,9},{9,8},{10,11... | collective-permute-start | bytes 1376264 | tf_op jit(solution)/shard_map/ppermute | solution.py:553
  217.6 12.7 %collective-permute-start.22 = (bf16[2,8,112,128]{3,2,1,0:T(8,128)(2,1)}, bf16[2,8,112,128]{3,2,1,0:T(8,128)(2,1)}, u32[]{:S(2)}, u32[]{:S(2)}) collective-permute-start(bf16[2,8,112,128]{3,2,1,0:T(8,128)(2,1)} %get-tuple-element.57), channel_id=1, source_target_pairs={{0,3},{1,2},{2,1},{3,0},{4,7},{5,6},{6,5},{7,4},{8,11},{9,10},{10,... | collective-permute-start | bytes 1376264 | tf_op jit(solution)/shard_map/ppermute | solution.py:554
  228.3 22.0 %collective-permute-start.17 = (bf16[2,8,112,128]{3,2,1,0:T(8,128)(2,1)}, bf16[2,8,112,128]{3,2,1,0:T(8,128)(2,1)S(1)}, u32[]{:S(2)}, u32[]{:S(2)}) collective-permute-start(bf16[2,8,112,128]{3,2,1,0:T(8,128)(2,1)} %get-tuple-element.46), channel_id=1, source_target_pairs={{0,1},{1,0},{2,3},{3,2},{4,5},{5,4},{6,7},{7,6},{8,9},{9,8},{10,11... | collective-permute-start | bytes 1376264 | tf_op jit(solution)/shard_map/ppermute | solution.py:553
  229.7 20.6 %collective-permute-start.18 = (bf16[2,8,112,128]{3,2,1,0:T(8,128)(2,1)}, bf16[2,8,112,128]{3,2,1,0:T(8,128)(2,1)S(1)}, u32[]{:S(2)}, u32[]{:S(2)}) collective-permute-start(bf16[2,8,112,128]{3,2,1,0:T(8,128)(2,1)} %get-tuple-element.48), channel_id=1, source_target_pairs={{0,3},{1,2},{2,1},{3,0},{4,7},{5,6},{6,5},{7,4},{8,11},{9,10},{10,... | collective-permute-start | bytes 1376264 | tf_op jit(solution)/shard_map/ppermute | solution.py:554
  231.6 10.7 %collective-permute-start.23 = (bf16[8,112,128]{2,1,0:T(8,128)(2,1)S(1)}, bf16[8,112,128]{2,1,0:T(8,128)(2,1)S(1)}, u32[]{:S(2)}, u32[]{:S(2)}) collective-permute-start(bf16[8,112,128]{2,1,0:T(8,128)(2,1)S(1)} %get-tuple-element.59), channel_id=1, source_target_pairs={{0,3},{1,2},{2,1},{3,0},{4,7},{5,6},{6,5},{7,4},{8,11},{9,10},{10,... | collective-permute-start | bytes 688136 | tf_op jit(solution)/shard_map/ppermute | solution.py:558
  243.1 16.3 %all-to-all-start.7 = ((bf16[16,112,128]{2,1,0:T(8,128)(2,1)}), bf16[16,112,128]{2,1,0:T(8,128)(2,1)S(1)}, u32[]{:S(2)}, u32[]{:S(2)}) async-start(bf16[16,112,128]{2,1,0:T(8,128)(2,1)} %shard_map.83), calls=%async_computation.7 | async-start | bytes 917504 | tf_op jit(solution)/shard_map/all_to_all | solution.py:529
  259.4 14.4 %all-to-all-start.5 = ((bf16[16,112,128]{2,1,0:T(8,128)(2,1)}), bf16[16,112,128]{2,1,0:T(8,128)(2,1)S(1)}, u32[]{:S(2)}, u32[]{:S(2)}) async-start(bf16[16,112,128]{2,1,0:T(8,128)(2,1)} %shard_map.80), calls=%async_computation.5 | async-start | bytes 917504 | tf_op jit(solution)/shard_map/all_to_all | solution.py:529
  (16 other events, 116.5 us)

commit v7 on v6

--- a/solution.py
+++ b/solution.py
@@ -200,14 +200,18 @@
     q_refs, (out_ref, q_ref, tmp_ref, rows_ref, sems) = rest[:-5], rest[-5:]
     own_ref, sib_ref = arrived_rows((own_ref, sib_ref), rows_ref, sems, stream)
     core, copy = at_ref[0], at_ref[1]
-    copies = len(q_refs)
+    copies = 4
     lanes = out_ref.shape[4]
+    low = pl.program_id(0) < pl.num_programs(0) // 2
     owner = lax.broadcasted_iota(jnp.int32, (128, lanes), 1) // 32
     for n in range(out_ref.shape[0]):
         part = q_refs[0].shape[1]
-        for shift, ref in enumerate(q_refs):
+        here = slice(stream * lanes, (stream + 1) * lanes)
+        for shift, ref in zip((0, 1, 3), q_refs):
             start = pl.multiple_of(part * ((copy + shift) % copies), 16)
-            q_ref[pl.ds(start, part), :] = ref[n, :, stream * lanes : (stream + 1) * lanes]
+            q_ref[pl.ds(start, part), :] = ref[n, :, here]
+        start = pl.multiple_of(part * ((copy + 2) % copies), 16)
+        q_ref[pl.ds(start, part), :] = jnp.where(low, q_refs[3][n, :, here], q_refs[4][n, :, here])
         for half, ref in enumerate((own_ref, sib_ref)):
             _, experts, rows, width = ref.shape
             got = lax.dot_general(
@@ -233,13 +237,18 @@
     def body(*refs):
         mix_kernel(*refs, stream=stream)
 
-    q_block = pl.BlockSpec((step, part, lanes * STREAMS), lambda i, _: (i, 0, 0))
+    half = chips // step // 2
+    q_shape = (step, part, lanes * STREAMS)
+    q_blocks = [pl.BlockSpec(q_shape, lambda i, _: (i, 0, 0))] * 3 + [
+        pl.BlockSpec(q_shape, lambda i, _: (jnp.minimum(i, half - 1), 0, 0)),
+        pl.BlockSpec(q_shape, lambda i, _: (jnp.maximum(i - half, 0), 0, 0)),
+    ]
     return pl.pallas_call(
         body,
         grid_spec=pltpu.PrefetchScalarGridSpec(
             num_scalar_prefetch=1,
             grid=(chips // step,),
-            in_specs=[block, block] + [q_block] * len(q_parts),
+            in_specs=[block, block] + q_blocks,
             out_specs=pl.BlockSpec((step, CAP, 2, 16, lanes), lambda i, _: (i, 0, 0, 0, 0)),
             scratch_shapes=[
                 pltpu.VMEM((width, lanes), BF16),
@@ -255,7 +264,7 @@
             bytes_accessed=4 * chips * experts * rows * width,
             transcendentals=0,
         ),
-    )(at, own, sib, *q_parts)
+    )(at, own, sib, *(from_hbm(q) for q in q_parts))
 
 
 def factor_kernel(copy_ref, parts_ref, hidden_ref, *refs):
@@ -568,7 +577,7 @@
     after = shift(part, copies - 1, copies)
     far_low = shift(before[:half], 1, copies)
     far_high = shift(after[half:], copies - 1, copies)
-    return [part, after, jnp.concatenate([far_low, far_high], axis=0), before]
+    return [part, after, before, far_low, far_high]
 
 
 def whole(out_grads, expert_ids, gate_probs, hidden_acts, q_previous):

time: 278 us -> 271 us (0.975)
  waiting for transfers between devices: 69.8 us -> 60.1 us
  Pallas kernels: 85 us -> 89.8 us
    ppermute x16, waiting for transfers between devices: 40.1 us -> 31.2 us  [shift(): lax.ppermute(value, 'dp', [(i, (i + step) % copies) for i in range(copies)])]
    pallas_call x2, Pallas kernels: 17.9 us -> 23.3 us  [mix(): pl.pallas_call(body, grid_spec=pltpu.PrefetchScalarGridSpec(num_scalar_pr...]
  transfers between devices with their start and end apart: 32 -> 32, of which waited for: 14 -> 10; matrix products, arithmetic and copies ran while one was open for 1% -> 1% of each run, Pallas kernels for 23% -> 28%
where the time goes in v7:
time: 271 us; the launch traced here: 267 us
  Pallas kernels  89.8 us (33%)
  starting transfers between devices  83.5 us (31%)
  waiting for transfers between devices  60.1 us (22%)
  blocking collectives  30 us (11%)
  local copies, waits for them, and re-layouts  3.01 us (1%)
    all_to_all x7, starting transfers between devices, exchange(): return lax.all_to_all(values, axes, split_axis=0, concat_axis=0, tiled=True)  50.1 us
    ppermute x16, waiting for transfers between devices, shift(): lax.ppermute(value, 'dp', [(i, (i + step) % copies) for i in range(copies)])  31.2 us
    all_to_all x1, blocking collectives, exchange(): return lax.all_to_all(values, axes, split_axis=0, concat_axis=0, tiled=True)  30 us
    ppermute x16, starting transfers between devices, shift(): lax.ppermute(value, 'dp', [(i, (i + step) % copies) for i in range(copies)])  23.6 us
    pallas_call x2, Pallas kernels, mix(): pl.pallas_call(body, grid_spec=pltpu.PrefetchScalarGridSpec(num_scalar_pr...  23.3 us
    pallas_call x2, Pallas kernels, second_terms(): pl.pallas_call(body, grid_spec=pltpu.PrefetchScalarGridSpec(num_scalar_pr...  17.7 us
    pallas_call x2, Pallas kernels, dispatch(): pl.pallas_call(body, grid_spec=pltpu.PrefetchScalarGridSpec(num_scalar_pr...  16.8 us
    all_to_all x7, waiting for transfers between devices, exchange(): return lax.all_to_all(values, axes, split_axis=0, concat_axis=0, tiled=True)  15.2 us
  transfers between devices with their start and end apart: 32, of which 10 were waited for; matrix products, arithmetic and copies ran while one was open for 1% of the time, Pallas kernels for 28%

profile of v7, /device:TPU:6, one launch (start us, length us, event | category | flops | bytes accessed | tf_op | source)
XLA Modules:
  0.0 267.2 jit_solution(5051127004910100802)
XLA Ops:
  2.8 7.4 %all-to-all-start = ((bf16[16,112,256]{2,1,0:T(8,128)(2,1)}), bf16[16,112,256]{2,1,0:T(8,128)(2,1)S(1)}, u32[]{:S(2)}, u32[]{:S(2)}) async-start(bf16[16,112,256]{2,1,0:T(8,128)(2,1)} %bitcast.32), calls=%async_computation | async-start | bytes 1835008 | tf_op jit(solution)/shard_map/all_to_all | solution.py:538
  10.2 4.0 %prepare.1 = bf16[16,480,128]{2,1,0:T(8,128)(2,1)} custom-call(s32[8,128]{1,0:T(8,128)} %bitcast.35, f32[8,128]{1,0:T(8,128)} %bitcast.36, bf16[128,7168]{1,0:T(8,128)(2,1)} %bitcast.34), custom_call_target="tpu_custom_call" | custom-call | tf_op jit(solution)/shard_map/prepare/pallas_call | solution.py:94
  14.2 9.1 %all-to-all-done.refs_3_ = bf16[16,112,256]{2,1,0:T(8,128)(2,1)S(1)} async-done(((bf16[16,112,256]{2,1,0:T(8,128)(2,1)}), bf16[16,112,256]{2,1,0:T(8,128)(2,1)S(1)}, u32[]{:S(2)}, u32[]{:S(2)}) %all-to-all-start) | async-done | bytes 917536 | tf_op jit(solution)/shard_map/all_to_all | solution.py:538
  23.4 30.0 %all_to_all.40.refs_1_ = bf16[16,480,128]{2,1,0:T(8,128)(2,1)S(1)} all-to-all(bf16[16,480,128]{2,1,0:T(8,128)(2,1)} %prepare.1), channel_id=1, replica_groups=mesh['chip'=16,'core'=2,'dp'=4] {'chip'}, dimensions={0} | all-to-all | bytes 3932160 | tf_op jit(solution)/shard_map/all_to_all | solution.py:538
  57.3 21.1 %collective-permute-done.2.refs_5_ = bf16[16,112,256]{2,1,0:T(8,128)(2,1)} collective-permute-done((bf16[16,112,256]{2,1,0:T(8,128)(2,1)S(1)}, bf16[16,112,256]{2,1,0:T(8,128)(2,1)}, u32[]{:S(2)}, u32[]{:S(2)}) %collective-permute-start.2) | collective-permute-done | bytes 917536 | tf_op jit(solution)/shard_map/ppermute | solution.py:542
  84.0 7.9 %shard_map.68 = bf16[128,128,448]{2,1,0:T(8,128)(2,1)} custom-call(s32[1]{0:T(128)} %bitcast.1.refs_0_, bf16[16,480,128]{2,1,0:T(8,128)(2,1)S(1)} %all_to_all.40.refs_1_), custom_call_target="tpu_custom_call" | custom-call | flops 1879048192 | bytes 14680064 | tf_op jit(solution)/shard_map/pallas_call | solution.py:156
  91.9 8.9 %shard_map.69 = bf16[128,128,448]{2,1,0:T(8,128)(2,1)} custom-call(s32[1]{0:T(128)} %bitcast.1.refs_0_, bf16[16,480,128]{2,1,0:T(8,128)(2,1)} %collective-permute-done.refs_1_), custom_call_target="tpu_custom_call" | custom-call | flops 1879048192 | bytes 14680064 | tf_op jit(solution)/shard_map/pallas_call | solution.py:156
  101.7 11.6 %shard_map.73 = bf16[16,6,2,16,128]{4,3,2,1,0:T(8,128)(2,1)} custom-call(s32[2]{0:T(128)S(1)} %pad_add_fusion.refs_0_, bf16[16,8,128,448]{3,2,1,0:T(8,128)(2,1)} %bitcast.19, bf16[16,8,128,448]{3,2,1,0:T(8,128)(2,1)} %bitcast.23, bf16[16,112,256]{2,1,0:T(8,128)(2,1)} %copy-done, bf16[16,112,256]{2,1,0:T(8,128)(2,1)} %collective-permute-done.1.refs_4_, ...), custom_call_target="tpu_custom_call" | custom-call | flops 3758096384 | bytes 14680064 | tf_op jit(solution)/shard_map/pallas_call | solution.py:246
  113.4 6.5 %all-to-all-start.3 = ((bf16[16,6,2,16,128]{4,3,2,1,0:T(8,128)(2,1)}), bf16[16,6,2,16,128]{4,3,2,1,0:T(8,128)(2,1)S(1)}, u32[]{:S(2)}, u32[]{:S(2)}) async-start(bf16[16,6,2,16,128]{4,3,2,1,0:T(8,128)(2,1)} %shard_map.73), calls=%async_computation.3 | async-start | bytes 1572864 | tf_op jit(solution)/shard_map/all_to_all | solution.py:538
  119.8 11.7 %shard_map.70 = bf16[16,6,2,16,128]{4,3,2,1,0:T(8,128)(2,1)} custom-call(s32[2]{0:T(128)S(1)} %pad_add_fusion.refs_0_, bf16[16,8,128,448]{3,2,1,0:T(8,128)(2,1)} %bitcast.20, bf16[16,8,128,448]{3,2,1,0:T(8,128)(2,1)} %bitcast.24, bf16[16,112,256]{2,1,0:T(8,128)(2,1)} %copy-done, bf16[16,112,256]{2,1,0:T(8,128)(2,1)} %collective-permute-done.1.refs_4_, ...), custom_call_target="tpu_custom_call" | custom-call | flops 3758096384 | bytes 14680064 | tf_op jit(solution)/shard_map/pallas_call | solution.py:246
  131.5 7.3 %all-to-all-start.2 = ((bf16[16,6,2,16,128]{4,3,2,1,0:T(8,128)(2,1)}), bf16[16,6,2,16,128]{4,3,2,1,0:T(8,128)(2,1)S(1)}, u32[]{:S(2)}, u32[]{:S(2)}) async-start(bf16[16,6,2,16,128]{4,3,2,1,0:T(8,128)(2,1)} %shard_map.70), calls=%async_computation.2 | async-start | bytes 1572864 | tf_op jit(solution)/shard_map/all_to_all | solution.py:538
  144.9 4.7 %collective-permute-done.11.refs_1_ = bf16[32,2048]{1,0:T(8,128)(2,1)S(1)} collective-permute-done((bf16[32,2048]{1,0:T(8,128)(2,1)S(1)}, bf16[32,2048]{1,0:T(8,128)(2,1)S(1)}, u32[]{:S(2)}, u32[]{:S(2)}) %collective-permute-start.11) | collective-permute-done | bytes 131104 | tf_op jit(solution)/shard_map/ppermute | solution.py:542
  165.8 3.8 %shard_map.76 = (f32[8,32,2048]{2,1,0:T(8,128)}, bf16[16,6,2,16,128]{4,3,2,1,0:T(8,128)(2,1)}) custom-call(s32[1]{0:T(128)} %bitcast.copy_ref.refs_0_, bf16[32,2048]{1,0:T(8,128)(2,1)S(1)} %shard_map.75.refs_1_, bf16[32,2048]{1,0:T(8,128)(2,1)S(1)} %collective-permute-done.14.refs_2_, bf16[32,2048]{1,0:T(8,128)(2,1)S(1)} %collective-permute-done.15.refs_3_, ...), custom_call_target="tpu_custom_call" | custom-call | flops 805306368 | bytes 3145728 | tf_op jit(solution)/shard_map/pallas_call | solution.py:400
  169.6 7.2 %all-to-all-start.6 = ((bf16[16,6,2,16,128]{4,3,2,1,0:T(8,128)(2,1)}), bf16[16,6,2,16,128]{4,3,2,1,0:T(8,128)(2,1)S(1)}, u32[]{:S(2)}, u32[]{:S(2)}) async-start(bf16[16,6,2,16,128]{4,3,2,1,0:T(8,128)(2,1)} %get-tuple-element.53), calls=%async_computation.6 | async-start | bytes 1572864 | tf_op jit(solution)/shard_map/all_to_all | solution.py:538
  184.4 3.8 %collective-permute-done.8.refs_2_ = bf16[32,2048]{1,0:T(8,128)(2,1)S(1)} collective-permute-done((bf16[32,2048]{1,0:T(8,128)(2,1)S(1)}, bf16[32,2048]{1,0:T(8,128)(2,1)S(1)}, u32[]{:S(2)}, u32[]{:S(2)}) %collective-permute-start.8) | collective-permute-done | bytes 131104 | tf_op jit(solution)/shard_map/ppermute | solution.py:542
  189.1 3.8 %shard_map.77 = (f32[8,32,2048]{2,1,0:T(8,128)}, bf16[16,6,2,16,128]{4,3,2,1,0:T(8,128)(2,1)}) custom-call(s32[1]{0:T(128)} %bitcast.copy_ref.refs_0_, bf16[32,2048]{1,0:T(8,128)(2,1)S(1)} %shard_map.72.refs_1_, bf16[32,2048]{1,0:T(8,128)(2,1)S(1)} %collective-permute-done.8.refs_2_, ...), custom_call_target="tpu_custom_call", output_to_operand_aliasing={{0}: (6, {})} | custom-call | flops 805306368 | bytes 3145728 | tf_op jit(solution)/shard_map/pallas_call | solution.py:400
  192.9 7.2 %all-to-all-start.4 = ((bf16[16,6,2,16,128]{4,3,2,1,0:T(8,128)(2,1)}), bf16[16,6,2,16,128]{4,3,2,1,0:T(8,128)(2,1)S(1)}, u32[]{:S(2)}, u32[]{:S(2)}) async-start(bf16[16,6,2,16,128]{4,3,2,1,0:T(8,128)(2,1)} %get-tuple-element.44), calls=%async_computation.4 | async-start | bytes 1572864 | tf_op jit(solution)/shard_map/all_to_all | solution.py:538
  200.2 8.8 %shard_map.81 = (bf16[2,8,112,128]{3,2,1,0:T(8,128)(2,1)}, bf16[2,8,112,128]{3,2,1,0:T(8,128)(2,1)S(1)}, bf16[2,8,112,128]{3,2,1,0:T(8,128)(2,1)}, bf16[2,8,112,128]{3,2,1,0:T(8,128)(2,1)S(1)}) custom-call(s32[2]{0:T(128)S(1)} %pad_add_fusion.refs_0_, bf16[16,8,128,448]{3,2,1,0:T(8,128)(2,1)} %bitcast.21, bf16[16,8,128,448]{3,2,1,0:T(8,128)(2,1)} %bitcast.25, ...), custom_call_target="tpu_custom_call" | custom-call | flops 3758096384 | bytes 14680064 | tf_op jit(solution)/shard_map/pallas_call | solution.py:483
  211.9 8.8 %shard_map.78 = (bf16[2,8,112,128]{3,2,1,0:T(8,128)(2,1)}, bf16[2,8,112,128]{3,2,1,0:T(8,128)(2,1)S(1)}, bf16[2,8,112,128]{3,2,1,0:T(8,128)(2,1)}, bf16[2,8,112,128]{3,2,1,0:T(8,128)(2,1)S(1)}) custom-call(s32[2]{0:T(128)S(1)} %pad_add_fusion.refs_0_, bf16[16,8,128,448]{3,2,1,0:T(8,128)(2,1)} %bitcast.22, bf16[16,8,128,448]{3,2,1,0:T(8,128)(2,1)} %bitcast.26, ...), custom_call_target="tpu_custom_call" | custom-call | flops 3758096384 | bytes 14680064 | tf_op jit(solution)/shard_map/pallas_call | solution.py:483
  226.6 7.8 %collective-permute-done.23.low_got_ref = bf16[8,112,128]{2,1,0:T(8,128)(2,1)S(1)} collective-permute-done((bf16[8,112,128]{2,1,0:T(8,128)(2,1)S(1)}, bf16[8,112,128]{2,1,0:T(8,128)(2,1)S(1)}, u32[]{:S(2)}, u32[]{:S(2)}) %collective-permute-start.23) | collective-permute-done | bytes 229408 | tf_op jit(solution)/shard_map/ppermute | solution.py:567
  235.3 7.2 %all-to-all-start.7 = ((bf16[16,112,128]{2,1,0:T(8,128)(2,1)}), bf16[16,112,128]{2,1,0:T(8,128)(2,1)S(1)}, u32[]{:S(2)}, u32[]{:S(2)}) async-start(bf16[16,112,128]{2,1,0:T(8,128)(2,1)} %shard_map.83), calls=%async_computation.7 | async-start | bytes 917504 | tf_op jit(solution)/shard_map/all_to_all | solution.py:538
  245.0 5.1 %collective-permute-done.19.low_got_ref = bf16[8,112,128]{2,1,0:T(8,128)(2,1)S(1)} collective-permute-done((bf16[8,112,128]{2,1,0:T(8,128)(2,1)S(1)}, bf16[8,112,128]{2,1,0:T(8,128)(2,1)S(1)}, u32[]{:S(2)}, u32[]{:S(2)}) %collective-permute-start.19) | collective-permute-done | bytes 229408 | tf_op jit(solution)/shard_map/ppermute | solution.py:567
  251.8 7.2 %all-to-all-start.5 = ((bf16[16,112,128]{2,1,0:T(8,128)(2,1)}), bf16[16,112,128]{2,1,0:T(8,128)(2,1)S(1)}, u32[]{:S(2)}, u32[]{:S(2)}) async-start(bf16[16,112,128]{2,1,0:T(8,128)(2,1)} %shard_map.80), calls=%async_computation.5 | async-start | bytes 917504 | tf_op jit(solution)/shard_map/all_to_all | solution.py:538
  260.1 6.1 %all-to-all-done.5 = bf16[16,112,128]{2,1,0:T(8,128)(2,1)S(1)} async-done(((bf16[16,112,128]{2,1,0:T(8,128)(2,1)}), bf16[16,112,128]{2,1,0:T(8,128)(2,1)S(1)}, u32[]{:S(2)}, u32[]{:S(2)}) %all-to-all-start.5) | async-done | bytes 458784 | tf_op jit(solution)/shard_map/all_to_all | solution.py:538
  (70 shorter events, 59.3 us)
Async XLA Ops:
  2.8 20.5 %all-to-all-start = ((bf16[16,112,256]{2,1,0:T(8,128)(2,1)}), bf16[16,112,256]{2,1,0:T(8,128)(2,1)S(1)}, u32[]{:S(2)}, u32[]{:S(2)}) async-start(bf16[16,112,256]{2,1,0:T(8,128)(2,1)} %bitcast.32), calls=%async_computation | async-start | bytes 1835008 | tf_op jit(solution)/shard_map/all_to_all | solution.py:538
  53.3 38.6 %collective-permute-start = (bf16[16,480,128]{2,1,0:T(8,128)(2,1)S(1)}, bf16[16,480,128]{2,1,0:T(8,128)(2,1)}, u32[]{:S(2)}, u32[]{:S(2)}) collective-permute-start(bf16[16,480,128]{2,1,0:T(8,128)(2,1)S(1)} %all_to_all.40.refs_1_), channel_id=1, source_target_pairs={{0,4},{4,0},{1,5},{5,1},{2,6},{6,2},{3,7},{7,3},{8,12},{12,8},{9,1... | collective-permute-start | bytes 5898248 | tf_op jit(solution)/shard_map/ppermute | solution.py:599
  53.3 25.2 %collective-permute-start.2 = (bf16[16,112,256]{2,1,0:T(8,128)(2,1)S(1)}, bf16[16,112,256]{2,1,0:T(8,128)(2,1)}, u32[]{:S(2)}, u32[]{:S(2)}) collective-permute-start(bf16[16,112,256]{2,1,0:T(8,128)(2,1)S(1)} %all-to-all-done.refs_3_), channel_id=1, source_target_pairs={{0,1},{1,2},{2,3},{3,0},{4,5},{5,6},{6,7},{7,4},{8,9},{9,10},{10,1... | collective-permute-start | bytes 2752520 | tf_op jit(solution)/shard_map/ppermute | solution.py:542
  55.2 24.4 %collective-permute-start.1 = (bf16[16,112,256]{2,1,0:T(8,128)(2,1)S(1)}, bf16[16,112,256]{2,1,0:T(8,128)(2,1)}, u32[]{:S(2)}, u32[]{:S(2)}) collective-permute-start(bf16[16,112,256]{2,1,0:T(8,128)(2,1)S(1)} %all-to-all-done.refs_3_), channel_id=1, source_target_pairs={{0,3},{1,0},{2,1},{3,2},{4,7},{5,4},{6,5},{7,6},{8,11},{9,8},{10,9... | collective-permute-start | bytes 2752520 | tf_op jit(solution)/shard_map/ppermute | solution.py:542
  79.5 21.3 %collective-permute-start.3 = (bf16[8,112,256]{2,1,0:T(8,128)(2,1)S(1)}, bf16[8,112,256]{2,1,0:T(8,128)(2,1)S(1)}, u32[]{:S(2)}, u32[]{:S(2)}) collective-permute-start(bf16[8,112,256]{2,1,0:T(8,128)(2,1)S(1)} %slice.8), channel_id=1, source_target_pairs={{0,1},{1,2},{2,3},{3,0},{4,5},{5,6},{6,7},{7,4},{8,9},{9,10},{10,1... | collective-permute-start | bytes 1376264 | tf_op jit(solution)/shard_map/ppermute | solution.py:542
  80.7 20.1 %collective-permute-start.4 = (bf16[8,112,256]{2,1,0:T(8,128)(2,1)S(1)}, bf16[8,112,256]{2,1,0:T(8,128)(2,1)S(1)}, u32[]{:S(2)}, u32[]{:S(2)}) collective-permute-start(bf16[8,112,256]{2,1,0:T(8,128)(2,1)S(1)} %slice.9), channel_id=1, source_target_pairs={{0,3},{1,0},{2,1},{3,2},{4,7},{5,4},{6,5},{7,6},{8,11},{9,8},{10,9... | collective-permute-start | bytes 1376264 | tf_op jit(solution)/shard_map/ppermute | solution.py:542
  113.4 18.1 %all-to-all-start.3 = ((bf16[16,6,2,16,128]{4,3,2,1,0:T(8,128)(2,1)}), bf16[16,6,2,16,128]{4,3,2,1,0:T(8,128)(2,1)S(1)}, u32[]{:S(2)}, u32[]{:S(2)}) async-start(bf16[16,6,2,16,128]{4,3,2,1,0:T(8,128)(2,1)} %shard_map.73), calls=%async_computation.3 | async-start | bytes 1572864 | tf_op jit(solution)/shard_map/all_to_all | solution.py:538
  131.5 26.4 %all-to-all-start.2 = ((bf16[16,6,2,16,128]{4,3,2,1,0:T(8,128)(2,1)}), bf16[16,6,2,16,128]{4,3,2,1,0:T(8,128)(2,1)S(1)}, u32[]{:S(2)}, u32[]{:S(2)}) async-start(bf16[16,6,2,16,128]{4,3,2,1,0:T(8,128)(2,1)} %shard_map.70), calls=%async_computation.2 | async-start | bytes 1572864 | tf_op jit(solution)/shard_map/all_to_all | solution.py:538
  141.6 8.0 %collective-permute-start.11 = (bf16[32,2048]{1,0:T(8,128)(2,1)S(1)}, bf16[32,2048]{1,0:T(8,128)(2,1)S(1)}, u32[]{:S(2)}, u32[]{:S(2)}) collective-permute-start(bf16[32,2048]{1,0:T(8,128)(2,1)S(1)} %get-tuple-element.39), channel_id=1, source_target_pairs={{0,1},{1,2},{2,3},{3,0},{4,5},{5,6},{6,7},{7,4},{8,9},{9,10},{10,1... | collective-permute-start | bytes 393224 | tf_op jit(solution)/shard_map/ppermute | solution.py:542
  141.6 7.9 %collective-permute-start.12 = (bf16[32,2048]{1,0:T(8,128)(2,1)S(1)}, bf16[32,2048]{1,0:T(8,128)(2,1)S(1)}, u32[]{:S(2)}, u32[]{:S(2)}) collective-permute-start(bf16[32,2048]{1,0:T(8,128)(2,1)S(1)} %get-tuple-element.40), channel_id=1, source_target_pairs={{0,2},{1,3},{2,0},{3,1},{4,6},{5,7},{6,4},{7,5},{8,10},{9,11},{10,... | collective-permute-start | bytes 393224 | tf_op jit(solution)/shard_map/ppermute | solution.py:542
  154.0 9.3 %collective-permute-start.14 = (bf16[32,2048]{1,0:T(8,128)(2,1)S(1)}, bf16[32,2048]{1,0:T(8,128)(2,1)S(1)}, u32[]{:S(2)}, u32[]{:S(2)}) collective-permute-start(bf16[32,2048]{1,0:T(8,128)(2,1)S(1)} %shard_map.75.refs_1_), channel_id=1, source_target_pairs={{0,1},{1,2},{2,3},{3,0},{4,5},{5,6},{6,7},{7,4},{8,9},{9,10},{10,1... | collective-permute-start | bytes 393224 | tf_op jit(solution)/shard_map/ppermute | solution.py:542
  154.6 11.2 %collective-permute-start.15 = (bf16[32,2048]{1,0:T(8,128)(2,1)S(1)}, bf16[32,2048]{1,0:T(8,128)(2,1)S(1)}, u32[]{:S(2)}, u32[]{:S(2)}) collective-permute-start(bf16[32,2048]{1,0:T(8,128)(2,1)S(1)} %shard_map.75.refs_1_), channel_id=1, source_target_pairs={{0,2},{1,3},{2,0},{3,1},{4,6},{5,7},{6,4},{7,5},{8,10},{9,11},{10,... | collective-permute-start | bytes 393224 | tf_op jit(solution)/shard_map/ppermute | solution.py:542
  160.7 16.2 %collective-permute-start.5 = (bf16[32,2048]{1,0:T(8,128)(2,1)S(1)}, bf16[32,2048]{1,0:T(8,128)(2,1)S(1)}, u32[]{:S(2)}, u32[]{:S(2)}) collective-permute-start(bf16[32,2048]{1,0:T(8,128)(2,1)S(1)} %get-tuple-element.35), channel_id=1, source_target_pairs={{0,1},{1,2},{2,3},{3,0},{4,5},{5,6},{6,7},{7,4},{8,9},{9,10},{10,1... | collective-permute-start | bytes 393224 | tf_op jit(solution)/shard_map/ppermute | solution.py:542
  162.8 14.1 %collective-permute-start.6 = (bf16[32,2048]{1,0:T(8,128)(2,1)S(1)}, bf16[32,2048]{1,0:T(8,128)(2,1)S(1)}, u32[]{:S(2)}, u32[]{:S(2)}) collective-permute-start(bf16[32,2048]{1,0:T(8,128)(2,1)S(1)} %get-tuple-element.36), channel_id=1, source_target_pairs={{0,2},{1,3},{2,0},{3,1},{4,6},{5,7},{6,4},{7,5},{8,10},{9,11},{10,... | collective-permute-start | bytes 393224 | tf_op jit(solution)/shard_map/ppermute | solution.py:542
  163.3 13.6 %collective-permute-start.7 = (bf16[32,2048]{1,0:T(8,128)(2,1)S(1)}, bf16[32,2048]{1,0:T(8,128)(2,1)S(1)}, u32[]{:S(2)}, u32[]{:S(2)}) collective-permute-start(bf16[32,2048]{1,0:T(8,128)(2,1)S(1)} %get-tuple-element.37), channel_id=1, source_target_pairs={{0,3},{1,0},{2,1},{3,2},{4,7},{5,4},{6,5},{7,6},{8,11},{9,8},{10,9... | collective-permute-start | bytes 393224 | tf_op jit(solution)/shard_map/ppermute | solution.py:542
  169.6 23.3 %all-to-all-start.6 = ((bf16[16,6,2,16,128]{4,3,2,1,0:T(8,128)(2,1)}), bf16[16,6,2,16,128]{4,3,2,1,0:T(8,128)(2,1)S(1)}, u32[]{:S(2)}, u32[]{:S(2)}) async-start(bf16[16,6,2,16,128]{4,3,2,1,0:T(8,128)(2,1)} %get-tuple-element.53), calls=%async_computation.6 | async-start | bytes 1572864 | tf_op jit(solution)/shard_map/all_to_all | solution.py:538
  192.9 18.9 %all-to-all-start.4 = ((bf16[16,6,2,16,128]{4,3,2,1,0:T(8,128)(2,1)}), bf16[16,6,2,16,128]{4,3,2,1,0:T(8,128)(2,1)S(1)}, u32[]{:S(2)}, u32[]{:S(2)}) async-start(bf16[16,6,2,16,128]{4,3,2,1,0:T(8,128)(2,1)} %get-tuple-element.44), calls=%async_computation.4 | async-start | bytes 1572864 | tf_op jit(solution)/shard_map/all_to_all | solution.py:538
  209.0 13.7 %collective-permute-start.21 = (bf16[2,8,112,128]{3,2,1,0:T(8,128)(2,1)}, bf16[2,8,112,128]{3,2,1,0:T(8,128)(2,1)S(1)}, u32[]{:S(2)}, u32[]{:S(2)}) collective-permute-start(bf16[2,8,112,128]{3,2,1,0:T(8,128)(2,1)} %get-tuple-element.55), channel_id=1, source_target_pairs={{0,1},{1,0},{2,3},{3,2},{4,5},{5,4},{6,7},{7,6},{8,9},{9,8},{10,11... | collective-permute-start | bytes 1376264 | tf_op jit(solution)/shard_map/ppermute | solution.py:562
  209.7 13.0 %collective-permute-start.22 = (bf16[2,8,112,128]{3,2,1,0:T(8,128)(2,1)}, bf16[2,8,112,128]{3,2,1,0:T(8,128)(2,1)}, u32[]{:S(2)}, u32[]{:S(2)}) collective-permute-start(bf16[2,8,112,128]{3,2,1,0:T(8,128)(2,1)} %get-tuple-element.57), channel_id=1, source_target_pairs={{0,3},{1,2},{2,1},{3,0},{4,7},{5,6},{6,5},{7,4},{8,11},{9,10},{10,... | collective-permute-start | bytes 1376264 | tf_op jit(solution)/shard_map/ppermute | solution.py:563
  220.7 21.8 %collective-permute-start.17 = (bf16[2,8,112,128]{3,2,1,0:T(8,128)(2,1)}, bf16[2,8,112,128]{3,2,1,0:T(8,128)(2,1)S(1)}, u32[]{:S(2)}, u32[]{:S(2)}) collective-permute-start(bf16[2,8,112,128]{3,2,1,0:T(8,128)(2,1)} %get-tuple-element.46), channel_id=1, source_target_pairs={{0,1},{1,0},{2,3},{3,2},{4,5},{5,4},{6,7},{7,6},{8,9},{9,8},{10,11... | collective-permute-start | bytes 1376264 | tf_op jit(solution)/shard_map/ppermute | solution.py:562
  222.1 20.4 %collective-permute-start.18 = (bf16[2,8,112,128]{3,2,1,0:T(8,128)(2,1)}, bf16[2,8,112,128]{3,2,1,0:T(8,128)(2,1)S(1)}, u32[]{:S(2)}, u32[]{:S(2)}) collective-permute-start(bf16[2,8,112,128]{3,2,1,0:T(8,128)(2,1)} %get-tuple-element.48), channel_id=1, source_target_pairs={{0,3},{1,2},{2,1},{3,0},{4,7},{5,6},{6,5},{7,4},{8,11},{9,10},{10,... | collective-permute-start | bytes 1376264 | tf_op jit(solution)/shard_map/ppermute | solution.py:563
  223.9 10.5 %collective-permute-start.23 = (bf16[8,112,128]{2,1,0:T(8,128)(2,1)S(1)}, bf16[8,112,128]{2,1,0:T(8,128)(2,1)S(1)}, u32[]{:S(2)}, u32[]{:S(2)}) collective-permute-start(bf16[8,112,128]{2,1,0:T(8,128)(2,1)S(1)} %get-tuple-element.59), channel_id=1, source_target_pairs={{0,3},{1,2},{2,1},{3,0},{4,7},{5,6},{6,5},{7,4},{8,11},{9,10},{10,... | collective-permute-start | bytes 688136 | tf_op jit(solution)/shard_map/ppermute | solution.py:567
  235.3 16.5 %all-to-all-start.7 = ((bf16[16,112,128]{2,1,0:T(8,128)(2,1)}), bf16[16,112,128]{2,1,0:T(8,128)(2,1)S(1)}, u32[]{:S(2)}, u32[]{:S(2)}) async-start(bf16[16,112,128]{2,1,0:T(8,128)(2,1)} %shard_map.83), calls=%async_computation.7 | async-start | bytes 917504 | tf_op jit(solution)/shard_map/all_to_all | solution.py:538
  251.8 14.4 %all-to-all-start.5 = ((bf16[16,112,128]{2,1,0:T(8,128)(2,1)}), bf16[16,112,128]{2,1,0:T(8,128)(2,1)S(1)}, u32[]{:S(2)}, u32[]{:S(2)}) async-start(bf16[16,112,128]{2,1,0:T(8,128)(2,1)} %shard_map.80), calls=%async_computation.5 | async-start | bytes 917504 | tf_op jit(solution)/shard_map/all_to_all | solution.py:538
  (11 other events, 114.6 us)

commit v8 on v6

--- a/solution.py
+++ b/solution.py
@@ -18,7 +18,7 @@
 STREAMS = 2
 BLOCKS = 4
 GROUP = 32
-MIX_STEP = 4
+MIX_STEP = 2
 TERMS_STEP = 2
 AHEAD = 3
 
@@ -207,7 +207,7 @@
         part = q_refs[0].shape[1]
         for shift, ref in enumerate(q_refs):
             start = pl.multiple_of(part * ((copy + shift) % copies), 16)
-            q_ref[pl.ds(start, part), :] = ref[n, :, stream * lanes : (stream + 1) * lanes]
+            q_ref[pl.ds(start, part), :] = ref[n]
         for half, ref in enumerate((own_ref, sib_ref)):
             _, experts, rows, width = ref.shape
             got = lax.dot_general(
@@ -233,7 +233,7 @@
     def body(*refs):
         mix_kernel(*refs, stream=stream)
 
-    q_block = pl.BlockSpec((step, part, lanes * STREAMS), lambda i, _: (i, 0, 0))
+    q_block = pl.BlockSpec((step, part, lanes), lambda i, _: (i, 0, stream))
     return pl.pallas_call(
         body,
         grid_spec=pltpu.PrefetchScalarGridSpec(
@@ -255,7 +255,7 @@
             bytes_accessed=4 * chips * experts * rows * width,
             transcendentals=0,
         ),
-    )(at, own, sib, *q_parts)
+    )(at, own, sib, *(q if k == 2 else from_hbm(q) for k, q in enumerate(q_parts)))
 
 
 def factor_kernel(copy_ref, parts_ref, hidden_ref, *refs):

time: 278 us -> 280 us (level)
  Pallas kernels: 85 us -> 88.3 us
    pallas_call x2, Pallas kernels: 17.9 us -> 21.8 us  [mix(): pl.pallas_call(body, grid_spec=pltpu.PrefetchScalarGridSpec(num_scalar_pr...]
  transfers between devices with their start and end apart: 32 -> 32, of which waited for: 14 -> 14; matrix products, arithmetic and copies ran while one was open for 1% -> 1% of each run, Pallas kernels for 23% -> 24%
where the time goes in v8:
time: 280 us; the launch traced here: 277 us
  Pallas kernels  88.3 us (32%)
  starting transfers between devices  85.2 us (30%)
  waiting for transfers between devices  69.1 us (25%)
  blocking collectives  30 us (11%)
  local copies, waits for them, and re-layouts  3.22 us (1%)
    all_to_all x7, starting transfers between devices, exchange(): return lax.all_to_all(values, axes, split_axis=0, concat_axis=0, tiled=True)  50 us
    ppermute x16, waiting for transfers between devices, shift(): lax.ppermute(value, 'dp', [(i, (i + step) % copies) for i in range(copies)])  40.1 us
    all_to_all x1, blocking collectives, exchange(): return lax.all_to_all(values, axes, split_axis=0, concat_axis=0, tiled=True)  30 us
    ppermute x16, starting transfers between devices, shift(): lax.ppermute(value, 'dp', [(i, (i + step) % copies) for i in range(copies)])  25.4 us
    pallas_call x2, Pallas kernels, mix(): pl.pallas_call(body, grid_spec=pltpu.PrefetchScalarGridSpec(num_scalar_pr...  21.8 us
    pallas_call x2, Pallas kernels, second_terms(): pl.pallas_call(body, grid_spec=pltpu.PrefetchScalarGridSpec(num_scalar_pr...  17.7 us
    pallas_call x2, Pallas kernels, dispatch(): pl.pallas_call(body, grid_spec=pltpu.PrefetchScalarGridSpec(num_scalar_pr...  16.8 us
    all_to_all x7, waiting for transfers between devices, exchange(): return lax.all_to_all(values, axes, split_axis=0, concat_axis=0, tiled=True)  15.3 us
  transfers between devices with their start and end apart: 32, of which 14 were waited for; matrix products, arithmetic and copies ran while one was open for 1% of the time, Pallas kernels for 24%

profile of v8, /device:TPU:6, one launch (start us, length us, event | category | flops | bytes accessed | tf_op | source)
XLA Modules:
  0.0 276.7 jit_solution(10239486788913531004)
XLA Ops:
  2.8 7.4 %all-to-all-start = ((bf16[16,112,256]{2,1,0:T(8,128)(2,1)}), bf16[16,112,256]{2,1,0:T(8,128)(2,1)S(1)}, u32[]{:S(2)}, u32[]{:S(2)}) async-start(bf16[16,112,256]{2,1,0:T(8,128)(2,1)} %bitcast.32), calls=%async_computation | async-start | bytes 1835008 | tf_op jit(solution)/shard_map/all_to_all | solution.py:529
  10.2 4.0 %prepare.1 = bf16[16,480,128]{2,1,0:T(8,128)(2,1)} custom-call(s32[8,128]{1,0:T(8,128)} %bitcast.35, f32[8,128]{1,0:T(8,128)} %bitcast.36, bf16[128,7168]{1,0:T(8,128)(2,1)} %bitcast.34), custom_call_target="tpu_custom_call" | custom-call | tf_op jit(solution)/shard_map/prepare/pallas_call | solution.py:94
  14.2 9.1 %all-to-all-done.refs_3_ = bf16[16,112,256]{2,1,0:T(8,128)(2,1)S(1)} async-done(((bf16[16,112,256]{2,1,0:T(8,128)(2,1)}), bf16[16,112,256]{2,1,0:T(8,128)(2,1)S(1)}, u32[]{:S(2)}, u32[]{:S(2)}) %all-to-all-start) | async-done | bytes 917536 | tf_op jit(solution)/shard_map/all_to_all | solution.py:529
  23.4 30.0 %all_to_all.40.refs_1_ = bf16[16,480,128]{2,1,0:T(8,128)(2,1)S(1)} all-to-all(bf16[16,480,128]{2,1,0:T(8,128)(2,1)} %prepare.1), channel_id=1, replica_groups=mesh['chip'=16,'core'=2,'dp'=4] {'chip'}, dimensions={0} | all-to-all | bytes 3932160 | tf_op jit(solution)/shard_map/all_to_all | solution.py:529
  57.3 21.0 %collective-permute-done.2.refs_6_ = bf16[16,112,256]{2,1,0:T(8,128)(2,1)S(1)} collective-permute-done((bf16[16,112,256]{2,1,0:T(8,128)(2,1)S(1)}, bf16[16,112,256]{2,1,0:T(8,128)(2,1)S(1)}, u32[]{:S(2)}, u32[]{:S(2)}) %collective-permute-start.2) | collective-permute-done | bytes 917536 | tf_op jit(solution)/shard_map/ppermute | solution.py:533
  83.6 9.4 %collective-permute-done.3 = bf16[8,112,256]{2,1,0:T(8,128)(2,1)S(1)} collective-permute-done((bf16[8,112,256]{2,1,0:T(8,128)(2,1)}, bf16[8,112,256]{2,1,0:T(8,128)(2,1)S(1)}, u32[]{:S(2)}, u32[]{:S(2)}) %collective-permute-start.3) | collective-permute-done | bytes 458784 | tf_op jit(solution)/shard_map/ppermute | solution.py:533
  94.5 7.9 %shard_map.68 = bf16[128,128,448]{2,1,0:T(8,128)(2,1)} custom-call(s32[1]{0:T(128)} %bitcast.1.refs_0_, bf16[16,480,128]{2,1,0:T(8,128)(2,1)S(1)} %all_to_all.40.refs_1_), custom_call_target="tpu_custom_call" | custom-call | flops 1879048192 | bytes 14680064 | tf_op jit(solution)/shard_map/pallas_call | solution.py:156
  102.4 8.9 %shard_map.69 = bf16[128,128,448]{2,1,0:T(8,128)(2,1)} custom-call(s32[1]{0:T(128)} %bitcast.1.refs_0_, bf16[16,480,128]{2,1,0:T(8,128)(2,1)} %collective-permute-done.refs_1_), custom_call_target="tpu_custom_call" | custom-call | flops 1879048192 | bytes 14680064 | tf_op jit(solution)/shard_map/pallas_call | solution.py:156
  111.3 10.9 %shard_map.73 = bf16[16,6,2,16,128]{4,3,2,1,0:T(8,128)(2,1)} custom-call(s32[2]{0:T(128)S(1)} %pad_add_fusion.refs_0_, bf16[16,8,128,448]{3,2,1,0:T(8,128)(2,1)} %bitcast.19, bf16[16,8,128,448]{3,2,1,0:T(8,128)(2,1)} %bitcast.23, bf16[16,112,256]{2,1,0:T(8,128)(2,1)} %copy-done, bf16[16,112,256]{2,1,0:T(8,128)(2,1)} %copy-done.2, ...), custom_call_target="tpu_custom_call" | custom-call | flops 3758096384 | bytes 14680064 | tf_op jit(solution)/shard_map/pallas_call | solution.py:237
  122.2 6.5 %all-to-all-start.3 = ((bf16[16,6,2,16,128]{4,3,2,1,0:T(8,128)(2,1)}), bf16[16,6,2,16,128]{4,3,2,1,0:T(8,128)(2,1)S(1)}, u32[]{:S(2)}, u32[]{:S(2)}) async-start(bf16[16,6,2,16,128]{4,3,2,1,0:T(8,128)(2,1)} %shard_map.73), calls=%async_computation.3 | async-start | bytes 1572864 | tf_op jit(solution)/shard_map/all_to_all | solution.py:529
  128.7 10.9 %shard_map.70 = bf16[16,6,2,16,128]{4,3,2,1,0:T(8,128)(2,1)} custom-call(s32[2]{0:T(128)S(1)} %pad_add_fusion.refs_0_, bf16[16,8,128,448]{3,2,1,0:T(8,128)(2,1)} %bitcast.20, bf16[16,8,128,448]{3,2,1,0:T(8,128)(2,1)} %bitcast.24, bf16[16,112,256]{2,1,0:T(8,128)(2,1)} %copy-done, bf16[16,112,256]{2,1,0:T(8,128)(2,1)} %copy-done.2, ...), custom_call_target="tpu_custom_call" | custom-call | flops 3758096384 | bytes 14680064 | tf_op jit(solution)/shard_map/pallas_call | solution.py:237
  139.7 7.2 %all-to-all-start.2 = ((bf16[16,6,2,16,128]{4,3,2,1,0:T(8,128)(2,1)}), bf16[16,6,2,16,128]{4,3,2,1,0:T(8,128)(2,1)S(1)}, u32[]{:S(2)}, u32[]{:S(2)}) async-start(bf16[16,6,2,16,128]{4,3,2,1,0:T(8,128)(2,1)} %shard_map.70), calls=%async_computation.2 | async-start | bytes 1572864 | tf_op jit(solution)/shard_map/all_to_all | solution.py:529
  150.2 4.6 %collective-permute-start.12 = (bf16[32,2048]{1,0:T(8,128)(2,1)S(1)}, bf16[32,2048]{1,0:T(8,128)(2,1)S(1)}, u32[]{:S(2)}, u32[]{:S(2)}) collective-permute-start(bf16[32,2048]{1,0:T(8,128)(2,1)S(1)} %get-tuple-element.40), channel_id=1, source_target_pairs={{0,2},{1,3},{2,0},{3,1},{4,6},{5,7},{6,4},{7,5},{8,10},{9,11},{10,... | collective-permute-start | bytes 393224 | tf_op jit(solution)/shard_map/ppermute | solution.py:533
  175.2 3.8 %shard_map.76 = (f32[8,32,2048]{2,1,0:T(8,128)}, bf16[16,6,2,16,128]{4,3,2,1,0:T(8,128)(2,1)}) custom-call(s32[1]{0:T(128)} %bitcast.copy_ref.refs_0_, bf16[32,2048]{1,0:T(8,128)(2,1)S(1)} %shard_map.75.refs_1_, bf16[32,2048]{1,0:T(8,128)(2,1)S(1)} %collective-permute-done.14.refs_2_, bf16[32,2048]{1,0:T(8,128)(2,1)S(1)} %collective-permute-done.15.refs_3_, ...), custom_call_target="tpu_custom_call" | custom-call | flops 805306368 | bytes 3145728 | tf_op jit(solution)/shard_map/pallas_call | solution.py:391
  179.1 7.2 %all-to-all-start.6 = ((bf16[16,6,2,16,128]{4,3,2,1,0:T(8,128)(2,1)}), bf16[16,6,2,16,128]{4,3,2,1,0:T(8,128)(2,1)S(1)}, u32[]{:S(2)}, u32[]{:S(2)}) async-start(bf16[16,6,2,16,128]{4,3,2,1,0:T(8,128)(2,1)} %get-tuple-element.53), calls=%async_computation.6 | async-start | bytes 1572864 | tf_op jit(solution)/shard_map/all_to_all | solution.py:529
  198.5 3.8 %shard_map.77 = (f32[8,32,2048]{2,1,0:T(8,128)}, bf16[16,6,2,16,128]{4,3,2,1,0:T(8,128)(2,1)}) custom-call(s32[1]{0:T(128)} %bitcast.copy_ref.refs_0_, bf16[32,2048]{1,0:T(8,128)(2,1)S(1)} %shard_map.72.refs_1_, bf16[32,2048]{1,0:T(8,128)(2,1)S(1)} %collective-permute-done.8.refs_2_, ...), custom_call_target="tpu_custom_call", output_to_operand_aliasing={{0}: (6, {})} | custom-call | flops 805306368 | bytes 3145728 | tf_op jit(solution)/shard_map/pallas_call | solution.py:391
  202.4 7.2 %all-to-all-start.4 = ((bf16[16,6,2,16,128]{4,3,2,1,0:T(8,128)(2,1)}), bf16[16,6,2,16,128]{4,3,2,1,0:T(8,128)(2,1)S(1)}, u32[]{:S(2)}, u32[]{:S(2)}) async-start(bf16[16,6,2,16,128]{4,3,2,1,0:T(8,128)(2,1)} %get-tuple-element.44), calls=%async_computation.4 | async-start | bytes 1572864 | tf_op jit(solution)/shard_map/all_to_all | solution.py:529
  209.6 8.8 %shard_map.81 = (bf16[2,8,112,128]{3,2,1,0:T(8,128)(2,1)}, bf16[2,8,112,128]{3,2,1,0:T(8,128)(2,1)S(1)}, bf16[2,8,112,128]{3,2,1,0:T(8,128)(2,1)}, bf16[2,8,112,128]{3,2,1,0:T(8,128)(2,1)S(1)}) custom-call(s32[2]{0:T(128)S(1)} %pad_add_fusion.refs_0_, bf16[16,8,128,448]{3,2,1,0:T(8,128)(2,1)} %bitcast.21, bf16[16,8,128,448]{3,2,1,0:T(8,128)(2,1)} %bitcast.25, ...), custom_call_target="tpu_custom_call" | custom-call | flops 3758096384 | bytes 14680064 | tf_op jit(solution)/shard_map/pallas_call | solution.py:474
  221.3 8.8 %shard_map.78 = (bf16[2,8,112,128]{3,2,1,0:T(8,128)(2,1)}, bf16[2,8,112,128]{3,2,1,0:T(8,128)(2,1)S(1)}, bf16[2,8,112,128]{3,2,1,0:T(8,128)(2,1)}, bf16[2,8,112,128]{3,2,1,0:T(8,128)(2,1)S(1)}) custom-call(s32[2]{0:T(128)S(1)} %pad_add_fusion.refs_0_, bf16[16,8,128,448]{3,2,1,0:T(8,128)(2,1)} %bitcast.22, bf16[16,8,128,448]{3,2,1,0:T(8,128)(2,1)} %bitcast.26, ...), custom_call_target="tpu_custom_call" | custom-call | flops 3758096384 | bytes 14680064 | tf_op jit(solution)/shard_map/pallas_call | solution.py:474
  236.3 7.7 %collective-permute-done.23.low_got_ref = bf16[8,112,128]{2,1,0:T(8,128)(2,1)S(1)} collective-permute-done((bf16[8,112,128]{2,1,0:T(8,128)(2,1)S(1)}, bf16[8,112,128]{2,1,0:T(8,128)(2,1)S(1)}, u32[]{:S(2)}, u32[]{:S(2)}) %collective-permute-start.23) | collective-permute-done | bytes 229408 | tf_op jit(solution)/shard_map/ppermute | solution.py:558
  244.9 7.2 %all-to-all-start.7 = ((bf16[16,112,128]{2,1,0:T(8,128)(2,1)}), bf16[16,112,128]{2,1,0:T(8,128)(2,1)S(1)}, u32[]{:S(2)}, u32[]{:S(2)}) async-start(bf16[16,112,128]{2,1,0:T(8,128)(2,1)} %shard_map.83), calls=%async_computation.7 | async-start | bytes 917504 | tf_op jit(solution)/shard_map/all_to_all | solution.py:529
  254.4 5.2 %collective-permute-done.19.low_got_ref = bf16[8,112,128]{2,1,0:T(8,128)(2,1)S(1)} collective-permute-done((bf16[8,112,128]{2,1,0:T(8,128)(2,1)S(1)}, bf16[8,112,128]{2,1,0:T(8,128)(2,1)S(1)}, u32[]{:S(2)}, u32[]{:S(2)}) %collective-permute-start.19) | collective-permute-done | bytes 229408 | tf_op jit(solution)/shard_map/ppermute | solution.py:558
  261.2 7.2 %all-to-all-start.5 = ((bf16[16,112,128]{2,1,0:T(8,128)(2,1)}), bf16[16,112,128]{2,1,0:T(8,128)(2,1)S(1)}, u32[]{:S(2)}, u32[]{:S(2)}) async-start(bf16[16,112,128]{2,1,0:T(8,128)(2,1)} %shard_map.80), calls=%async_computation.5 | async-start | bytes 917504 | tf_op jit(solution)/shard_map/all_to_all | solution.py:529
  269.5 6.1 %all-to-all-done.5 = bf16[16,112,128]{2,1,0:T(8,128)(2,1)S(1)} async-done(((bf16[16,112,128]{2,1,0:T(8,128)(2,1)}), bf16[16,112,128]{2,1,0:T(8,128)(2,1)S(1)}, u32[]{:S(2)}, u32[]{:S(2)}) %all-to-all-start.5) | async-done | bytes 458784 | tf_op jit(solution)/shard_map/all_to_all | solution.py:529
  (72 shorter events, 64.8 us)
Async XLA Ops:
  2.8 20.5 %all-to-all-start = ((bf16[16,112,256]{2,1,0:T(8,128)(2,1)}), bf16[16,112,256]{2,1,0:T(8,128)(2,1)S(1)}, u32[]{:S(2)}, u32[]{:S(2)}) async-start(bf16[16,112,256]{2,1,0:T(8,128)(2,1)} %bitcast.32), calls=%async_computation | async-start | bytes 1835008 | tf_op jit(solution)/shard_map/all_to_all | solution.py:529
  53.3 49.1 %collective-permute-start = (bf16[16,480,128]{2,1,0:T(8,128)(2,1)S(1)}, bf16[16,480,128]{2,1,0:T(8,128)(2,1)}, u32[]{:S(2)}, u32[]{:S(2)}) collective-permute-start(bf16[16,480,128]{2,1,0:T(8,128)(2,1)S(1)} %all_to_all.40.refs_1_), channel_id=1, source_target_pairs={{0,4},{4,0},{1,5},{5,1},{2,6},{6,2},{3,7},{7,3},{8,12},{12,8},{9,1... | collective-permute-start | bytes 5898248 | tf_op jit(solution)/shard_map/ppermute | solution.py:590
  53.3 25.1 %collective-permute-start.2 = (bf16[16,112,256]{2,1,0:T(8,128)(2,1)S(1)}, bf16[16,112,256]{2,1,0:T(8,128)(2,1)S(1)}, u32[]{:S(2)}, u32[]{:S(2)}) collective-permute-start(bf16[16,112,256]{2,1,0:T(8,128)(2,1)S(1)} %all-to-all-done.refs_3_), channel_id=1, source_target_pairs={{0,1},{1,2},{2,3},{3,0},{4,5},{5,6},{6,7},{7,4},{8,9},{9,10},{10,1... | collective-permute-start | bytes 2752520 | tf_op jit(solution)/shard_map/ppermute | solution.py:533
  55.2 24.0 %collective-permute-start.1 = (bf16[16,112,256]{2,1,0:T(8,128)(2,1)S(1)}, bf16[16,112,256]{2,1,0:T(8,128)(2,1)S(1)}, u32[]{:S(2)}, u32[]{:S(2)}) collective-permute-start(bf16[16,112,256]{2,1,0:T(8,128)(2,1)S(1)} %all-to-all-done.refs_3_), channel_id=1, source_target_pairs={{0,3},{1,0},{2,1},{3,2},{4,7},{5,4},{6,5},{7,6},{8,11},{9,8},{10,9... | collective-permute-start | bytes 2752520 | tf_op jit(solution)/shard_map/ppermute | solution.py:533
  79.2 13.8 %collective-permute-start.3 = (bf16[8,112,256]{2,1,0:T(8,128)(2,1)}, bf16[8,112,256]{2,1,0:T(8,128)(2,1)S(1)}, u32[]{:S(2)}, u32[]{:S(2)}) collective-permute-start(bf16[8,112,256]{2,1,0:T(8,128)(2,1)} %slice.8), channel_id=1, source_target_pairs={{0,1},{1,2},{2,3},{3,0},{4,5},{5,6},{6,7},{7,4},{8,9},{9,10},{10,1... | collective-permute-start | bytes 1376264 | tf_op jit(solution)/shard_map/ppermute | solution.py:533
  80.5 12.9 %collective-permute-start.4 = (bf16[8,112,256]{2,1,0:T(8,128)(2,1)}, bf16[8,112,256]{2,1,0:T(8,128)(2,1)}, u32[]{:S(2)}, u32[]{:S(2)}) collective-permute-start(bf16[8,112,256]{2,1,0:T(8,128)(2,1)} %slice.9), channel_id=1, source_target_pairs={{0,3},{1,0},{2,1},{3,2},{4,7},{5,4},{6,5},{7,6},{8,11},{9,8},{10,9... | collective-permute-start | bytes 1376264 | tf_op jit(solution)/shard_map/ppermute | solution.py:533
  122.2 17.5 %all-to-all-start.3 = ((bf16[16,6,2,16,128]{4,3,2,1,0:T(8,128)(2,1)}), bf16[16,6,2,16,128]{4,3,2,1,0:T(8,128)(2,1)S(1)}, u32[]{:S(2)}, u32[]{:S(2)}) async-start(bf16[16,6,2,16,128]{4,3,2,1,0:T(8,128)(2,1)} %shard_map.73), calls=%async_computation.3 | async-start | bytes 1572864 | tf_op jit(solution)/shard_map/all_to_all | solution.py:529
  139.7 28.0 %all-to-all-start.2 = ((bf16[16,6,2,16,128]{4,3,2,1,0:T(8,128)(2,1)}), bf16[16,6,2,16,128]{4,3,2,1,0:T(8,128)(2,1)S(1)}, u32[]{:S(2)}, u32[]{:S(2)}) async-start(bf16[16,6,2,16,128]{4,3,2,1,0:T(8,128)(2,1)} %shard_map.70), calls=%async_computation.2 | async-start | bytes 1572864 | tf_op jit(solution)/shard_map/all_to_all | solution.py:529
  150.2 9.0 %collective-permute-start.12 = (bf16[32,2048]{1,0:T(8,128)(2,1)S(1)}, bf16[32,2048]{1,0:T(8,128)(2,1)S(1)}, u32[]{:S(2)}, u32[]{:S(2)}) collective-permute-start(bf16[32,2048]{1,0:T(8,128)(2,1)S(1)} %get-tuple-element.40), channel_id=1, source_target_pairs={{0,2},{1,3},{2,0},{3,1},{4,6},{5,7},{6,4},{7,5},{8,10},{9,11},{10,... | collective-permute-start | bytes 393224 | tf_op jit(solution)/shard_map/ppermute | solution.py:533
  163.5 9.1 %collective-permute-start.14 = (bf16[32,2048]{1,0:T(8,128)(2,1)S(1)}, bf16[32,2048]{1,0:T(8,128)(2,1)S(1)}, u32[]{:S(2)}, u32[]{:S(2)}) collective-permute-start(bf16[32,2048]{1,0:T(8,128)(2,1)S(1)} %shard_map.75.refs_1_), channel_id=1, source_target_pairs={{0,1},{1,2},{2,3},{3,0},{4,5},{5,6},{6,7},{7,4},{8,9},{9,10},{10,1... | collective-permute-start | bytes 393224 | tf_op jit(solution)/shard_map/ppermute | solution.py:533
  163.6 11.6 %collective-permute-start.15 = (bf16[32,2048]{1,0:T(8,128)(2,1)S(1)}, bf16[32,2048]{1,0:T(8,128)(2,1)S(1)}, u32[]{:S(2)}, u32[]{:S(2)}) collective-permute-start(bf16[32,2048]{1,0:T(8,128)(2,1)S(1)} %shard_map.75.refs_1_), channel_id=1, source_target_pairs={{0,2},{1,3},{2,0},{3,1},{4,6},{5,7},{6,4},{7,5},{8,10},{9,11},{10,... | collective-permute-start | bytes 393224 | tf_op jit(solution)/shard_map/ppermute | solution.py:533
  167.0 8.3 %collective-permute-start.16 = (bf16[32,2048]{1,0:T(8,128)(2,1)S(1)}, bf16[32,2048]{1,0:T(8,128)(2,1)S(1)}, u32[]{:S(2)}, u32[]{:S(2)}) collective-permute-start(bf16[32,2048]{1,0:T(8,128)(2,1)S(1)} %shard_map.75.refs_1_), channel_id=1, source_target_pairs={{0,3},{1,0},{2,1},{3,2},{4,7},{5,4},{6,5},{7,6},{8,11},{9,8},{10,9... | collective-permute-start | bytes 393224 | tf_op jit(solution)/shard_map/ppermute | solution.py:533
  170.5 15.8 %collective-permute-start.5 = (bf16[32,2048]{1,0:T(8,128)(2,1)S(1)}, bf16[32,2048]{1,0:T(8,128)(2,1)S(1)}, u32[]{:S(2)}, u32[]{:S(2)}) collective-permute-start(bf16[32,2048]{1,0:T(8,128)(2,1)S(1)} %get-tuple-element.35), channel_id=1, source_target_pairs={{0,1},{1,2},{2,3},{3,0},{4,5},{5,6},{6,7},{7,4},{8,9},{9,10},{10,1... | collective-permute-start | bytes 393224 | tf_op jit(solution)/shard_map/ppermute | solution.py:533
  171.8 14.5 %collective-permute-start.6 = (bf16[32,2048]{1,0:T(8,128)(2,1)S(1)}, bf16[32,2048]{1,0:T(8,128)(2,1)S(1)}, u32[]{:S(2)}, u32[]{:S(2)}) collective-permute-start(bf16[32,2048]{1,0:T(8,128)(2,1)S(1)} %get-tuple-element.36), channel_id=1, source_target_pairs={{0,2},{1,3},{2,0},{3,1},{4,6},{5,7},{6,4},{7,5},{8,10},{9,11},{10,... | collective-permute-start | bytes 393224 | tf_op jit(solution)/shard_map/ppermute | solution.py:533
  172.7 13.6 %collective-permute-start.7 = (bf16[32,2048]{1,0:T(8,128)(2,1)S(1)}, bf16[32,2048]{1,0:T(8,128)(2,1)S(1)}, u32[]{:S(2)}, u32[]{:S(2)}) collective-permute-start(bf16[32,2048]{1,0:T(8,128)(2,1)S(1)} %get-tuple-element.37), channel_id=1, source_target_pairs={{0,3},{1,0},{2,1},{3,2},{4,7},{5,4},{6,5},{7,6},{8,11},{9,8},{10,9... | collective-permute-start | bytes 393224 | tf_op jit(solution)/shard_map/ppermute | solution.py:533
  179.1 23.3 %all-to-all-start.6 = ((bf16[16,6,2,16,128]{4,3,2,1,0:T(8,128)(2,1)}), bf16[16,6,2,16,128]{4,3,2,1,0:T(8,128)(2,1)S(1)}, u32[]{:S(2)}, u32[]{:S(2)}) async-start(bf16[16,6,2,16,128]{4,3,2,1,0:T(8,128)(2,1)} %get-tuple-element.53), calls=%async_computation.6 | async-start | bytes 1572864 | tf_op jit(solution)/shard_map/all_to_all | solution.py:529
  202.4 18.9 %all-to-all-start.4 = ((bf16[16,6,2,16,128]{4,3,2,1,0:T(8,128)(2,1)}), bf16[16,6,2,16,128]{4,3,2,1,0:T(8,128)(2,1)S(1)}, u32[]{:S(2)}, u32[]{:S(2)}) async-start(bf16[16,6,2,16,128]{4,3,2,1,0:T(8,128)(2,1)} %get-tuple-element.44), calls=%async_computation.4 | async-start | bytes 1572864 | tf_op jit(solution)/shard_map/all_to_all | solution.py:529
  218.4 13.7 %collective-permute-start.21 = (bf16[2,8,112,128]{3,2,1,0:T(8,128)(2,1)}, bf16[2,8,112,128]{3,2,1,0:T(8,128)(2,1)S(1)}, u32[]{:S(2)}, u32[]{:S(2)}) collective-permute-start(bf16[2,8,112,128]{3,2,1,0:T(8,128)(2,1)} %get-tuple-element.55), channel_id=1, source_target_pairs={{0,1},{1,0},{2,3},{3,2},{4,5},{5,4},{6,7},{7,6},{8,9},{9,8},{10,11... | collective-permute-start | bytes 1376264 | tf_op jit(solution)/shard_map/ppermute | solution.py:553
  219.4 12.7 %collective-permute-start.22 = (bf16[2,8,112,128]{3,2,1,0:T(8,128)(2,1)}, bf16[2,8,112,128]{3,2,1,0:T(8,128)(2,1)}, u32[]{:S(2)}, u32[]{:S(2)}) collective-permute-start(bf16[2,8,112,128]{3,2,1,0:T(8,128)(2,1)} %get-tuple-element.57), channel_id=1, source_target_pairs={{0,3},{1,2},{2,1},{3,0},{4,7},{5,6},{6,5},{7,4},{8,11},{9,10},{10,... | collective-permute-start | bytes 1376264 | tf_op jit(solution)/shard_map/ppermute | solution.py:554
  230.1 22.0 %collective-permute-start.17 = (bf16[2,8,112,128]{3,2,1,0:T(8,128)(2,1)}, bf16[2,8,112,128]{3,2,1,0:T(8,128)(2,1)S(1)}, u32[]{:S(2)}, u32[]{:S(2)}) collective-permute-start(bf16[2,8,112,128]{3,2,1,0:T(8,128)(2,1)} %get-tuple-element.46), channel_id=1, source_target_pairs={{0,1},{1,0},{2,3},{3,2},{4,5},{5,4},{6,7},{7,6},{8,9},{9,8},{10,11... | collective-permute-start | bytes 1376264 | tf_op jit(solution)/shard_map/ppermute | solution.py:553
  231.5 20.6 %collective-permute-start.18 = (bf16[2,8,112,128]{3,2,1,0:T(8,128)(2,1)}, bf16[2,8,112,128]{3,2,1,0:T(8,128)(2,1)S(1)}, u32[]{:S(2)}, u32[]{:S(2)}) collective-permute-start(bf16[2,8,112,128]{3,2,1,0:T(8,128)(2,1)} %get-tuple-element.48), channel_id=1, source_target_pairs={{0,3},{1,2},{2,1},{3,0},{4,7},{5,6},{6,5},{7,4},{8,11},{9,10},{10,... | collective-permute-start | bytes 1376264 | tf_op jit(solution)/shard_map/ppermute | solution.py:554
  233.4 10.7 %collective-permute-start.23 = (bf16[8,112,128]{2,1,0:T(8,128)(2,1)S(1)}, bf16[8,112,128]{2,1,0:T(8,128)(2,1)S(1)}, u32[]{:S(2)}, u32[]{:S(2)}) collective-permute-start(bf16[8,112,128]{2,1,0:T(8,128)(2,1)S(1)} %get-tuple-element.59), channel_id=1, source_target_pairs={{0,3},{1,2},{2,1},{3,0},{4,7},{5,6},{6,5},{7,4},{8,11},{9,10},{10,... | collective-permute-start | bytes 688136 | tf_op jit(solution)/shard_map/ppermute | solution.py:558
  244.9 16.3 %all-to-all-start.7 = ((bf16[16,112,128]{2,1,0:T(8,128)(2,1)}), bf16[16,112,128]{2,1,0:T(8,128)(2,1)S(1)}, u32[]{:S(2)}, u32[]{:S(2)}) async-start(bf16[16,112,128]{2,1,0:T(8,128)(2,1)} %shard_map.83), calls=%async_computation.7 | async-start | bytes 917504 | tf_op jit(solution)/shard_map/all_to_all | solution.py:529
  261.2 14.4 %all-to-all-start.5 = ((bf16[16,112,128]{2,1,0:T(8,128)(2,1)}), bf16[16,112,128]{2,1,0:T(8,128)(2,1)S(1)}, u32[]{:S(2)}, u32[]{:S(2)}) async-start(bf16[16,112,128]{2,1,0:T(8,128)(2,1)} %shard_map.80), calls=%async_computation.5 | async-start | bytes 917504 | tf_op jit(solution)/shard_map/all_to_all | solution.py:529
  (11 other events, 112.9 us)
